TPU v7x, 16 devices: a whole 2x2x2 slice. The times are simulated.
16 devices in a mesh: data: 16 (over z, y, x, core).
Axes of the slice: x: 2, y: 2, z: 2, core: 2. Of those that a mesh axis runs over, the one named last changes fastest.
Arguments:
- tokens: bfloat16 [16384, 1536], P('data')
- upstream: bfloat16 [16384, 1536], P('data')
- norm_gain: bfloat16 [2, 1536], replicated
- w_up: bfloat16 [2, 1536, 6144], replicated
- bias_up: bfloat16 [2, 6144], replicated
- w_down: bfloat16 [2, 6144, 1536], replicated
- bias_down: bfloat16 [2, 1536], replicated
Outputs:
- output 1: float32 [2, 1536], replicated
- output 2: float32 [2, 1536, 6144], replicated
- output 3: float32 [2, 6144], replicated
- output 4: float32 [2, 6144, 1536], replicated
- output 5: float32 [2, 1536], replicated
All inputs are finite; a program needn't handle non-finite values.
Results may differ from a plain program's by a relative error of at most 0.0070572.
Values are sent between devices in bfloat16 or wider.
A program may use at most 1 GiB of HBM per device.

v0:
```python
import functools

import jax
import jax.numpy as jnp
from jax import lax
from jax.experimental import pallas as pl
from jax.experimental.pallas import tpu as pltpu
from jax.sharding import PartitionSpec as P


EPSILON = 1e-6
TOKEN_DIMS = (((0,), (0,)), ((), ()))
FEATURE_DIMS = (((1,), (1,)), ((), ()))
MESH = pl.DeviceIdType.MESH
COLORS = 3
CORE, DIM_X, DIM_Y, DIM_Z = range(4)
COLOR_DIMS = ((DIM_X, DIM_Y, DIM_Z), (DIM_Y, DIM_Z, DIM_X), (DIM_Z, DIM_X, DIM_Y))
PIPELINE = (
    ("send_back_2", 4), ("load", 0), ("compute_sent", 0), ("send_back_3", 3), ("send_back_core", 6), ("share_core", 0),
    ("send_3", 2), ("compute_kept", 0), ("load_weights", 0), ("backward_0", 0), ("send_back_1", 5), ("store", 6), ("send_2", 1),
    ("backward_1", 0), ("send_1", 0), ("backward_2", 0), ("input_grad", 0),
)
MAX_LAG = 6
PART_GROUPS = (8, 4, 4)
RECV_SLOTS = 2
KEPT_SLOTS = 3
GATHER_SLOTS = 6
TILE = 256
UP_COLS = 512
ACT_ROWS = 16
ACT_COLS = 256
STREAM_SLOTS = 4
NORM_ROWS = 128
GELU_SCALE = 0.7978845608028654
GELU_CUBIC = 0.044715


def inverse_rms(hid_f):
    return lax.rsqrt(jnp.mean(hid_f * hid_f, axis=-1, keepdims=True) + EPSILON)


def gelu(values):
    return (0.5 * values) * (1.0 + jnp.tanh(values * (GELU_SCALE + GELU_SCALE * GELU_CUBIC * (values * values))))


def forward_kernel(
    sizes, tokens, upstream, w_up, w_down, gain_in, bias_up_in, bias_down_in, hid_out, normed_out, pre_act_out, act_out,
    grad_top_out, grad_top_b_out, small_out, hid, normed, branch, up_buf, down_buf, pre_buf, act_buf, up_rows, grad_b_buf,
    gain, bias_up, bias_down, io_sem, up_sem, down_sem, pre_sem, act_sem,
):
    num_layers, num_tiles, tile_cols = sizes
    num_tokens, row_dim = hid.shape
    steps = num_tiles + 1
    parts = tile_cols // UP_COLS

    def up_load(layer, tile):
        cols = pl.ds(pl.multiple_of(tile * tile_cols, 128), tile_cols)
        return pltpu.make_async_copy(w_up.at[layer, :, cols], up_buf.at[tile % 2], up_sem.at[tile % 2])

    def down_load(layer, tile):
        rows = pl.ds(pl.multiple_of(tile * tile_cols, 128), tile_cols)
        return pltpu.make_async_copy(w_down.at[layer, rows, :], down_buf.at[tile % 2], down_sem.at[tile % 2])

    def pre_store(layer, tile):
        cols = pl.ds(pl.multiple_of(tile * tile_cols, 128), tile_cols)
        return pltpu.make_async_copy(pre_buf.at[tile % 2], pre_act_out.at[layer, :, cols], pre_sem.at[tile % 2])

    def act_store(layer, tile):
        cols = pl.ds(pl.multiple_of(tile * tile_cols, 128), tile_cols)
        return pltpu.make_async_copy(act_buf.at[tile % 2], act_out.at[layer, :, cols], act_sem.at[tile % 2])

    def normed_store(layer):
        return pltpu.make_async_copy(normed, normed_out.at[layer], io_sem.at[1])

    def hid_store():
        return pltpu.make_async_copy(hid, hid_out, io_sem.at[2])

    tokens_load = pltpu.make_async_copy(tokens, hid, io_sem.at[0])
    tokens_load.start()
    up_load(0, 0).start()
    down_load(0, 0).start()
    upstream_load = pltpu.make_async_copy(upstream, up_rows, io_sem.at[3])
    upstream_load.start()
    small_out[...] = jnp.zeros_like(small_out)
    gain[...] = gain_in[...].astype(jnp.float32)
    bias_up[...] = bias_up_in[...].astype(jnp.float32)
    bias_down[...] = bias_down_in[...].astype(jnp.float32)
    tokens_load.wait()

    def each_block(action):
        @pl.loop(0, num_tokens // NORM_ROWS)
        def _(block):
            action(pl.ds(pl.multiple_of(block * NORM_ROWS, NORM_ROWS), NORM_ROWS))

    def normalize(layer, rows, hid_f):
        normed[rows, :] = ((hid_f * inverse_rms(hid_f)) * gain[pl.ds(layer, 1), :]).astype(jnp.bfloat16)

    def next_rows(layer, rows):
        new = ((hid[rows, :].astype(jnp.float32) + branch[rows, :]) + bias_down[pl.ds(layer, 1), :]).astype(jnp.bfloat16)
        hid[rows, :] = new
        return new.astype(jnp.float32)

    def activate(slot, part):
        start = part * UP_COLS
        for row in range(0, num_tokens, ACT_ROWS):
            for col in range(0, UP_COLS, ACT_COLS):
                piece = (slot, pl.ds(row, ACT_ROWS), pl.ds(pl.multiple_of(start + col, 128), ACT_COLS))
                act_buf[piece] = gelu(pre_buf[piece].astype(jnp.float32)).astype(jnp.bfloat16)

    def up_product(layer, tile):
        @pl.loop(0, parts)
        def _(part):
            fresh = tile * parts + part == 0
            last_slot = jnp.where((part == 0) & (tile > 0), (tile + 1) % 2, tile % 2)
            activate(last_slot, jnp.where(fresh, 0, (part + parts - 1) % parts))
            cols = pl.ds(pl.multiple_of(part * UP_COLS, 128), UP_COLS)
            bias = bias_up[pl.ds(layer, 1), pl.ds(pl.multiple_of(tile * tile_cols + part * UP_COLS, 128), UP_COLS)]
            pre_buf[tile % 2, :, cols] = (
                jnp.dot(normed[...], up_buf[tile % 2, :, cols], preferred_element_type=jnp.float32) + bias
            ).astype(jnp.bfloat16)

    def down_product(tile):
        slot = tile % 2
        for part in range(row_dim // UP_COLS):
            cols = slice(part * UP_COLS, (part + 1) * UP_COLS)
            branch[:, cols] += jnp.dot(act_buf[slot], down_buf[slot, :, cols], preferred_element_type=jnp.float32)

    pre_buf[0, :, :UP_COLS] = jnp.zeros((num_tokens, UP_COLS), jnp.bfloat16)
    each_block(lambda rows: normalize(0, rows, hid[rows, :].astype(jnp.float32)))
    normed_store(0).start()
    branch[...] = jnp.zeros_like(branch)

    @pl.loop(0, num_layers * steps)
    def _(step):
        layer, tile = step // steps, step % steps

        @pl.when(tile < num_tiles)
        def _():
            up_load(layer, tile).wait()

            @pl.when(tile + 1 < num_tiles)
            def _():
                up_load(layer, tile + 1).start()

            @pl.when((tile == num_tiles - 1) & (layer + 1 < num_layers))
            def _():
                up_load(layer + 1, 0).start()

            @pl.when(tile > 1)
            def _():
                pre_store(layer, tile - 2).wait()
                act_store(layer, tile - 2).wait()

            up_product(layer, tile)
            pre_store(layer, tile).start()

        @pl.when(tile == num_tiles)
        def _():
            activate((num_tiles - 1) % 2, parts - 1)

        @pl.when(tile > 0)
        def _():
            act_store(layer, tile - 1).start()
            down_load(layer, tile - 1).wait()

            @pl.when(tile < num_tiles)
            def _():
                down_load(layer, tile).start()

            @pl.when((tile == num_tiles) & (layer + 1 < num_layers))
            def _():
                down_load(layer + 1, 0).start()

            down_product(tile - 1)

        @pl.when(tile == num_tiles)
        def _():
            for back in (2, 1):
                pre_store(layer, num_tiles - back).wait()
                act_store(layer, num_tiles - back).wait()
            normed_store(layer).wait()

            @pl.when(layer + 1 < num_layers)
            def _():
                def to_next(rows):
                    normalize(layer + 1, rows, next_rows(layer, rows))
                    branch[rows, :] = jnp.zeros((NORM_ROWS, row_dim), jnp.float32)

                each_block(to_next)
                hid_store().start()
                normed_store(layer + 1).start()

    hid_store().wait()
    upstream_load.wait()
    bias_start = small_out.shape[1] - row_dim

    def grad_stores(rows):
        return (
            pltpu.make_async_copy(branch.at[rows, :], grad_top_out.at[rows, :], io_sem.at[0]),
            pltpu.make_async_copy(grad_b_buf.at[rows, :], grad_top_b_out.at[rows, :], io_sem.at[1]),
        )

    def top_rows(rows):
        top_f = next_rows(num_layers - 1, rows)
        top_scale = inverse_rms(top_f)
        top_hat = top_f * top_scale
        up_f = up_rows[rows, :].astype(jnp.float32)
        grad = top_scale * (up_f - top_hat * jnp.mean(up_f * top_hat, axis=-1, keepdims=True))
        branch[rows, :] = grad
        grad_b_buf[rows, :] = grad.astype(jnp.bfloat16)
        small_out[num_layers - 1:, bias_start:] += jnp.sum(grad, axis=0, keepdims=True)
        for copy in grad_stores(rows):
            copy.start()

    each_block(top_rows)
    for copy in grad_stores(pl.ds(0, num_tokens)):
        copy.wait()


def forward_pass(tokens, upstream, norm_gain, w_up, bias_up, w_down, bias_down, tile_cols):
    num_tokens, row_dim = tokens.shape
    num_layers, _, hidden = w_up.shape
    bf16, f32 = jnp.bfloat16, jnp.float32
    dma = pltpu.SemaphoreType.DMA
    any_spec = pl.BlockSpec(memory_space=pl.ANY)
    vmem_spec = pl.BlockSpec(memory_space=pltpu.VMEM)
    rows = (num_tokens, row_dim)
    wide = (num_layers, num_tokens, hidden)
    return pl.pallas_call(
        functools.partial(forward_kernel, (num_layers, hidden // tile_cols, tile_cols)),
        out_shape=(
            jax.ShapeDtypeStruct(rows, bf16),
            jax.ShapeDtypeStruct((num_layers,) + rows, bf16),
            jax.ShapeDtypeStruct(wide, bf16),
            jax.ShapeDtypeStruct(wide, bf16),
            jax.ShapeDtypeStruct(rows, f32),
            jax.ShapeDtypeStruct(rows, bf16),
            jax.ShapeDtypeStruct((num_layers, 2 * row_dim + hidden), f32),
        ),
        in_specs=[any_spec] * 4 + [vmem_spec] * 3,
        out_specs=(any_spec,) * 6 + (vmem_spec,),
        scratch_shapes=[
            pltpu.VMEM(rows, bf16),
            pltpu.VMEM(rows, bf16),
            pltpu.VMEM(rows, f32),
            pltpu.VMEM((2, row_dim, tile_cols), bf16),
            pltpu.VMEM((2, tile_cols, row_dim), bf16),
            pltpu.VMEM((2, num_tokens, tile_cols), bf16),
            pltpu.VMEM((2, num_tokens, tile_cols), bf16),
            pltpu.VMEM(rows, bf16),
            pltpu.VMEM(rows, bf16),
            pltpu.VMEM((num_layers, row_dim), f32),
            pltpu.VMEM((num_layers, hidden), f32),
            pltpu.VMEM((num_layers, row_dim), f32),
            dma((4,)), dma((2,)), dma((2,)), dma((2,)), dma((2,)),
        ],
        compiler_params=pltpu.CompilerParams(vmem_limit_bytes=60 * 2**20),
        name="forward",
    )(tokens, upstream, w_up, w_down, norm_gain, bias_up, bias_down)


def gelu_slope(values):
    square = values * values
    bend = jnp.tanh(values * (GELU_SCALE + GELU_SCALE * GELU_CUBIC * square))
    return 0.5 * (1.0 + bend) + (0.5 * values) * (1.0 - bend * bend) * (GELU_SCALE + 3.0 * GELU_SCALE * GELU_CUBIC * square)


def backward_kernel(sizes, *refs):
    num_layers, chunks_per_mat, row_dim, chunk_cols, region, down_subs, axis = sizes
    num_mats = 2 * num_layers
    hidden_dim = chunks_per_mat * chunk_cols
    hid_refs, refs = refs[:num_layers], refs[num_layers:]
    (normed, pre_act, activated, grad_top, grad_top_b, w_up, w_down, gain_in, small_in,
     gathered, small_out, grad_pre_hbm, grad_b_hbm) = refs[:13]
    part_count = 2 * COLORS * len(PART_GROUPS)
    part_refs, refs = refs[13:13 + part_count], refs[13 + part_count:]
    (rows_buf, cols_buf, sent_core, kept, recv_core, sent_1, sent_2, sent_3, recv_1, recv_2, recv_3, ring,
     weight_buf, pre_buf, grad_pre_buf, grad_b, grad_normed, hid_buf, grad_buf,
     small_recv, load_sem, grad_pre_sem, norm_sem, grad_b_sem, core_send, core_recv, out_send, out_recv, back_send, back_recv,
     share_send, share_recv, store_sem, small_send_sem, small_recv_sem, part_sem) = refs
    num_chunks = num_mats * chunks_per_mat
    full_chunks = num_chunks - sum(PART_GROUPS)
    half = COLORS * region
    me = lax.axis_index(axis)
    bits = [me % 2, (me // 2) % 2, (me // 4) % 2, me // 8]
    partners = [me + (1 << d) - 2 * (1 << d) * bits[d] for d in range(4)]
    core = bits[CORE]
    sent_bufs, recv_bufs = (sent_1, sent_2, sent_3), (recv_1, recv_2, recv_3)
    spans = (region // 2, region // 4, region // 8)

    def base(color, level):
        total = 0
        for step in range(level):
            total = total + bits[COLOR_DIMS[color][step]] * spans[step]
        return total

    def other(color, level):
        return base(color, level) + (1 - bits[COLOR_DIMS[color][level]]) * spans[level]

    def rows_at(start, size):
        return pl.ds(pl.multiple_of(start, spans[2]), size)

    def rows_load(mat, chunk):
        layer = num_layers - 1 - mat // 2
        if mat % 2 == 0:
            start = ((chunk % chunks_per_mat) // down_subs) * row_dim
            source = activated.at[layer, :, pl.ds(pl.multiple_of(start, 128), row_dim)]
        else:
            source = normed.at[layer]
        return pltpu.make_async_copy(source, rows_buf.at[chunk % 2], load_sem.at[0, chunk % 2])

    def weight_loads(mat, chunk):
        slot = chunk % 2
        layer = num_layers - 1 - mat // 2
        cols = pl.ds(pl.multiple_of((chunk % chunks_per_mat) * chunk_cols, 128), chunk_cols)
        if mat % 2 == 0:
            return [
                pltpu.make_async_copy(w_down.at[layer, cols, :], weight_buf.at[slot], load_sem.at[1, slot]),
                pltpu.make_async_copy(pre_act.at[layer, :, cols], pre_buf.at[slot], load_sem.at[2, slot]),
            ]
        return [
            pltpu.make_async_copy(
                w_up.at[layer, part * chunk_cols:(part + 1) * chunk_cols, cols],
                weight_buf.at[slot, :, part * chunk_cols:(part + 1) * chunk_cols], load_sem.at[1 + part, slot])
            for part in range(down_subs)
        ]

    def cols_load(mat, chunk):
        sub = chunk % chunks_per_mat
        if mat % 2 == 0:
            source = grad_top_b if mat == 0 else grad_b_hbm
            source = source.at[:, pl.ds(pl.multiple_of((sub % down_subs) * chunk_cols, 128), chunk_cols)]
        else:
            source = grad_pre_hbm.at[sub]
        return pltpu.make_async_copy(source, cols_buf.at[chunk % 2], load_sem.at[3, chunk % 2])

    def for_mat(chunk, action):
        for mat in range(num_mats):
            @pl.when(chunk // chunks_per_mat == mat)
            def _(mat=mat):
                action(mat)

    def grad_pre_store(sub):
        return pltpu.make_async_copy(grad_pre_buf, grad_pre_hbm.at[sub], grad_pre_sem)

    def core_copy(chunk):
        slot = chunk % RECV_SLOTS
        return pltpu.make_async_remote_copy(
            src_ref=sent_core, dst_ref=recv_core.at[slot], send_sem=core_send, recv_sem=core_recv.at[slot],
            device_id=(partners[CORE],), device_id_type=MESH)

    def out_copy(level, color, chunk):
        slot = chunk % RECV_SLOTS
        return pltpu.make_async_remote_copy(
            src_ref=sent_bufs[level].at[color], dst_ref=recv_bufs[level].at[slot, color],
            send_sem=out_send.at[level, color], recv_sem=out_recv.at[level, color, slot],
            device_id=(partners[COLOR_DIMS[color][level]],), device_id_type=MESH)

    def back_copy(level, color, chunk, arriving):
        slot = chunk % GATHER_SLOTS
        mine = ring.at[slot, core, color, rows_at(base(color, level + 1), spans[level]), :]
        theirs = ring.at[slot, core, color, rows_at(other(color, level), spans[level]), :]
        return pltpu.make_async_remote_copy(
            src_ref=mine, dst_ref=theirs if arriving else mine,
            send_sem=back_send.at[level, color, slot], recv_sem=back_recv.at[level, color, slot],
            device_id=(partners[COLOR_DIMS[color][level]],), device_id_type=MESH)

    def part_rows(color):
        return rows_at(base(color, 1), spans[0])

    def part_share_copy(color, chunk, arriving):
        slot = chunk % GATHER_SLOTS
        mine = ring.at[slot, core, color, part_rows(color), :]
        theirs = ring.at[slot, 1 - core, color, part_rows(color), :]
        return pltpu.make_async_remote_copy(
            src_ref=mine, dst_ref=theirs if arriving else mine,
            send_sem=back_send.at[0, color, slot], recv_sem=back_recv.at[0, color, slot],
            device_id=(partners[CORE],), device_id_type=MESH)

    def part_stores(group, chunk):
        slot = chunk % GATHER_SLOTS
        place = chunk - full_chunks - sum(PART_GROUPS[:group])
        copies = []
        for color in range(COLORS):
            for which in range(2):
                out_ref = part_refs[(group * COLORS + color) * 2 + which]
                source = ring.at[slot, core if which == 0 else 1 - core, color, part_rows(color), :]
                copies.append(pltpu.make_async_copy(
                    source, out_ref.at[place], part_sem.at[color, which, slot]))
        return copies

    def share_copy(chunk, arriving):
        slot = chunk % GATHER_SLOTS
        return pltpu.make_async_remote_copy(
            src_ref=ring.at[slot, core], dst_ref=ring.at[slot, 1 - core if arriving else core],
            send_sem=share_send.at[slot], recv_sem=share_recv.at[slot],
            device_id=(partners[CORE],), device_id_type=MESH)

    def store_copy(chunk):
        slot = chunk % GATHER_SLOTS
        return pltpu.make_async_copy(ring.at[slot], gathered.at[chunk], store_sem.at[slot])

    def small_copy(step):
        return pltpu.make_async_remote_copy(
            src_ref=small_out, dst_ref=small_recv.at[step], send_sem=small_send_sem.at[step],
            recv_sem=small_recv_sem.at[step], device_id=(partners[step],), device_id_type=MESH)

    def product(chunk, which_core, color):
        slot = chunk % 2
        start = pl.multiple_of(which_core * half + color * region, 128)
        return lax.dot_general(
            rows_buf[slot, :, pl.ds(start, region)], cols_buf[slot], TOKEN_DIMS, preferred_element_type=jnp.float32)

    def opens_layer(chunk):
        return (chunk > 0) & (chunk % (2 * chunks_per_mat) == 0)

    def load(chunk):
        for_mat(chunk, lambda mat: rows_load(mat, chunk).wait())
        for_mat(chunk, lambda mat: cols_load(mat, chunk).wait())
        after = chunk + 1

        @pl.when(after < num_chunks)
        def _():
            for_mat(after, lambda mat: rows_load(mat, after).start())

        @pl.when((after < num_chunks) & jnp.logical_not(opens_layer(after)))
        def _():
            for_mat(after, lambda mat: cols_load(mat, after).start())

    def load_weights(chunk):
        def arrive(mat):
            for copy in weight_loads(mat, chunk):
                copy.wait()

        for_mat(chunk, arrive)
        after, before = chunk + 1, chunk - 1

        @pl.when(after < num_chunks)
        def _():
            def start(mat):
                for copy in weight_loads(mat, after):
                    copy.start()

            for_mat(after, start)

        @pl.when((before >= 0) & ((before // chunks_per_mat) % 2 == 0))
        def _():
            grad_pre_store(before % chunks_per_mat).wait()

    def compute_sent(chunk):
        @pl.loop(0, COLORS)
        def _(color):
            sent_core[color] = product(chunk, 1 - core, color).astype(jnp.bfloat16)

    def share_core(chunk):
        core_copy(chunk).start()

    def compute_kept(chunk):
        slot = chunk % KEPT_SLOTS

        @pl.loop(0, COLORS)
        def _(color):
            kept[slot, color] = product(chunk, core, color)

    def halve(level, chunk, arrived):
        slot = chunk % KEPT_SLOTS
        recv_slot = chunk % RECV_SLOTS
        for color in range(COLORS):
            if level > 0:
                out_copy(level - 1, color, chunk).wait()
            held = base(color, level)

            def total(start, size, color=color, held=held):
                own = kept[slot, color, rows_at(start, size), :]
                return own + arrived[recv_slot, color, rows_at(start - held, size), :].astype(jnp.float32)

            if level < 3:
                mine = base(color, level + 1)
                sent_bufs[level][color] = total(other(color, level), spans[level]).astype(jnp.bfloat16)
                kept[slot, color, rows_at(mine, spans[level]), :] = total(mine, spans[level])
                out_copy(level, color, chunk).start()
            else:
                gather_slot = chunk % GATHER_SLOTS
                ring[gather_slot, core, color, rows_at(held, spans[2]), :] = total(held, spans[2]).astype(jnp.bfloat16)
                back_copy(2, color, chunk, False).start()

    def send_1(chunk):
        core_copy(chunk).wait()
        halve(0, chunk, recv_core)

    def send_2(chunk):
        halve(1, chunk, recv_1)

    def send_3(chunk):
        halve(2, chunk, recv_2)

    def send_back_3(chunk):
        halve(3, chunk, recv_3)

    def pass_back(level, chunk):
        for color in range(COLORS):
            back_copy(level + 1, color, chunk, True).wait()
            back_copy(level, color, chunk, False).start()

    def send_back_2(chunk):
        pass_back(1, chunk)

    def send_back_1(chunk):
        @pl.when(chunk < full_chunks)
        def _():
            pass_back(0, chunk)

        @pl.when(chunk >= full_chunks)
        def _():
            for color in range(COLORS):
                back_copy(1, color, chunk, True).wait()
                part_share_copy(color, chunk, False).start()

    def send_back_core(chunk):
        @pl.when(chunk < full_chunks)
        def _():
            for color in range(COLORS):
                back_copy(0, color, chunk, True).wait()
            share_copy(chunk, False).start()

        @pl.when(chunk >= full_chunks)
        def _():
            for color in range(COLORS):
                part_share_copy(color, chunk, True).wait()

        for group, size in enumerate(PART_GROUPS):
            first = full_chunks + sum(PART_GROUPS[:group])

            @pl.when((chunk >= first) & (chunk < first + size))
            def _(group=group):
                for copy in part_stores(group, chunk):
                    copy.start()

    def store(chunk):
        @pl.when(chunk < full_chunks)
        def _():
            share_copy(chunk, True).wait()
            store_copy(chunk).start()

        @pl.when((chunk > 0) & (chunk <= full_chunks))
        def _():
            store_copy(chunk - 1).wait()

        for group, size in enumerate(PART_GROUPS):
            first = full_chunks + sum(PART_GROUPS[:group])

            @pl.when((chunk >= first) & (chunk < first + size))
            def _(group=group):
                for copy in part_stores(group, chunk):
                    copy.wait()

    token_half = grad_b.shape[0] // 2

    def backward(part, chunk):
        slot = chunk % 2
        sub = chunk % chunks_per_mat
        mat = chunk // chunks_per_mat
        layer = num_layers - 1 - mat // 2

        @pl.when(mat % 2 == 0)
        def _():
            cols = slice(part * TILE, (part + 1) * TILE)

            @pl.loop(0, 2)
            def _(which):
                rows = pl.ds(pl.multiple_of(which * token_half, 128), token_half)
                grad_act = lax.dot_general(
                    grad_b[rows, :], weight_buf[slot, cols, :], FEATURE_DIMS, preferred_element_type=jnp.float32)
                grad_pre = grad_act * gelu_slope(pre_buf[slot, rows, cols].astype(jnp.float32))
                grad_pre_buf[rows, cols] = grad_pre.astype(jnp.bfloat16)
                start = row_dim + sub * chunk_cols + part * TILE
                small_out[pl.ds(layer, 1), pl.ds(pl.multiple_of(start, 128), TILE)] += jnp.sum(grad_pre, axis=0, keepdims=True)

            if part == chunk_cols // TILE - 1:
                grad_pre_store(sub).start()

        @pl.when(mat % 2 == 1)
        def _():
            pieces = row_dim // chunk_cols * (chunk_cols // TILE) // 3
            grad_rows = []
            for piece in range(part * pieces, (part + 1) * pieces):
                start, first = divmod(piece * TILE, chunk_cols)
                grad_rows.append((piece, lax.dot_general(
                    cols_buf[slot], weight_buf[slot, first:first + TILE, start * chunk_cols:(start + 1) * chunk_cols],
                    FEATURE_DIMS, preferred_element_type=jnp.float32)))
            for piece, value in grad_rows:
                grad_normed[:, piece * TILE:(piece + 1) * TILE] += value

    def norm_loads(layer, block):
        rows = pl.ds(pl.multiple_of(block * NORM_ROWS, NORM_ROWS), NORM_ROWS)
        slot = block % 2
        copies = [pltpu.make_async_copy(hid_refs[layer].at[rows, :], hid_buf.at[slot], norm_sem.at[0, slot])]
        if layer > 0:
            copies.append(pltpu.make_async_copy(grad_top.at[rows, :], grad_buf.at[slot], norm_sem.at[1, slot]))
        return copies

    def layer_input_grad(layer):
        num_blocks = grad_b.shape[0] // NORM_ROWS
        for copy in norm_loads(layer, 0):
            copy.start()

        @pl.loop(0, num_blocks)
        def _(block):
            @pl.when(block + 1 < num_blocks)
            def _():
                for copy in norm_loads(layer, block + 1):
                    copy.start()

            for copy in norm_loads(layer, block):
                copy.wait()
            rows = pl.ds(pl.multiple_of(block * NORM_ROWS, NORM_ROWS), NORM_ROWS)
            hid_f = hid_buf[block % 2].astype(jnp.float32)
            hid_scale = inverse_rms(hid_f)
            hid_hat = hid_f * hid_scale
            normed_grad = grad_normed[rows, :]
            small_out[layer:layer + 1, :row_dim] += jnp.sum(normed_grad * hid_hat, axis=0, keepdims=True)
            if layer > 0:
                grad_normed[rows, :] = jnp.zeros((NORM_ROWS, row_dim), jnp.float32)
                grad_hat = normed_grad * gain_in[layer:layer + 1, :].astype(jnp.float32)
                grad_new = grad_buf[block % 2] + hid_scale * (
                    grad_hat - hid_hat * jnp.mean(grad_hat * hid_hat, axis=-1, keepdims=True))
                grad_b[rows, :] = grad_new.astype(jnp.bfloat16)
                small_out[layer - 1:layer, row_dim + hidden_dim:] += jnp.sum(grad_new, axis=0, keepdims=True)

        if layer > 0:
            copy = pltpu.make_async_copy(grad_b, grad_b_hbm, grad_b_sem)
            copy.start()
            copy.wait()
            following = jnp.int32((num_layers - layer) * 2 * chunks_per_mat)
            cols_load((num_layers - layer) * 2, following).start()

    def input_grad(chunk):
        for layer in range(num_layers):
            last = (num_layers - 1 - layer) * 2 * chunks_per_mat + 2 * chunks_per_mat - 1

            @pl.when(chunk == last)
            def _(layer=layer):
                layer_input_grad(layer)

    events = dict(
        load=load, load_weights=load_weights, compute_sent=compute_sent, share_core=share_core, compute_kept=compute_kept, send_1=send_1, send_2=send_2, send_3=send_3,
        send_back_3=send_back_3, send_back_2=send_back_2, send_back_1=send_back_1, send_back_core=send_back_core, store=store,
        backward_0=functools.partial(backward, 0), backward_1=functools.partial(backward, 1),
        backward_2=functools.partial(backward, 2), input_grad=input_grad)

    first = jnp.int32(0)
    rows_load(0, first).start()
    cols_load(0, first).start()
    for copy in weight_loads(0, first):
        copy.start()
    grad_b_copy = pltpu.make_async_copy(grad_top_b, grad_b, grad_b_sem)
    grad_b_copy.start()
    barrier = pltpu.get_barrier_semaphore()
    for partner in partners:
        pl.semaphore_signal(barrier, inc=1, device_id=(partner,), device_id_type=MESH)
    small_out[...] = small_in[...]
    grad_normed[...] = jnp.zeros_like(grad_normed)
    grad_b_copy.wait()
    pl.semaphore_wait(barrier, 4)

    @pl.loop(0, num_chunks + MAX_LAG)
    def _(it):
        for step in range(4):
            @pl.when(it == num_chunks + step)
            def _(step=step):
                small_copy(step).start()
        for name, lag in PIPELINE:
            chunk = it - lag

            @pl.when((chunk >= 0) & (chunk < num_chunks))
            def _(name=name, chunk=chunk):
                events[name](chunk)
        for step in range(4):
            @pl.when(it == num_chunks + step)
            def _(step=step):
                small_copy(step).wait()
                small_out[...] += small_recv[step]


def backward_pass(hid_rows, saved, grad_top, grad_top_b, norm_gain, w_up, w_down, small, axis, chunk_cols):
    num_layers, row_dim, hidden = w_up.shape
    tokens = grad_top.shape[0]
    chunks_per_mat = hidden // chunk_cols
    region = row_dim // (2 * COLORS)
    half = (COLORS, region, chunk_cols)
    sizes = (num_layers, chunks_per_mat, row_dim, chunk_cols, region, row_dim // chunk_cols, axis)
    num_chunks = 2 * num_layers * chunks_per_mat
    bf16, f32 = jnp.bfloat16, jnp.float32
    dma = pltpu.SemaphoreType.DMA
    any_spec = pl.BlockSpec(memory_space=pl.ANY)
    vmem_spec = pl.BlockSpec(memory_space=pltpu.VMEM)
    full_chunks = num_chunks - sum(PART_GROUPS)
    part_shapes = [jax.ShapeDtypeStruct((size, region // 2, chunk_cols), bf16) for size in PART_GROUPS for _ in range(2 * COLORS)]
    gathered, small_sum, _, _, *parts = pl.pallas_call(
        functools.partial(backward_kernel, sizes),
        out_shape=[
            jax.ShapeDtypeStruct((full_chunks, 2) + half, bf16),
            jax.ShapeDtypeStruct(small.shape, f32),
            jax.ShapeDtypeStruct((chunks_per_mat, tokens, chunk_cols), bf16),
            jax.ShapeDtypeStruct((tokens, row_dim), bf16),
        ] + part_shapes,
        in_specs=[any_spec] * (num_layers + 7) + [vmem_spec] * 2,
        out_specs=[any_spec, vmem_spec, any_spec, any_spec] + [any_spec] * len(part_shapes),
        scratch_shapes=[
            pltpu.VMEM((2, tokens, row_dim), bf16),
            pltpu.VMEM((2, tokens, chunk_cols), bf16),
            pltpu.VMEM(half, bf16),
            pltpu.VMEM((KEPT_SLOTS,) + half, f32),
            pltpu.VMEM((RECV_SLOTS,) + half, bf16),
            pltpu.VMEM((COLORS, region // 2, chunk_cols), bf16),
            pltpu.VMEM((COLORS, region // 4, chunk_cols), bf16),
            pltpu.VMEM((COLORS, region // 8, chunk_cols), bf16),
            pltpu.VMEM((RECV_SLOTS, COLORS, region // 2, chunk_cols), bf16),
            pltpu.VMEM((RECV_SLOTS, COLORS, region // 4, chunk_cols), bf16),
            pltpu.VMEM((RECV_SLOTS, COLORS, region // 8, chunk_cols), bf16),
            pltpu.VMEM((GATHER_SLOTS, 2) + half, bf16),
            pltpu.VMEM((2, chunk_cols, row_dim), bf16),
            pltpu.VMEM((2, tokens, chunk_cols), bf16),
            pltpu.VMEM((tokens, chunk_cols), bf16),
            pltpu.VMEM((tokens, row_dim), bf16),
            pltpu.VMEM((tokens, row_dim), f32),
            pltpu.VMEM((2, NORM_ROWS, row_dim), bf16),
            pltpu.VMEM((2, NORM_ROWS, row_dim), f32),
            pltpu.VMEM((4,) + small.shape, f32),
            dma((4, 2)), dma, dma((2, 2)), dma,
            dma, dma((RECV_SLOTS,)), dma((3, COLORS)), dma((3, COLORS, RECV_SLOTS)),
            dma((3, COLORS, GATHER_SLOTS)), dma((3, COLORS, GATHER_SLOTS)), dma((GATHER_SLOTS,)), dma((GATHER_SLOTS,)),
            dma((GATHER_SLOTS,)), dma((4,)), dma((4,)), dma((COLORS, 2, GATHER_SLOTS)),
        ],
        compiler_params=pltpu.CompilerParams(collective_id=0, has_side_effects=True, vmem_limit_bytes=67043328),
        name="backward",
    )(*hid_rows, *saved, grad_top, grad_top_b, w_up, w_down, norm_gain, small)
    return gathered, small_sum, parts


def flip_pairs(num_devices, bit):
    return [(dev, dev ^ (1 << bit)) for dev in range(num_devices)]


def stream_blocks(num_blocks, start_loads, wait_loads, store_of, in_buf, out_buf):
    slots, region = in_buf.shape[0], in_buf.shape[2]
    for block in range(min(slots - 1, num_blocks)):
        start_loads(jnp.int32(block), block)

    @pl.loop(0, num_blocks)
    def _(block):
        slot = block % slots

        @pl.when(block + slots - 1 < num_blocks)
        def _():
            start_loads(block + slots - 1, (block + slots - 1) % slots)

        wait_loads(block, slot)

        @pl.when(block >= slots)
        def _():
            store_of(block - slots, slot).wait()

        for color in range(COLORS):
            out_buf[slot, color * region:(color + 1) * region, :] = in_buf[slot, color].astype(jnp.float32)
        store_of(block, slot).start()

    for block in range(max(num_blocks - slots, 0), num_blocks):
        store_of(jnp.int32(block), block % slots).wait()


def block_target(out_ref, layer, kind, down_subs, chunk, which_core, rows, cols):
    half = pl.multiple_of(which_core * rows, rows)
    if kind == 0:
        first = pl.multiple_of((chunk // down_subs) * 2 * rows + half, rows)
        return out_ref.at[layer, pl.ds(first, rows), pl.ds(pl.multiple_of((chunk % down_subs) * cols, 128), cols)]
    return out_ref.at[layer, pl.ds(half, rows), pl.ds(pl.multiple_of(chunk * cols, 128), cols)]


def widen_kernel(spec, *refs):
    first, count, place, layer, kind, down_subs, small_widths = spec
    if small_widths:
        gathered, small, out_ref, *small_outs, in_buf, out_buf, in_sem, out_sem = refs
        start = 0
        for width, small_out in zip(small_widths, small_outs):
            small_out[...] = small[:, start:start + width]
            start += width
    else:
        gathered, out_ref, in_buf, out_buf, in_sem, out_sem = refs
    rows, cols = out_buf.shape[1:]

    def load(block, slot):
        return pltpu.make_async_copy(gathered.at[first + block // 2, block % 2], in_buf.at[slot], in_sem.at[slot])

    def store(block, slot):
        target = block_target(out_ref, layer, kind, down_subs, place + block // 2, block % 2, rows, cols)
        return pltpu.make_async_copy(out_buf.at[slot], target, out_sem.at[slot])

    stream_blocks(
        2 * count, lambda block, slot: load(block, slot).start(), lambda block, slot: load(block, slot).wait(),
        store, in_buf, out_buf)


def join_kernel(spec, *refs):
    count, place, layer, kind, down_subs, axis = spec
    parts, (_, out_ref, in_buf, out_buf, in_sem, out_sem) = refs[:4 * COLORS], refs[4 * COLORS:]
    rows, cols = out_buf.shape[1:]
    part_rows = in_buf.shape[2] // 2
    me = lax.axis_index(axis)
    core = me % 2

    def copies(which, chunk, slot):
        found = []
        for color in range(COLORS):
            upper = (me >> COLOR_DIMS[color][0]) & 1
            for far in range(2):
                start = pl.multiple_of((upper if far == 0 else 1 - upper) * part_rows, part_rows)
                found.append(pltpu.make_async_copy(
                    parts[color * 4 + far * 2 + which].at[chunk],
                    in_buf.at[slot, color, pl.ds(start, part_rows), :], in_sem.at[slot]))
        return found

    def start_loads(block, slot):
        for which in range(2):
            @pl.when(block % 2 == which)
            def _(which=which):
                for copy in copies(which, block // 2, slot):
                    copy.start()

    def wait_loads(block, slot):
        for copy in copies(0, block // 2, slot):
            copy.wait()

    def store(block, slot):
        which_core = jnp.where(block % 2 == 0, core, 1 - core)
        target = block_target(out_ref, layer, kind, down_subs, place + block // 2, which_core, rows, cols)
        return pltpu.make_async_copy(out_buf.at[slot], target, out_sem.at[slot])

    stream_blocks(2 * count, start_loads, wait_loads, store, in_buf, out_buf)


def widen_scratch(region, cols):
    return [
        pltpu.VMEM((STREAM_SLOTS, COLORS, region, cols), jnp.bfloat16),
        pltpu.VMEM((STREAM_SLOTS, COLORS * region, cols), jnp.float32),
        pltpu.SemaphoreType.DMA((STREAM_SLOTS,)),
        pltpu.SemaphoreType.DMA((STREAM_SLOTS,)),
    ]


def widen_cost(count, region, cols):
    size = count * 2 * COLORS * region * cols
    return pl.CostEstimate(flops=500 * size, bytes_accessed=6 * size, transcendentals=0)


def widen(gathered, first, count, layer, kind, shape, down_subs, small, small_widths):
    region, cols = gathered.shape[3:]
    any_spec = pl.BlockSpec(memory_space=pl.ANY)
    vmem_spec = pl.BlockSpec(memory_space=pltpu.VMEM)
    smalls = [jax.ShapeDtypeStruct((small.shape[0], width), jnp.float32) for width in small_widths]
    return pl.pallas_call(
        functools.partial(widen_kernel, (first, count, 0, layer, kind, down_subs, small_widths)),
        in_specs=[any_spec] + [vmem_spec] * bool(smalls),
        out_specs=[any_spec] + [vmem_spec] * len(smalls),
        out_shape=[jax.ShapeDtypeStruct(shape, jnp.float32)] + smalls,
        scratch_shapes=widen_scratch(region, cols),
        cost_estimate=widen_cost(count, region, cols),
        compiler_params=pltpu.CompilerParams(vmem_limit_bytes=67043328),
    )(gathered, *([small] if smalls else []))


def join(parts, place, layer, kind, into, down_subs, axis):
    count, part_rows, cols = parts[0].shape
    any_spec = pl.BlockSpec(memory_space=pl.ANY)
    return pl.pallas_call(
        functools.partial(join_kernel, (count, place, layer, kind, down_subs, axis)),
        in_specs=[any_spec] * (len(parts) + 1),
        out_specs=any_spec,
        out_shape=jax.ShapeDtypeStruct(into.shape, jnp.float32),
        scratch_shapes=widen_scratch(2 * part_rows, cols),
        input_output_aliases={len(parts): 0},
        cost_estimate=widen_cost(count, 2 * part_rows, cols),
        compiler_params=pltpu.CompilerParams(vmem_limit_bytes=67043328),
    )(*parts, into)


def swap(array, axis, num_devices, bit):
    return lax.ppermute(array, axis, flip_pairs(num_devices, bit))


def full_gradients(gathered, parts, small, num_layers, row_dim, hidden, chunk_cols, axis, num_devices):
    per_mat = hidden // chunk_cols
    down_subs = row_dim // chunk_cols
    groups = range(len(PART_GROUPS))
    mine = [[parts[(group * COLORS + color) * 2] for color in range(COLORS)] for group in groups]
    theirs = [[parts[(group * COLORS + color) * 2 + 1] for color in range(COLORS)] for group in groups]
    far = [[swap(mine[group][color], axis, num_devices, COLOR_DIMS[color][0])
            for color in range(COLORS)] for group in groups]
    last = num_layers - 1
    down, *smalls = widen(
        gathered, 0, per_mat, last, 0, (num_layers, hidden, row_dim), down_subs, small, (row_dim, hidden, row_dim))
    up, = widen(gathered, per_mat, per_mat, last, 1, (num_layers, row_dim, hidden), down_subs, small, ())
    full = [down, up]
    for group in groups:
        kind, place = divmod(sum(PART_GROUPS[:group]), per_mat)
        pieces = []
        for color in range(COLORS):
            shared = swap(far[group][color], axis, num_devices, CORE)
            pieces += [mine[group][color], theirs[group][color], far[group][color], shared]
        full[kind] = join(pieces, place, 0, kind, full[kind], down_subs, axis)
    return smalls[0], full[1], smalls[1], full[0], smalls[2]


def solution(mesh):
    axis = mesh.axis_names[0]

    def device_grads(tokens, upstream, norm_gain, w_up, bias_up, w_down, bias_down):
        num_layers, width = norm_gain.shape
        hidden_width = w_up.shape[2]
        chunk_cols = width // 2
        hid_1, normed, pre_act, activated, grad_top, grad_top_b, small = forward_pass(
            tokens, upstream, norm_gain, w_up, bias_up, w_down, bias_down, width)
        gathered, small, parts = backward_pass(
            (tokens, hid_1), (normed, pre_act, activated), grad_top, grad_top_b, norm_gain, w_up, w_down, small, axis, chunk_cols)
        return full_gradients(gathered, parts, small, num_layers, width, hidden_width, chunk_cols, axis, mesh.size)

    row_spec = P(axis, None)
    full_spec = P()
    return jax.shard_map(
        device_grads,
        mesh=mesh,
        in_specs=(row_spec, row_spec, full_spec, full_spec, full_spec, full_spec, full_spec),
        out_specs=(full_spec, full_spec, full_spec, full_spec, full_spec),
        check_vma=False,
    )
```

profile of v0, /device:TPU:0, one launch (start us, length us, event | category | flops | bytes accessed | tf_op | source)
XLA Modules:
  0.0 691.9 jit_solution(1755597210152748614)
XLA Ops:
  0.6 98.2 %forward.1 = (bf16[1024,1536]{1,0:T(8,128)(2,1)}, bf16[2,1024,1536]{2,1,0:T(8,128)(2,1)}, bf16[2,1024,6144]{2,1,0:T(8,128)(2,1)}, bf16[2,1024,6144]{2,1,0:T(8,12...) custom-call(bf16[1024,1536]{1,0:T(8,128)(2,1)} %refs_0_.1, ...), custom_call_target="tpu_custom_call" | custom-call | tf_op jit(solution)/shard_map/forward/pallas_call | solution.py:229
  98.8 438.1 %backward.1 = (bf16[16,2,3,256,768]{4,3,2,1,0:T(8,128)(2,1)}, f32[2,9216]{1,0:T(2,128)}, bf16[8,1024,768]{2,1,0:T(8,128)(2,1)}, bf16[1024,1536]{1,0:T(8,128)(2,1...) custom-call(bf16[1024,1536]{1,0:T(8,128)(2,1)} %refs_0_.1, ...), custom_call_target="tpu_custom_call" | custom-call | tf_op jit(solution)/shard_map/backward/pallas_call | solution.py:699
  536.9 1.9 collective-permute-start.10
  538.8 1.7 collective-permute-start.8
  540.5 0.7 collective-permute-start
  541.3 1.3 collective-permute-start.12
  542.6 14.5 %collective-permute-done.10.refs_10_ = bf16[4,128,768]{2,1,0:T(8,128)(2,1)S(1)} collective-permute-done((bf16[4,128,768]{2,1,0:T(8,128)(2,1)}, bf16[4,128,768]{2,1,0:T(8,128)(2,1)S(1)}, u32[]{:S(2)}, u32[]{:S(2)}) %collective-permute-start.10) | collective-permute-done | bytes 786464 | tf_op jit(solution)/shard_map/ppermute | solution.py:888
  557.1 1.6 collective-permute-start.14
  558.6 0.8 collective-permute-done.6.refs_2_
  559.6 1.7 collective-permute-start.2
  561.3 15.0 %collective-permute-done.refs_2_ = bf16[4,128,768]{2,1,0:T(8,128)(2,1)S(1)} collective-permute-done((bf16[4,128,768]{2,1,0:T(8,128)(2,1)}, bf16[4,128,768]{2,1,0:T(8,128)(2,1)S(1)}, u32[]{:S(2)}, u32[]{:S(2)}) %collective-permute-start) | collective-permute-done | bytes 786464 | tf_op jit(solution)/shard_map/ppermute | solution.py:888
  576.4 33.7 %collective-permute-done.2.refs_6_ = bf16[4,128,768]{2,1,0:T(8,128)(2,1)} collective-permute-done((bf16[4,128,768]{2,1,0:T(8,128)(2,1)}, bf16[4,128,768]{2,1,0:T(8,128)(2,1)}, u32[]{:S(2)}, u32[]{:S(2)}) %collective-permute-start.2) | collective-permute-done | bytes 786464 | tf_op jit(solution)/shard_map/ppermute | solution.py:888
  610.1 1.2 collective-permute-done.4.refs_10_
  611.3 0.5 collective-permute-start.9
  611.9 0.5 collective-permute-start.13
  612.6 1.1 collective-permute-done.7.refs_3_
  613.8 1.0 collective-permute-done.9.refs_7_
  614.9 1.0 collective-permute-done.1.refs_3_
  616.0 0.7 copy-done.5
  616.8 18.3 %shard_map.111.refs_12_ = f32[2,1536,6144]{2,1,0:T(8,128)} custom-call(bf16[16,2,3,256,768]{4,3,2,1,0:T(8,128)(2,1)} %get-tuple-element.43.refs_0_), custom_call_target="tpu_custom_call" | custom-call | flops 4718592000 | bytes 56623104 | tf_op jit(solution)/shard_map/pallas_call | solution.py:861
  635.1 19.8 %shard_map.110 = (f32[2,6144,1536]{2,1,0:T(8,128)}, f32[2,1536]{1,0:T(2,128)}, f32[2,6144]{1,0:T(2,128)}, f32[2,1536]{1,0:T(2,128)}) custom-call(bf16[16,2,3,256,768]{4,3,2,1,0:T(8,128)(2,1)} %get-tuple-element.43.refs_0_, f32[2,9216]{1,0:T(2,128)} %get-tuple-element.44.refs_1_), custom_call_target="tpu_custom_call" | custom-call | flops 4718592000 | bytes 56623104 | tf_op jit(solution)/shard_map/pallas_call | solution.py:861
  655.0 9.2 %shard_map.112.refs_12_ = f32[2,1536,6144]{2,1,0:T(8,128)} custom-call(bf16[4,128,768]{2,1,0:T(8,128)(2,1)} %get-tuple-element.52.refs_0_, bf16[4,128,768]{2,1,0:T(8,128)(2,1)} %get-tuple-element.53.refs_1_, bf16[4,128,768]{2,1,0:T(8,128)(2,1)} %copy-done.2, bf16[4,128,768]{2,1,0:T(8,128)(2,1)} %copy-done.6, ...), custom_call_target="tpu_custom_call", output_to_operand_aliasing={{}: (12, {})} | custom-call | flops 2359296000 | bytes 28311552 | tf_op jit(solution)/shard_map/pallas_call | solution.py:875
  664.1 9.2 %shard_map.113 = f32[2,1536,6144]{2,1,0:T(8,128)} custom-call(bf16[4,128,768]{2,1,0:T(8,128)(2,1)} %get-tuple-element.46.refs_0_, bf16[4,128,768]{2,1,0:T(8,128)(2,1)} %get-tuple-element.47.refs_1_, bf16[4,128,768]{2,1,0:T(8,128)(2,1)} %copy-done, bf16[4,128,768]{2,1,0:T(8,128)(2,1)} %copy-done.5, ...), custom_call_target="tpu_custom_call", output_to_operand_aliasing={{}: (12, {})} | custom-call | flops 2359296000 | bytes 28311552 | tf_op jit(solution)/shard_map/pallas_call | solution.py:875
  673.3 18.4 %shard_map.114 = f32[2,6144,1536]{2,1,0:T(8,128)} custom-call(bf16[8,128,768]{2,1,0:T(8,128)(2,1)} %get-tuple-element.59.refs_0_, bf16[8,128,768]{2,1,0:T(8,128)(2,1)} %get-tuple-element.60.refs_1_, bf16[8,128,768]{2,1,0:T(8,128)(2,1)} %collective-permute-done.12.refs_2_, ...), custom_call_target="tpu_custom_call", output_to_operand_aliasing={{}: (12, {})} | custom-call | flops 4718592000 | bytes 56623104 | tf_op jit(solution)/shard_map/pallas_call | solution.py:875
  (35 shorter events, 1.1 us)
Async XLA Ops:
  536.9 20.2 %collective-permute-start.10 = (bf16[4,128,768]{2,1,0:T(8,128)(2,1)}, bf16[4,128,768]{2,1,0:T(8,128)(2,1)S(1)}, u32[]{:S(2)}, u32[]{:S(2)}) collective-permute-start(bf16[4,128,768]{2,1,0:T(8,128)(2,1)} %get-tuple-element.56.refs_8_), channel_id=1, source_target_pairs={{0,8},{1,9},{2,10},{3,11},{4,12},{5,13},{6,14},{7,15},{8,0},{9,1},... | collective-permute-start | bytes 2359304 | tf_op jit(solution)/shard_map/ppermute | solution.py:888
  538.8 20.6 %collective-permute-start.6 = (bf16[4,128,768]{2,1,0:T(8,128)(2,1)}, bf16[4,128,768]{2,1,0:T(8,128)(2,1)S(1)}, u32[]{:S(2)}, u32[]{:S(2)}) collective-permute-start(bf16[4,128,768]{2,1,0:T(8,128)(2,1)} %get-tuple-element.52.refs_0_), channel_id=1, source_target_pairs={{0,2},{1,3},{2,0},{3,1},{4,6},{5,7},{6,4},{7,5},{8,10},{9,11},{10,... | collective-permute-start | bytes 2359304 | tf_op jit(solution)/shard_map/ppermute | solution.py:888
  538.8 20.8 %collective-permute-start.8 = (bf16[4,128,768]{2,1,0:T(8,128)(2,1)}, bf16[4,128,768]{2,1,0:T(8,128)(2,1)S(1)}, u32[]{:S(2)}, u32[]{:S(2)}) collective-permute-start(bf16[4,128,768]{2,1,0:T(8,128)(2,1)} %get-tuple-element.54.refs_4_), channel_id=1, source_target_pairs={{0,4},{1,5},{2,6},{3,7},{4,0},{5,1},{6,2},{7,3},{8,12},{9,13},{10,... | collective-permute-start | bytes 2359304 | tf_op jit(solution)/shard_map/ppermute | solution.py:888
  540.5 35.7 %collective-permute-start = (bf16[4,128,768]{2,1,0:T(8,128)(2,1)}, bf16[4,128,768]{2,1,0:T(8,128)(2,1)S(1)}, u32[]{:S(2)}, u32[]{:S(2)}) collective-permute-start(bf16[4,128,768]{2,1,0:T(8,128)(2,1)} %get-tuple-element.46.refs_0_), channel_id=1, source_target_pairs={{0,2},{1,3},{2,0},{3,1},{4,6},{5,7},{6,4},{7,5},{8,10},{9,11},{10,... | collective-permute-start | bytes 2359304 | tf_op jit(solution)/shard_map/ppermute | solution.py:888
  541.3 70.1 %collective-permute-start.12 = (bf16[8,128,768]{2,1,0:T(8,128)(2,1)}, bf16[8,128,768]{2,1,0:T(8,128)(2,1)}, u32[]{:S(2)}, u32[]{:S(2)}) collective-permute-start(bf16[8,128,768]{2,1,0:T(8,128)(2,1)} %get-tuple-element.59.refs_0_), channel_id=1, source_target_pairs={{0,2},{1,3},{2,0},{3,1},{4,6},{5,7},{6,4},{7,5},{8,10},{9,11},{10,... | collective-permute-start | bytes 4718600 | tf_op jit(solution)/shard_map/ppermute | solution.py:888
  557.1 58.8 %copy-start.1 = (bf16[4,128,768]{2,1,0:T(8,128)(2,1)}, bf16[4,128,768]{2,1,0:T(8,128)(2,1)S(1)}, u32[]{:S(2)}) copy-start(bf16[4,128,768]{2,1,0:T(8,128)(2,1)S(1)} %collective-permute-done.10.refs_10_) | copy-start | bytes 2359300
  557.1 54.8 %collective-permute-start.14 = (bf16[8,128,768]{2,1,0:T(8,128)(2,1)}, bf16[8,128,768]{2,1,0:T(8,128)(2,1)}, u32[]{:S(2)}, u32[]{:S(2)}) collective-permute-start(bf16[8,128,768]{2,1,0:T(8,128)(2,1)} %get-tuple-element.61.refs_4_), channel_id=1, source_target_pairs={{0,4},{1,5},{2,6},{3,7},{4,0},{5,1},{6,2},{7,3},{8,12},{9,13},{10,... | collective-permute-start | bytes 4718600 | tf_op jit(solution)/shard_map/ppermute | solution.py:888
  559.4 56.6 %copy-start.2 = (bf16[4,128,768]{2,1,0:T(8,128)(2,1)}, bf16[4,128,768]{2,1,0:T(8,128)(2,1)S(1)}, u32[]{:S(2)}) copy-start(bf16[4,128,768]{2,1,0:T(8,128)(2,1)S(1)} %collective-permute-done.6.refs_2_) | copy-start | bytes 2359300
  559.4 52.5 %collective-permute-start.16 = (bf16[8,128,768]{2,1,0:T(8,128)(2,1)}, bf16[8,128,768]{2,1,0:T(8,128)(2,1)}, u32[]{:S(2)}, u32[]{:S(2)}) collective-permute-start(bf16[8,128,768]{2,1,0:T(8,128)(2,1)} %get-tuple-element.63.refs_8_), channel_id=1, source_target_pairs={{0,8},{1,9},{2,10},{3,11},{4,12},{5,13},{6,14},{7,15},{8,0},{9,1},... | collective-permute-start | bytes 4718600 | tf_op jit(solution)/shard_map/ppermute | solution.py:888
  559.6 56.4 %copy-start.3 = (bf16[4,128,768]{2,1,0:T(8,128)(2,1)}, bf16[4,128,768]{2,1,0:T(8,128)(2,1)S(1)}, u32[]{:S(2)}) copy-start(bf16[4,128,768]{2,1,0:T(8,128)(2,1)S(1)} %collective-permute-done.8.refs_6_) | copy-start | bytes 2359300
  559.6 50.5 %collective-permute-start.2 = (bf16[4,128,768]{2,1,0:T(8,128)(2,1)}, bf16[4,128,768]{2,1,0:T(8,128)(2,1)}, u32[]{:S(2)}, u32[]{:S(2)}) collective-permute-start(bf16[4,128,768]{2,1,0:T(8,128)(2,1)} %get-tuple-element.48.refs_4_), channel_id=1, source_target_pairs={{0,4},{1,5},{2,6},{3,7},{4,0},{5,1},{6,2},{7,3},{8,12},{9,13},{10,... | collective-permute-start | bytes 2359304 | tf_op jit(solution)/shard_map/ppermute | solution.py:888
  576.3 35.6 %copy-start = (bf16[4,128,768]{2,1,0:T(8,128)(2,1)}, bf16[4,128,768]{2,1,0:T(8,128)(2,1)S(1)}, u32[]{:S(2)}) copy-start(bf16[4,128,768]{2,1,0:T(8,128)(2,1)S(1)} %collective-permute-done.refs_2_) | copy-start | bytes 2359300
  576.3 35.1 %collective-permute-start.4 = (bf16[4,128,768]{2,1,0:T(8,128)(2,1)}, bf16[4,128,768]{2,1,0:T(8,128)(2,1)}, u32[]{:S(2)}, u32[]{:S(2)}) collective-permute-start(bf16[4,128,768]{2,1,0:T(8,128)(2,1)} %get-tuple-element.50.refs_8_), channel_id=1, source_target_pairs={{0,8},{1,9},{2,10},{3,11},{4,12},{5,13},{6,14},{7,15},{8,0},{9,1},... | collective-permute-start | bytes 2359304 | tf_op jit(solution)/shard_map/ppermute | solution.py:888
  610.1 2.3 collective-permute-start.11
  611.3 2.3 collective-permute-start.7
  611.3 3.4 collective-permute-start.9
  611.9 4.0 collective-permute-start.1
  611.9 61.4 %collective-permute-start.13 = (bf16[8,128,768]{2,1,0:T(8,128)(2,1)}, bf16[8,128,768]{2,1,0:T(8,128)(2,1)}, u32[]{:S(2)}, u32[]{:S(2)}) collective-permute-start(bf16[8,128,768]{2,1,0:T(8,128)(2,1)} %collective-permute-done.12.refs_2_), channel_id=1, source_target_pairs={{0,1},{1,0},{2,3},{3,2},{4,5},{5,4},{6,7},{7,6},{8,9},{9,8},{10,11... | collective-permute-start | bytes 4718600 | tf_op jit(solution)/shard_map/ppermute | solution.py:888
  612.4 3.6 copy-start.4
  612.4 60.9 %collective-permute-start.15 = (bf16[8,128,768]{2,1,0:T(8,128)(2,1)}, bf16[8,128,768]{2,1,0:T(8,128)(2,1)}, u32[]{:S(2)}, u32[]{:S(2)}) collective-permute-start(bf16[8,128,768]{2,1,0:T(8,128)(2,1)} %collective-permute-done.14.refs_6_), channel_id=1, source_target_pairs={{0,1},{1,0},{2,3},{3,2},{4,5},{5,4},{6,7},{7,6},{8,9},{9,8},{10,11... | collective-permute-start | bytes 4718600 | tf_op jit(solution)/shard_map/ppermute | solution.py:888
  613.6 2.4 copy-start.6
  613.6 59.7 %collective-permute-start.17 = (bf16[8,128,768]{2,1,0:T(8,128)(2,1)}, bf16[8,128,768]{2,1,0:T(8,128)(2,1)}, u32[]{:S(2)}, u32[]{:S(2)}) collective-permute-start(bf16[8,128,768]{2,1,0:T(8,128)(2,1)} %collective-permute-done.16.refs_10_), channel_id=1, source_target_pairs={{0,1},{1,0},{2,3},{3,2},{4,5},{5,4},{6,7},{7,6},{8,9},{9,8},{10,11... | collective-permute-start | bytes 4718600 | tf_op jit(solution)/shard_map/ppermute | solution.py:888
  614.7 49.4 %collective-permute-start.3 = (bf16[4,128,768]{2,1,0:T(8,128)(2,1)}, bf16[4,128,768]{2,1,0:T(8,128)(2,1)}, u32[]{:S(2)}, u32[]{:S(2)}) collective-permute-start(bf16[4,128,768]{2,1,0:T(8,128)(2,1)} %collective-permute-done.2.refs_6_), channel_id=1, source_target_pairs={{0,1},{1,0},{2,3},{3,2},{4,5},{5,4},{6,7},{7,6},{8,9},{9,8},{10,11... | collective-permute-start | bytes 2359304 | tf_op jit(solution)/shard_map/ppermute | solution.py:888
  615.9 48.3 %collective-permute-start.5 = (bf16[4,128,768]{2,1,0:T(8,128)(2,1)}, bf16[4,128,768]{2,1,0:T(8,128)(2,1)}, u32[]{:S(2)}, u32[]{:S(2)}) collective-permute-start(bf16[4,128,768]{2,1,0:T(8,128)(2,1)} %collective-permute-done.4.refs_10_), channel_id=1, source_target_pairs={{0,1},{1,0},{2,3},{3,2},{4,5},{5,4},{6,7},{7,6},{8,9},{9,8},{10,11... | collective-permute-start | bytes 2359304 | tf_op jit(solution)/shard_map/ppermute | solution.py:888
  (2 other events, 2.2 us)
where the time goes:
time: 692 us
  Pallas kernels  611 us (88%)
  waiting for transfers between devices  68.3 us (10%)
  starting transfers between devices  10.8 us (2%)
    pallas_call x1, Pallas kernels, backward_pass(): pl.pallas_call(functools.partial(backward_kernel, sizes), out_shape=[jax....  438 us
    pallas_call x1, Pallas kernels, forward_pass(): pl.pallas_call(functools.partial(forward_kernel, (num_layers, hidden // t...  98.2 us
    ppermute x18, waiting for transfers between devices, swap(): return lax.ppermute(array, axis, flip_pairs(num_devices, bit))  68.3 us
    pallas_call x2, Pallas kernels, widen(): pl.pallas_call(functools.partial(widen_kernel, (first, count, 0, layer, k...  38.2 us
    pallas_call x3, Pallas kernels, join(): pl.pallas_call(functools.partial(join_kernel, (count, place, layer, kind,...  36.7 us
  transfers between devices with their start and end apart: 18, of which 9 were waited for; matrix products, arithmetic and copies ran while one was open for 0% of the time, Pallas kernels for 8%

commit v1 on v0

--- a/solution.py
+++ b/solution.py
@@ -16,12 +16,13 @@
 CORE, DIM_X, DIM_Y, DIM_Z = range(4)
 COLOR_DIMS = ((DIM_X, DIM_Y, DIM_Z), (DIM_Y, DIM_Z, DIM_X), (DIM_Z, DIM_X, DIM_Y))
 PIPELINE = (
-    ("send_back_2", 4), ("load", 0), ("compute_sent", 0), ("send_back_3", 3), ("send_back_core", 6), ("share_core", 0),
-    ("send_3", 2), ("compute_kept", 0), ("load_weights", 0), ("backward_0", 0), ("send_back_1", 5), ("store", 6), ("send_2", 1),
-    ("backward_1", 0), ("send_1", 0), ("backward_2", 0), ("input_grad", 0),
+    ("load", 0), ("compute_sent", 0), ("share_core", 0), ("send_3", 2), ("send_back_2", 4), ("send_back_1", 5),
+    ("compute_kept", 0), ("send_back_core", 6), ("load_weights", 0), ("backward_0", 0), ("send_2", 1), ("backward_1", 0),
+    ("send_1", 0), ("backward_2", 0), ("send_back_3", 2), ("store", 6), ("input_grad", 0),
 )
 MAX_LAG = 6
 PART_GROUPS = (8, 4, 4)
+WIDEN_CALLS = (8, 6, 2)
 RECV_SLOTS = 2
 KEPT_SLOTS = 3
 GATHER_SLOTS = 6
@@ -78,10 +79,10 @@
     tokens_load = pltpu.make_async_copy(tokens, hid, io_sem.at[0])
     tokens_load.start()
     up_load(0, 0).start()
-    down_load(0, 0).start()
     upstream_load = pltpu.make_async_copy(upstream, up_rows, io_sem.at[3])
-    upstream_load.start()
     small_out[...] = jnp.zeros_like(small_out)
+    branch[...] = jnp.zeros_like(branch)
+    pre_buf[0, :, :UP_COLS] = jnp.zeros((num_tokens, UP_COLS), jnp.bfloat16)
     gain[...] = gain_in[...].astype(jnp.float32)
     bias_up[...] = bias_up_in[...].astype(jnp.float32)
     bias_down[...] = bias_down_in[...].astype(jnp.float32)
@@ -125,10 +126,7 @@
             cols = slice(part * UP_COLS, (part + 1) * UP_COLS)
             branch[:, cols] += jnp.dot(act_buf[slot], down_buf[slot, :, cols], preferred_element_type=jnp.float32)
 
-    pre_buf[0, :, :UP_COLS] = jnp.zeros((num_tokens, UP_COLS), jnp.bfloat16)
     each_block(lambda rows: normalize(0, rows, hid[rows, :].astype(jnp.float32)))
-    normed_store(0).start()
-    branch[...] = jnp.zeros_like(branch)
 
     @pl.loop(0, num_layers * steps)
     def _(step):
@@ -145,6 +143,12 @@
             @pl.when((tile == num_tiles - 1) & (layer + 1 < num_layers))
             def _():
                 up_load(layer + 1, 0).start()
+
+            @pl.when(step == 0)
+            def _():
+                normed_store(0).start()
+                down_load(0, 0).start()
+                upstream_load.start()
 
             @pl.when(tile > 1)
             def _():
@@ -419,6 +423,12 @@
         for_mat(chunk, lambda mat: cols_load(mat, chunk).wait())
         after = chunk + 1
 
+        @pl.when(chunk == 0)
+        def _():
+            grad_b_copy.start()
+            for copy in weight_loads(0, chunk):
+                copy.start()
+
         @pl.when(after < num_chunks)
         def _():
             for_mat(after, lambda mat: rows_load(mat, after).start())
@@ -434,6 +444,10 @@
 
         for_mat(chunk, arrive)
         after, before = chunk + 1, chunk - 1
+
+        @pl.when(chunk == 0)
+        def _():
+            grad_b_copy.wait()
 
         @pl.when(after < num_chunks)
         def _():
@@ -651,16 +665,12 @@
     first = jnp.int32(0)
     rows_load(0, first).start()
     cols_load(0, first).start()
-    for copy in weight_loads(0, first):
-        copy.start()
     grad_b_copy = pltpu.make_async_copy(grad_top_b, grad_b, grad_b_sem)
-    grad_b_copy.start()
     barrier = pltpu.get_barrier_semaphore()
     for partner in partners:
         pl.semaphore_signal(barrier, inc=1, device_id=(partner,), device_id_type=MESH)
     small_out[...] = small_in[...]
     grad_normed[...] = jnp.zeros_like(grad_normed)
-    grad_b_copy.wait()
     pl.semaphore_wait(barrier, 4)
 
     @pl.loop(0, num_chunks + MAX_LAG)
@@ -778,7 +788,9 @@
 
 
 def widen_kernel(spec, *refs):
-    first, count, place, layer, kind, down_subs, small_widths = spec
+    first, count, place, layer, kind, down_subs, small_widths, in_place = spec
+    if in_place:
+        refs = refs[:1 + bool(small_widths)] + refs[2 + bool(small_widths):]
     if small_widths:
         gathered, small, out_ref, *small_outs, in_buf, out_buf, in_sem, out_sem = refs
         start = 0
@@ -853,20 +865,21 @@
     return pl.CostEstimate(flops=500 * size, bytes_accessed=6 * size, transcendentals=0)
 
 
-def widen(gathered, first, count, layer, kind, shape, down_subs, small, small_widths):
+def widen(gathered, first, count, place, layer, kind, shape, into, down_subs, small, small_widths):
     region, cols = gathered.shape[3:]
     any_spec = pl.BlockSpec(memory_space=pl.ANY)
     vmem_spec = pl.BlockSpec(memory_space=pltpu.VMEM)
     smalls = [jax.ShapeDtypeStruct((small.shape[0], width), jnp.float32) for width in small_widths]
     return pl.pallas_call(
-        functools.partial(widen_kernel, (first, count, 0, layer, kind, down_subs, small_widths)),
-        in_specs=[any_spec] + [vmem_spec] * bool(smalls),
+        functools.partial(widen_kernel, (first, count, place, layer, kind, down_subs, small_widths, into is not None)),
+        in_specs=[any_spec] + [vmem_spec] * bool(smalls) + [any_spec] * (into is not None),
         out_specs=[any_spec] + [vmem_spec] * len(smalls),
         out_shape=[jax.ShapeDtypeStruct(shape, jnp.float32)] + smalls,
+        input_output_aliases={} if into is None else {1 + bool(smalls): 0},
         scratch_shapes=widen_scratch(region, cols),
         cost_estimate=widen_cost(count, region, cols),
         compiler_params=pltpu.CompilerParams(vmem_limit_bytes=67043328),
-    )(gathered, *([small] if smalls else []))
+    )(gathered, *([small] if smalls else []), *([] if into is None else [into]))
 
 
 def join(parts, place, layer, kind, into, down_subs, axis):
@@ -897,10 +910,15 @@
     far = [[swap(mine[group][color], axis, num_devices, COLOR_DIMS[color][0])
             for color in range(COLORS)] for group in groups]
     last = num_layers - 1
-    down, *smalls = widen(
-        gathered, 0, per_mat, last, 0, (num_layers, hidden, row_dim), down_subs, small, (row_dim, hidden, row_dim))
-    up, = widen(gathered, per_mat, per_mat, last, 1, (num_layers, row_dim, hidden), down_subs, small, ())
-    full = [down, up]
+    full = [None, None]
+    shapes = ((num_layers, hidden, row_dim), (num_layers, row_dim, hidden))
+    for call, count in enumerate(WIDEN_CALLS):
+        first = sum(WIDEN_CALLS[:call])
+        kind, place = divmod(first, per_mat)
+        small_widths = (row_dim, hidden, row_dim) if call == 0 else ()
+        full[kind], *rest = widen(
+            gathered, first, count, place, last, kind, shapes[kind], full[kind], down_subs, small, small_widths)
+        smalls = rest or smalls
     for group in groups:
         kind, place = divmod(sum(PART_GROUPS[:group]), per_mat)
         pieces = []

time: 692 us -> 686 us (level)
  waiting for transfers between devices: 68.3 us -> 61.1 us
    ppermute x18, waiting for transfers between devices: 68.3 us -> 61.1 us  [swap(): return lax.ppermute(array, axis, flip_pairs(num_devices, bit))]
    pallas_call x2 -> x3, Pallas kernels: 38.2 us -> 38.6 us  [widen(): pl.pallas_call(functools.partial(widen_kernel, (first, count, place, laye...]
where the time goes in v1:
time: 686 us
  Pallas kernels  609 us (89%)
  waiting for transfers between devices  61.1 us (9%)
  starting transfers between devices  13.6 us (2%)
    pallas_call x1, Pallas kernels, backward_pass(): pl.pallas_call(functools.partial(backward_kernel, sizes), out_shape=[jax....  436 us
    pallas_call x1, Pallas kernels, forward_pass(): pl.pallas_call(functools.partial(forward_kernel, (num_layers, hidden // t...  97.7 us
    ppermute x18, waiting for transfers between devices, swap(): return lax.ppermute(array, axis, flip_pairs(num_devices, bit))  61.1 us
    pallas_call x3, Pallas kernels, widen(): pl.pallas_call(functools.partial(widen_kernel, (first, count, place, laye...  38.6 us
    pallas_call x3, Pallas kernels, join(): pl.pallas_call(functools.partial(join_kernel, (count, place, layer, kind,...  36.7 us
  transfers between devices with their start and end apart: 18, of which 9 were waited for; matrix products, arithmetic and copies ran while one was open for 0% of the time, Pallas kernels for 8%

profile of v1, /device:TPU:0, one launch (start us, length us, event | category | flops | bytes accessed | tf_op | source)
XLA Modules:
  0.0 685.8 jit_solution(5197046425002308007)
XLA Ops:
  0.6 97.7 %forward.1 = (bf16[1024,1536]{1,0:T(8,128)(2,1)}, bf16[2,1024,1536]{2,1,0:T(8,128)(2,1)}, bf16[2,1024,6144]{2,1,0:T(8,128)(2,1)}, bf16[2,1024,6144]{2,1,0:T(8,12...) custom-call(bf16[1024,1536]{1,0:T(8,128)(2,1)} %refs_0_.1, ...), custom_call_target="tpu_custom_call" | custom-call | tf_op jit(solution)/shard_map/forward/pallas_call | solution.py:233
  98.3 436.3 %backward.1 = (bf16[16,2,3,256,768]{4,3,2,1,0:T(8,128)(2,1)}, f32[2,9216]{1,0:T(2,128)}, bf16[8,1024,768]{2,1,0:T(8,128)(2,1)}, bf16[1024,1536]{1,0:T(8,128)(2,1...) custom-call(bf16[1024,1536]{1,0:T(8,128)(2,1)} %refs_0_.1, ...), custom_call_target="tpu_custom_call" | custom-call | tf_op jit(solution)/shard_map/backward/pallas_call | solution.py:709
  534.7 2.4 collective-permute-start
  537.1 0.6 collective-permute-start.2
  537.7 0.9 collective-permute-start.4
  539.2 2.0 collective-permute-start.8
  541.2 14.5 %collective-permute-done.refs_2_ = bf16[4,128,768]{2,1,0:T(8,128)(2,1)S(1)} collective-permute-done((bf16[4,128,768]{2,1,0:T(8,128)(2,1)}, bf16[4,128,768]{2,1,0:T(8,128)(2,1)S(1)}, u32[]{:S(2)}, u32[]{:S(2)}) %collective-permute-start) | collective-permute-done | bytes 786464 | tf_op jit(solution)/shard_map/ppermute | solution.py:901
  555.7 2.0 collective-permute-start.10
  558.2 1.7 collective-permute-start.14
  559.9 12.7 %collective-permute-done.6.refs_2_ = bf16[4,128,768]{2,1,0:T(8,128)(2,1)S(1)} collective-permute-done((bf16[4,128,768]{2,1,0:T(8,128)(2,1)}, bf16[4,128,768]{2,1,0:T(8,128)(2,1)S(1)}, u32[]{:S(2)}, u32[]{:S(2)}) %collective-permute-start.6) | collective-permute-done | bytes 786464 | tf_op jit(solution)/shard_map/ppermute | solution.py:901
  572.6 2.0 collective-permute-start.16
  575.2 1.8 collective-permute-done.1.refs_3_
  577.1 1.0 collective-permute-done.7.refs_3_
  578.2 27.9 %collective-permute-done.12.refs_2_ = bf16[8,128,768]{2,1,0:T(8,128)(2,1)} collective-permute-done((bf16[8,128,768]{2,1,0:T(8,128)(2,1)}, bf16[8,128,768]{2,1,0:T(8,128)(2,1)}, u32[]{:S(2)}, u32[]{:S(2)}) %collective-permute-start.12) | collective-permute-done | bytes 1572896 | tf_op jit(solution)/shard_map/ppermute | solution.py:901
  606.1 1.5 collective-permute-done.14.refs_6_
  607.5 1.2 collective-permute-done.16.refs_10_
  608.8 0.5 collective-permute-start.3
  609.7 0.6 copy-done.7
  610.2 13.6 %shard_map.111.refs_1_ = f32[2,1536,6144]{2,1,0:T(8,128)} custom-call(bf16[16,2,3,256,768]{4,3,2,1,0:T(8,128)(2,1)} %get-tuple-element.43.refs_0_), custom_call_target="tpu_custom_call" | custom-call | flops 3538944000 | bytes 42467328 | tf_op jit(solution)/shard_map/pallas_call | solution.py:873
  623.9 5.2 shard_map.112.refs_12_
  629.0 19.8 %shard_map.110 = (f32[2,6144,1536]{2,1,0:T(8,128)}, f32[2,1536]{1,0:T(2,128)}, f32[2,6144]{1,0:T(2,128)}, f32[2,1536]{1,0:T(2,128)}) custom-call(bf16[16,2,3,256,768]{4,3,2,1,0:T(8,128)(2,1)} %get-tuple-element.43.refs_0_, f32[2,9216]{1,0:T(2,128)} %get-tuple-element.44.refs_1_), custom_call_target="tpu_custom_call" | custom-call | flops 4718592000 | bytes 56623104 | tf_op jit(solution)/shard_map/pallas_call | solution.py:873
  648.9 9.2 %shard_map.113.refs_12_ = f32[2,1536,6144]{2,1,0:T(8,128)} custom-call(bf16[4,128,768]{2,1,0:T(8,128)(2,1)} %get-tuple-element.52.refs_0_, bf16[4,128,768]{2,1,0:T(8,128)(2,1)} %get-tuple-element.53.refs_1_, bf16[4,128,768]{2,1,0:T(8,128)(2,1)} %copy-done.1, bf16[4,128,768]{2,1,0:T(8,128)(2,1)} %copy-done.5, ...), custom_call_target="tpu_custom_call", output_to_operand_aliasing={{}: (12, {})} | custom-call | flops 2359296000 | bytes 28311552 | tf_op jit(solution)/shard_map/pallas_call | solution.py:888
  658.1 9.2 %shard_map.114 = f32[2,1536,6144]{2,1,0:T(8,128)} custom-call(bf16[4,128,768]{2,1,0:T(8,128)(2,1)} %get-tuple-element.46.refs_0_, bf16[4,128,768]{2,1,0:T(8,128)(2,1)} %get-tuple-element.47.refs_1_, bf16[4,128,768]{2,1,0:T(8,128)(2,1)} %copy-done, bf16[4,128,768]{2,1,0:T(8,128)(2,1)} %copy-done.4, ...), custom_call_target="tpu_custom_call", output_to_operand_aliasing={{}: (12, {})} | custom-call | flops 2359296000 | bytes 28311552 | tf_op jit(solution)/shard_map/pallas_call | solution.py:888
  667.3 18.4 %shard_map.115 = f32[2,6144,1536]{2,1,0:T(8,128)} custom-call(bf16[8,128,768]{2,1,0:T(8,128)(2,1)} %get-tuple-element.59.refs_0_, bf16[8,128,768]{2,1,0:T(8,128)(2,1)} %get-tuple-element.60.refs_1_, bf16[8,128,768]{2,1,0:T(8,128)(2,1)} %collective-permute-done.12.refs_2_, ...), custom_call_target="tpu_custom_call", output_to_operand_aliasing={{}: (12, {})} | custom-call | flops 4718592000 | bytes 56623104 | tf_op jit(solution)/shard_map/pallas_call | solution.py:888
  (36 shorter events, 2.1 us)
Async XLA Ops:
  534.7 21.0 %collective-permute-start = (bf16[4,128,768]{2,1,0:T(8,128)(2,1)}, bf16[4,128,768]{2,1,0:T(8,128)(2,1)S(1)}, u32[]{:S(2)}, u32[]{:S(2)}) collective-permute-start(bf16[4,128,768]{2,1,0:T(8,128)(2,1)} %get-tuple-element.46.refs_0_), channel_id=1, source_target_pairs={{0,2},{1,3},{2,0},{3,1},{4,6},{5,7},{6,4},{7,5},{8,10},{9,11},{10,... | collective-permute-start | bytes 2359304 | tf_op jit(solution)/shard_map/ppermute | solution.py:901
  537.1 20.7 %collective-permute-start.2 = (bf16[4,128,768]{2,1,0:T(8,128)(2,1)}, bf16[4,128,768]{2,1,0:T(8,128)(2,1)}, u32[]{:S(2)}, u32[]{:S(2)}) collective-permute-start(bf16[4,128,768]{2,1,0:T(8,128)(2,1)} %get-tuple-element.48.refs_4_), channel_id=1, source_target_pairs={{0,4},{1,5},{2,6},{3,7},{4,0},{5,1},{6,2},{7,3},{8,12},{9,13},{10,... | collective-permute-start | bytes 2359304 | tf_op jit(solution)/shard_map/ppermute | solution.py:901
  537.7 20.4 %collective-permute-start.4 = (bf16[4,128,768]{2,1,0:T(8,128)(2,1)}, bf16[4,128,768]{2,1,0:T(8,128)(2,1)}, u32[]{:S(2)}, u32[]{:S(2)}) collective-permute-start(bf16[4,128,768]{2,1,0:T(8,128)(2,1)} %get-tuple-element.50.refs_8_), channel_id=1, source_target_pairs={{0,8},{1,9},{2,10},{3,11},{4,12},{5,13},{6,14},{7,15},{8,0},{9,1},... | collective-permute-start | bytes 2359304 | tf_op jit(solution)/shard_map/ppermute | solution.py:901
  538.6 33.9 %collective-permute-start.6 = (bf16[4,128,768]{2,1,0:T(8,128)(2,1)}, bf16[4,128,768]{2,1,0:T(8,128)(2,1)S(1)}, u32[]{:S(2)}, u32[]{:S(2)}) collective-permute-start(bf16[4,128,768]{2,1,0:T(8,128)(2,1)} %get-tuple-element.52.refs_0_), channel_id=1, source_target_pairs={{0,2},{1,3},{2,0},{3,1},{4,6},{5,7},{6,4},{7,5},{8,10},{9,11},{10,... | collective-permute-start | bytes 2359304 | tf_op jit(solution)/shard_map/ppermute | solution.py:901
  539.2 35.5 %collective-permute-start.8 = (bf16[4,128,768]{2,1,0:T(8,128)(2,1)}, bf16[4,128,768]{2,1,0:T(8,128)(2,1)S(1)}, u32[]{:S(2)}, u32[]{:S(2)}) collective-permute-start(bf16[4,128,768]{2,1,0:T(8,128)(2,1)} %get-tuple-element.54.refs_4_), channel_id=1, source_target_pairs={{0,4},{1,5},{2,6},{3,7},{4,0},{5,1},{6,2},{7,3},{8,12},{9,13},{10,... | collective-permute-start | bytes 2359304 | tf_op jit(solution)/shard_map/ppermute | solution.py:901
  555.7 18.9 %copy-start = (bf16[4,128,768]{2,1,0:T(8,128)(2,1)}, bf16[4,128,768]{2,1,0:T(8,128)(2,1)S(1)}, u32[]{:S(2)}) copy-start(bf16[4,128,768]{2,1,0:T(8,128)(2,1)S(1)} %collective-permute-done.refs_2_) | copy-start | bytes 2359300
  555.7 19.3 %collective-permute-start.10 = (bf16[4,128,768]{2,1,0:T(8,128)(2,1)}, bf16[4,128,768]{2,1,0:T(8,128)(2,1)S(1)}, u32[]{:S(2)}, u32[]{:S(2)}) collective-permute-start(bf16[4,128,768]{2,1,0:T(8,128)(2,1)} %get-tuple-element.56.refs_8_), channel_id=1, source_target_pairs={{0,8},{1,9},{2,10},{3,11},{4,12},{5,13},{6,14},{7,15},{8,0},{9,1},... | collective-permute-start | bytes 2359304 | tf_op jit(solution)/shard_map/ppermute | solution.py:901
  557.9 48.2 %collective-permute-start.12 = (bf16[8,128,768]{2,1,0:T(8,128)(2,1)}, bf16[8,128,768]{2,1,0:T(8,128)(2,1)}, u32[]{:S(2)}, u32[]{:S(2)}) collective-permute-start(bf16[8,128,768]{2,1,0:T(8,128)(2,1)} %get-tuple-element.59.refs_0_), channel_id=1, source_target_pairs={{0,2},{1,3},{2,0},{3,1},{4,6},{5,7},{6,4},{7,5},{8,10},{9,11},{10,... | collective-permute-start | bytes 4718600 | tf_op jit(solution)/shard_map/ppermute | solution.py:901
  558.2 49.4 %collective-permute-start.14 = (bf16[8,128,768]{2,1,0:T(8,128)(2,1)}, bf16[8,128,768]{2,1,0:T(8,128)(2,1)}, u32[]{:S(2)}, u32[]{:S(2)}) collective-permute-start(bf16[8,128,768]{2,1,0:T(8,128)(2,1)} %get-tuple-element.61.refs_4_), channel_id=1, source_target_pairs={{0,4},{1,5},{2,6},{3,7},{4,0},{5,1},{6,2},{7,3},{8,12},{9,13},{10,... | collective-permute-start | bytes 4718600 | tf_op jit(solution)/shard_map/ppermute | solution.py:901
  572.6 4.4 copy-start.1
  572.6 36.2 %collective-permute-start.16 = (bf16[8,128,768]{2,1,0:T(8,128)(2,1)}, bf16[8,128,768]{2,1,0:T(8,128)(2,1)}, u32[]{:S(2)}, u32[]{:S(2)}) collective-permute-start(bf16[8,128,768]{2,1,0:T(8,128)(2,1)} %get-tuple-element.63.refs_8_), channel_id=1, source_target_pairs={{0,8},{1,9},{2,10},{3,11},{4,12},{5,13},{6,14},{7,15},{8,0},{9,1},... | collective-permute-start | bytes 4718600 | tf_op jit(solution)/shard_map/ppermute | solution.py:901
  574.6 3.4 copy-start.2
  574.6 2.3 collective-permute-start.1
  575.1 33.7 %copy-start.3 = (bf16[4,128,768]{2,1,0:T(8,128)(2,1)}, bf16[4,128,768]{2,1,0:T(8,128)(2,1)S(1)}, u32[]{:S(2)}) copy-start(bf16[4,128,768]{2,1,0:T(8,128)(2,1)S(1)} %collective-permute-done.10.refs_10_) | copy-start | bytes 2359300
  575.1 3.0 collective-permute-start.7
  576.9 32.4 %copy-start.4 = (bf16[4,128,768]{2,1,0:T(8,128)(2,1)}, bf16[4,128,768]{2,1,0:T(8,128)(2,1)S(1)}, u32[]{:S(2)}) copy-start(bf16[4,128,768]{2,1,0:T(8,128)(2,1)S(1)} %collective-permute-done.1.refs_3_) | copy-start | bytes 2359300
  576.9 31.8 %collective-permute-start.9 = (bf16[4,128,768]{2,1,0:T(8,128)(2,1)S(1)}, bf16[4,128,768]{2,1,0:T(8,128)(2,1)S(1)}, u32[]{:S(2)}, u32[]{:S(2)}) collective-permute-start(bf16[4,128,768]{2,1,0:T(8,128)(2,1)S(1)} %collective-permute-done.8.refs_6_), channel_id=1, source_target_pairs={{0,1},{1,0},{2,3},{3,2},{4,5},{5,4},{6,7},{7,6},{8,9},{9,8},{10,11... | collective-permute-start | bytes 2359304 | tf_op jit(solution)/shard_map/ppermute | solution.py:901
  578.1 31.3 %copy-start.5 = (bf16[4,128,768]{2,1,0:T(8,128)(2,1)}, bf16[4,128,768]{2,1,0:T(8,128)(2,1)S(1)}, u32[]{:S(2)}) copy-start(bf16[4,128,768]{2,1,0:T(8,128)(2,1)S(1)} %collective-permute-done.7.refs_3_) | copy-start | bytes 2359300
  578.1 31.3 %collective-permute-start.11 = (bf16[4,128,768]{2,1,0:T(8,128)(2,1)S(1)}, bf16[4,128,768]{2,1,0:T(8,128)(2,1)S(1)}, u32[]{:S(2)}, u32[]{:S(2)}) collective-permute-start(bf16[4,128,768]{2,1,0:T(8,128)(2,1)S(1)} %collective-permute-done.10.refs_10_), channel_id=1, source_target_pairs={{0,1},{1,0},{2,3},{3,2},{4,5},{5,4},{6,7},{7,6},{8,9},{9,8},{10,11... | collective-permute-start | bytes 2359304 | tf_op jit(solution)/shard_map/ppermute | solution.py:901
  606.1 61.2 %collective-permute-start.13 = (bf16[8,128,768]{2,1,0:T(8,128)(2,1)}, bf16[8,128,768]{2,1,0:T(8,128)(2,1)}, u32[]{:S(2)}, u32[]{:S(2)}) collective-permute-start(bf16[8,128,768]{2,1,0:T(8,128)(2,1)} %collective-permute-done.12.refs_2_), channel_id=1, source_target_pairs={{0,1},{1,0},{2,3},{3,2},{4,5},{5,4},{6,7},{7,6},{8,9},{9,8},{10,11... | collective-permute-start | bytes 4718600 | tf_op jit(solution)/shard_map/ppermute | solution.py:901
  607.5 59.7 %collective-permute-start.15 = (bf16[8,128,768]{2,1,0:T(8,128)(2,1)}, bf16[8,128,768]{2,1,0:T(8,128)(2,1)}, u32[]{:S(2)}, u32[]{:S(2)}) collective-permute-start(bf16[8,128,768]{2,1,0:T(8,128)(2,1)} %collective-permute-done.14.refs_6_), channel_id=1, source_target_pairs={{0,1},{1,0},{2,3},{3,2},{4,5},{5,4},{6,7},{7,6},{8,9},{9,8},{10,11... | collective-permute-start | bytes 4718600 | tf_op jit(solution)/shard_map/ppermute | solution.py:901
  608.8 58.5 %collective-permute-start.17 = (bf16[8,128,768]{2,1,0:T(8,128)(2,1)}, bf16[8,128,768]{2,1,0:T(8,128)(2,1)}, u32[]{:S(2)}, u32[]{:S(2)}) collective-permute-start(bf16[8,128,768]{2,1,0:T(8,128)(2,1)} %collective-permute-done.16.refs_10_), channel_id=1, source_target_pairs={{0,1},{1,0},{2,3},{3,2},{4,5},{5,4},{6,7},{7,6},{8,9},{9,8},{10,11... | collective-permute-start | bytes 4718600 | tf_op jit(solution)/shard_map/ppermute | solution.py:901
  608.8 49.2 %collective-permute-start.3 = (bf16[4,128,768]{2,1,0:T(8,128)(2,1)}, bf16[4,128,768]{2,1,0:T(8,128)(2,1)}, u32[]{:S(2)}, u32[]{:S(2)}) collective-permute-start(bf16[4,128,768]{2,1,0:T(8,128)(2,1)} %collective-permute-done.2.refs_6_), channel_id=1, source_target_pairs={{0,1},{1,0},{2,3},{3,2},{4,5},{5,4},{6,7},{7,6},{8,9},{9,8},{10,11... | collective-permute-start | bytes 2359304 | tf_op jit(solution)/shard_map/ppermute | solution.py:901
  609.3 48.7 %collective-permute-start.5 = (bf16[4,128,768]{2,1,0:T(8,128)(2,1)}, bf16[4,128,768]{2,1,0:T(8,128)(2,1)}, u32[]{:S(2)}, u32[]{:S(2)}) collective-permute-start(bf16[4,128,768]{2,1,0:T(8,128)(2,1)} %collective-permute-done.4.refs_10_), channel_id=1, source_target_pairs={{0,1},{1,0},{2,3},{3,2},{4,5},{5,4},{6,7},{7,6},{8,9},{9,8},{10,11... | collective-permute-start | bytes 2359304 | tf_op jit(solution)/shard_map/ppermute | solution.py:901
  (2 other events, 1.8 us)

commit v2 on v1

--- a/solution.py
+++ b/solution.py
@@ -9,7 +9,6 @@
 
 
 EPSILON = 1e-6
-TOKEN_DIMS = (((0,), (0,)), ((), ()))
 FEATURE_DIMS = (((1,), (1,)), ((), ()))
 MESH = pl.DeviceIdType.MESH
 COLORS = 3
@@ -21,8 +20,8 @@
     ("send_1", 0), ("backward_2", 0), ("send_back_3", 2), ("store", 6), ("input_grad", 0),
 )
 MAX_LAG = 6
-PART_GROUPS = (8, 4, 4)
-WIDEN_CALLS = (8, 6, 2)
+PART_GROUPS = (7, 5, 3, 3)
+WIDEN_CALLS = (8, 6)
 RECV_SLOTS = 2
 KEPT_SLOTS = 3
 GATHER_SLOTS = 6
@@ -278,7 +277,7 @@
      gathered, small_out, grad_pre_hbm, grad_b_hbm) = refs[:13]
     part_count = 2 * COLORS * len(PART_GROUPS)
     part_refs, refs = refs[13:13 + part_count], refs[13 + part_count:]
-    (rows_buf, cols_buf, sent_core, kept, recv_core, sent_1, sent_2, sent_3, recv_1, recv_2, recv_3, ring,
+    (rows_buf, turned, cols_buf, sent_core, kept, recv_core, sent_1, sent_2, sent_3, recv_1, recv_2, recv_3, ring,
      weight_buf, pre_buf, grad_pre_buf, grad_b, grad_normed, hid_buf, grad_buf,
      small_recv, load_sem, grad_pre_sem, norm_sem, grad_b_sem, core_send, core_recv, out_send, out_recv, back_send, back_recv,
      share_send, share_recv, store_sem, small_send_sem, small_recv_sem, part_sem) = refs
@@ -311,7 +310,7 @@
             source = activated.at[layer, :, pl.ds(pl.multiple_of(start, 128), row_dim)]
         else:
             source = normed.at[layer]
-        return pltpu.make_async_copy(source, rows_buf.at[chunk % 2], load_sem.at[0, chunk % 2])
+        return pltpu.make_async_copy(source, rows_buf, load_sem.at[0, 0])
 
     def weight_loads(mat, chunk):
         slot = chunk % 2
@@ -409,17 +408,30 @@
             src_ref=small_out, dst_ref=small_recv.at[step], send_sem=small_send_sem.at[step],
             recv_sem=small_recv_sem.at[step], device_id=(partners[step],), device_id_type=MESH)
 
-    def product(chunk, which_core, color):
-        slot = chunk % 2
-        start = pl.multiple_of(which_core * half + color * region, 128)
-        return lax.dot_general(
-            rows_buf[slot, :, pl.ds(start, region)], cols_buf[slot], TOKEN_DIMS, preferred_element_type=jnp.float32)
+    def product(chunk, which_core):
+        rows = pl.ds(pl.multiple_of(which_core * half, 128), half)
+        return jnp.dot(turned[rows, :], cols_buf[chunk % 2], preferred_element_type=jnp.float32)
 
     def opens_layer(chunk):
         return (chunk > 0) & (chunk % (2 * chunks_per_mat) == 0)
 
+    def turn_rows(chunk):
+        down = (chunk // chunks_per_mat) % 2 == 0
+
+        @pl.when((chunk % chunks_per_mat == 0) | (down & (chunk % down_subs == 0)))
+        def _():
+            rows_load(1, chunk).wait()
+            for start in range(0, row_dim, TILE):
+                turned[start:start + TILE, :] = rows_buf[:, start:start + TILE].T
+            for period, here in ((down_subs, down), (chunks_per_mat, jnp.logical_not(down))):
+                following = chunk + period
+
+                @pl.when(here & (following < num_chunks))
+                def _(following=following):
+                    for_mat(following, lambda mat: rows_load(mat, following).start())
+
     def load(chunk):
-        for_mat(chunk, lambda mat: rows_load(mat, chunk).wait())
+        turn_rows(chunk)
         for_mat(chunk, lambda mat: cols_load(mat, chunk).wait())
         after = chunk + 1
 
@@ -428,10 +440,6 @@
             grad_b_copy.start()
             for copy in weight_loads(0, chunk):
                 copy.start()
-
-        @pl.when(after < num_chunks)
-        def _():
-            for_mat(after, lambda mat: rows_load(mat, after).start())
 
         @pl.when((after < num_chunks) & jnp.logical_not(opens_layer(after)))
         def _():
@@ -462,19 +470,17 @@
             grad_pre_store(before % chunks_per_mat).wait()
 
     def compute_sent(chunk):
-        @pl.loop(0, COLORS)
-        def _(color):
-            sent_core[color] = product(chunk, 1 - core, color).astype(jnp.bfloat16)
+        value = product(chunk, 1 - core).astype(jnp.bfloat16)
+        for color in range(COLORS):
+            sent_core[color] = value[color * region:(color + 1) * region]
 
     def share_core(chunk):
         core_copy(chunk).start()
 
     def compute_kept(chunk):
-        slot = chunk % KEPT_SLOTS
-
-        @pl.loop(0, COLORS)
-        def _(color):
-            kept[slot, color] = product(chunk, core, color)
+        value = product(chunk, core)
+        for color in range(COLORS):
+            kept[chunk % KEPT_SLOTS, color] = value[color * region:(color + 1) * region]
 
     def halve(level, chunk, arrived):
         slot = chunk % KEPT_SLOTS
@@ -717,7 +723,8 @@
         in_specs=[any_spec] * (num_layers + 7) + [vmem_spec] * 2,
         out_specs=[any_spec, vmem_spec, any_spec, any_spec] + [any_spec] * len(part_shapes),
         scratch_shapes=[
-            pltpu.VMEM((2, tokens, row_dim), bf16),
+            pltpu.VMEM((tokens, row_dim), bf16),
+            pltpu.VMEM((row_dim, tokens), bf16),
             pltpu.VMEM((2, tokens, chunk_cols), bf16),
             pltpu.VMEM(half, bf16),
             pltpu.VMEM((KEPT_SLOTS,) + half, f32),
@@ -814,7 +821,7 @@
 
 
 def join_kernel(spec, *refs):
-    count, place, layer, kind, down_subs, axis = spec
+    skip, count, place, layer, kind, down_subs, axis = spec
     parts, (_, out_ref, in_buf, out_buf, in_sem, out_sem) = refs[:4 * COLORS], refs[4 * COLORS:]
     rows, cols = out_buf.shape[1:]
     part_rows = in_buf.shape[2] // 2
@@ -828,7 +835,7 @@
             for far in range(2):
                 start = pl.multiple_of((upper if far == 0 else 1 - upper) * part_rows, part_rows)
                 found.append(pltpu.make_async_copy(
-                    parts[color * 4 + far * 2 + which].at[chunk],
+                    parts[color * 4 + far * 2 + which].at[skip + chunk],
                     in_buf.at[slot, color, pl.ds(start, part_rows), :], in_sem.at[slot]))
         return found
 
@@ -882,11 +889,19 @@
     )(gathered, *([small] if smalls else []), *([] if into is None else [into]))
 
 
-def join(parts, place, layer, kind, into, down_subs, axis):
-    count, part_rows, cols = parts[0].shape
+def split_at_gradients(first, count, per_mat):
+    sizes = []
+    while count:
+        sizes.append(min(count, per_mat - first % per_mat))
+        first, count = first + sizes[-1], count - sizes[-1]
+    return sizes
+
+
+def join(parts, skip, count, place, layer, kind, into, down_subs, axis):
+    _, part_rows, cols = parts[0].shape
     any_spec = pl.BlockSpec(memory_space=pl.ANY)
     return pl.pallas_call(
-        functools.partial(join_kernel, (count, place, layer, kind, down_subs, axis)),
+        functools.partial(join_kernel, (skip, count, place, layer, kind, down_subs, axis)),
         in_specs=[any_spec] * (len(parts) + 1),
         out_specs=any_spec,
         out_shape=jax.ShapeDtypeStruct(into.shape, jnp.float32),
@@ -919,13 +934,18 @@
         full[kind], *rest = widen(
             gathered, first, count, place, last, kind, shapes[kind], full[kind], down_subs, small, small_widths)
         smalls = rest or smalls
+    chunk = 2 * num_layers * per_mat - sum(PART_GROUPS)
     for group in groups:
-        kind, place = divmod(sum(PART_GROUPS[:group]), per_mat)
         pieces = []
         for color in range(COLORS):
             shared = swap(far[group][color], axis, num_devices, CORE)
             pieces += [mine[group][color], theirs[group][color], far[group][color], shared]
-        full[kind] = join(pieces, place, 0, kind, full[kind], down_subs, axis)
+        skip = 0
+        for count in split_at_gradients(chunk, PART_GROUPS[group], per_mat):
+            mat, place = divmod(chunk, per_mat)
+            kind, layer = mat % 2, last - mat // 2
+            full[kind] = join(pieces, skip, count, place, layer, kind, full[kind], down_subs, axis)
+            chunk, skip = chunk + count, skip + count
     return smalls[0], full[1], smalls[1], full[0], smalls[2]
 
 

time: 686 us -> 693 us (1.010)
  waiting for transfers between devices: 61.1 us -> 73.8 us
  Pallas kernels: 609 us -> 600 us
    ppermute x18 -> x24, waiting for transfers between devices: 61.1 us -> 73.8 us  [swap(): return lax.ppermute(array, axis, flip_pairs(num_devices, bit))]
    pallas_call x1, Pallas kernels: 436 us -> 427 us  [backward_pass(): pl.pallas_call(functools.partial(backward_kernel, sizes), out_shape=[jax....]
    pallas_call x3 -> x6, Pallas kernels: 36.7 us -> 42.5 us  [join(): pl.pallas_call(functools.partial(join_kernel, (skip, count, place, layer,...]
    pallas_call x3 -> x2, Pallas kernels: 38.6 us -> 33.5 us  [widen(): pl.pallas_call(functools.partial(widen_kernel, (first, count, place, laye...]
    ppermute x18 -> x24, starting transfers between devices: 13.6 us -> 14.6 us  [swap(): return lax.ppermute(array, axis, flip_pairs(num_devices, bit))]
  transfers between devices with their start and end apart: 18 -> 24, of which waited for: 9 -> 8; matrix products, arithmetic and copies ran while one was open for 0% -> 0% of each run, Pallas kernels for 8% -> 10%
where the time goes in v2:
time: 693 us; the launch traced here: 692 us
  Pallas kernels  600 us (87%)
  waiting for transfers between devices  73.8 us (11%)
  starting transfers between devices  14.6 us (2%)
    pallas_call x1, Pallas kernels, backward_pass(): pl.pallas_call(functools.partial(backward_kernel, sizes), out_shape=[jax....  427 us
    pallas_call x1, Pallas kernels, forward_pass(): pl.pallas_call(functools.partial(forward_kernel, (num_layers, hidden // t...  97.7 us
    ppermute x24, waiting for transfers between devices, swap(): return lax.ppermute(array, axis, flip_pairs(num_devices, bit))  73.8 us
    pallas_call x6, Pallas kernels, join(): pl.pallas_call(functools.partial(join_kernel, (skip, count, place, layer,...  42.5 us
    pallas_call x2, Pallas kernels, widen(): pl.pallas_call(functools.partial(widen_kernel, (first, count, place, laye...  33.5 us
    ppermute x24, starting transfers between devices, swap(): return lax.ppermute(array, axis, flip_pairs(num_devices, bit))  14.6 us
  transfers between devices with their start and end apart: 24, of which 8 were waited for; matrix products, arithmetic and copies ran while one was open for 0% of the time, Pallas kernels for 10%

profile of v2, /device:TPU:0, one launch (start us, length us, event | category | flops | bytes accessed | tf_op | source)
XLA Modules:
  0.0 692.0 jit_solution(8023168283693878302)
XLA Ops:
  0.6 97.7 %forward.1 = (bf16[1024,1536]{1,0:T(8,128)(2,1)}, bf16[2,1024,1536]{2,1,0:T(8,128)(2,1)}, bf16[2,1024,6144]{2,1,0:T(8,128)(2,1)}, bf16[2,1024,6144]{2,1,0:T(8,12...) custom-call(bf16[1024,1536]{1,0:T(8,128)(2,1)} %refs_0_.1, ...), custom_call_target="tpu_custom_call" | custom-call | tf_op jit(solution)/shard_map/forward/pallas_call | solution.py:232
  98.4 426.7 %backward.1 = (bf16[14,2,3,256,768]{4,3,2,1,0:T(8,128)(2,1)}, f32[2,9216]{1,0:T(2,128)}, bf16[8,1024,768]{2,1,0:T(8,128)(2,1)}, bf16[1024,1536]{1,0:T(8,128)(2,1...) custom-call(bf16[1024,1536]{1,0:T(8,128)(2,1)} %refs_0_.1, ...), custom_call_target="tpu_custom_call" | custom-call | tf_op jit(solution)/shard_map/backward/pallas_call | solution.py:715
  526.1 1.0 collective-permute-start.6
  530.0 11.5 %collective-permute-done.refs_2_ = bf16[3,128,768]{2,1,0:T(8,128)(2,1)S(1)} collective-permute-done((bf16[3,128,768]{2,1,0:T(8,128)(2,1)}, bf16[3,128,768]{2,1,0:T(8,128)(2,1)S(1)}, u32[]{:S(2)}, u32[]{:S(2)}) %collective-permute-start) | collective-permute-done | bytes 589856 | tf_op jit(solution)/shard_map/ppermute | solution.py:916
  541.5 1.0 collective-permute-start.10
  542.5 11.7 %collective-permute-done.6.refs_2_ = bf16[3,128,768]{2,1,0:T(8,128)(2,1)} collective-permute-done((bf16[3,128,768]{2,1,0:T(8,128)(2,1)}, bf16[3,128,768]{2,1,0:T(8,128)(2,1)}, u32[]{:S(2)}, u32[]{:S(2)}) %collective-permute-start.6) | collective-permute-done | bytes 589856 | tf_op jit(solution)/shard_map/ppermute | solution.py:916
  555.1 1.1 collective-permute-start.20
  556.3 1.0 collective-permute-start.22
  557.3 17.9 %collective-permute-done.12.refs_2_ = bf16[5,128,768]{2,1,0:T(8,128)(2,1)S(1)} collective-permute-done((bf16[5,128,768]{2,1,0:T(8,128)(2,1)}, bf16[5,128,768]{2,1,0:T(8,128)(2,1)S(1)}, u32[]{:S(2)}, u32[]{:S(2)}) %collective-permute-start.12) | collective-permute-done | bytes 983072 | tf_op jit(solution)/shard_map/ppermute | solution.py:916
  575.2 1.0 collective-permute-start.16
  576.2 2.8 collective-permute-done.14.refs_6_
  579.1 25.0 %collective-permute-done.18.refs_2_ = bf16[7,128,768]{2,1,0:T(8,128)(2,1)S(1)} collective-permute-done((bf16[7,128,768]{2,1,0:T(8,128)(2,1)}, bf16[7,128,768]{2,1,0:T(8,128)(2,1)S(1)}, u32[]{:S(2)}, u32[]{:S(2)}) %collective-permute-start.18) | collective-permute-done | bytes 1376288 | tf_op jit(solution)/shard_map/ppermute | solution.py:916
  604.1 1.1 copy-done
  605.2 2.8 collective-permute-done.16.refs_10_
  609.0 1.5 collective-permute-done.15.refs_7_
  613.0 1.1 copy-done.1
  614.1 19.8 %shard_map.110 = (f32[2,6144,1536]{2,1,0:T(8,128)}, f32[2,1536]{1,0:T(2,128)}, f32[2,6144]{1,0:T(2,128)}, f32[2,1536]{1,0:T(2,128)}) custom-call(bf16[14,2,3,256,768]{4,3,2,1,0:T(8,128)(2,1)} %get-tuple-element.49.refs_0_, f32[2,9216]{1,0:T(2,128)} %get-tuple-element.50.refs_1_), custom_call_target="tpu_custom_call" | custom-call | flops 4718592000 | bytes 56623104 | tf_op jit(solution)/shard_map/pallas_call | solution.py:880
  634.0 13.6 %shard_map.111.refs_12_ = f32[2,1536,6144]{2,1,0:T(8,128)} custom-call(bf16[14,2,3,256,768]{4,3,2,1,0:T(8,128)(2,1)} %get-tuple-element.49.refs_0_), custom_call_target="tpu_custom_call" | custom-call | flops 3538944000 | bytes 42467328 | tf_op jit(solution)/shard_map/pallas_call | solution.py:880
  648.2 5.2 shard_map.112.refs_12_
  653.4 5.2 shard_map.113.refs_12_
  659.7 11.4 %shard_map.116.refs_12_ = f32[2,6144,1536]{2,1,0:T(8,128)} custom-call(bf16[7,128,768]{2,1,0:T(8,128)(2,1)} %get-tuple-element.70.refs_0_, bf16[7,128,768]{2,1,0:T(8,128)(2,1)} %get-tuple-element.71.refs_1_, bf16[7,128,768]{2,1,0:T(8,128)(2,1)} %copy-done, bf16[7,128,768]{2,1,0:T(8,128)(2,1)} %copy-done.1, ...), custom_call_target="tpu_custom_call", output_to_operand_aliasing={{}: (12, {})} | custom-call | flops 2949120000 | bytes 35389440 | tf_op jit(solution)/shard_map/pallas_call | solution.py:903
  671.1 6.9 shard_map.117
  678.0 6.9 shard_map.114.refs_12_
  684.9 6.9 shard_map.115
  (56 shorter events, 9.9 us)
Async XLA Ops:
  525.0 16.4 %collective-permute-start = (bf16[3,128,768]{2,1,0:T(8,128)(2,1)}, bf16[3,128,768]{2,1,0:T(8,128)(2,1)S(1)}, u32[]{:S(2)}, u32[]{:S(2)}) collective-permute-start(bf16[3,128,768]{2,1,0:T(8,128)(2,1)} %get-tuple-element.52.refs_0_), channel_id=1, source_target_pairs={{0,2},{1,3},{2,0},{3,1},{4,6},{5,7},{6,4},{7,5},{8,10},{9,11},{10,... | collective-permute-start | bytes 1769480 | tf_op jit(solution)/shard_map/ppermute | solution.py:916
  526.1 28.2 %collective-permute-start.6 = (bf16[3,128,768]{2,1,0:T(8,128)(2,1)}, bf16[3,128,768]{2,1,0:T(8,128)(2,1)}, u32[]{:S(2)}, u32[]{:S(2)}) collective-permute-start(bf16[3,128,768]{2,1,0:T(8,128)(2,1)} %get-tuple-element.58.refs_0_), channel_id=1, source_target_pairs={{0,2},{1,3},{2,0},{3,1},{4,6},{5,7},{6,4},{7,5},{8,10},{9,11},{10,... | collective-permute-start | bytes 1769480 | tf_op jit(solution)/shard_map/ppermute | solution.py:916
  527.1 48.1 %collective-permute-start.12 = (bf16[5,128,768]{2,1,0:T(8,128)(2,1)}, bf16[5,128,768]{2,1,0:T(8,128)(2,1)S(1)}, u32[]{:S(2)}, u32[]{:S(2)}) collective-permute-start(bf16[5,128,768]{2,1,0:T(8,128)(2,1)} %get-tuple-element.64.refs_0_), channel_id=1, source_target_pairs={{0,2},{1,3},{2,0},{3,1},{4,6},{5,7},{6,4},{7,5},{8,10},{9,11},{10,... | collective-permute-start | bytes 2949128 | tf_op jit(solution)/shard_map/ppermute | solution.py:916
  528.1 27.0 %collective-permute-start.8 = (bf16[3,128,768]{2,1,0:T(8,128)(2,1)}, bf16[3,128,768]{2,1,0:T(8,128)(2,1)S(1)}, u32[]{:S(2)}, u32[]{:S(2)}) collective-permute-start(bf16[3,128,768]{2,1,0:T(8,128)(2,1)} %get-tuple-element.60.refs_4_), channel_id=1, source_target_pairs={{0,4},{1,5},{2,6},{3,7},{4,0},{5,1},{6,2},{7,3},{8,12},{9,13},{10,... | collective-permute-start | bytes 1769480 | tf_op jit(solution)/shard_map/ppermute | solution.py:916
  529.0 75.1 %collective-permute-start.18 = (bf16[7,128,768]{2,1,0:T(8,128)(2,1)}, bf16[7,128,768]{2,1,0:T(8,128)(2,1)S(1)}, u32[]{:S(2)}, u32[]{:S(2)}) collective-permute-start(bf16[7,128,768]{2,1,0:T(8,128)(2,1)} %get-tuple-element.70.refs_0_), channel_id=1, source_target_pairs={{0,2},{1,3},{2,0},{3,1},{4,6},{5,7},{6,4},{7,5},{8,10},{9,11},{10,... | collective-permute-start | bytes 4128776 | tf_op jit(solution)/shard_map/ppermute | solution.py:916
  541.5 14.8 %collective-permute-start.10 = (bf16[3,128,768]{2,1,0:T(8,128)(2,1)}, bf16[3,128,768]{2,1,0:T(8,128)(2,1)S(1)}, u32[]{:S(2)}, u32[]{:S(2)}) collective-permute-start(bf16[3,128,768]{2,1,0:T(8,128)(2,1)} %get-tuple-element.62.refs_8_), channel_id=1, source_target_pairs={{0,8},{1,9},{2,10},{3,11},{4,12},{5,13},{6,14},{7,15},{8,0},{9,1},... | collective-permute-start | bytes 1769480 | tf_op jit(solution)/shard_map/ppermute | solution.py:916
  554.2 24.8 %collective-permute-start.14 = (bf16[5,128,768]{2,1,0:T(8,128)(2,1)}, bf16[5,128,768]{2,1,0:T(8,128)(2,1)S(1)}, u32[]{:S(2)}, u32[]{:S(2)}) collective-permute-start(bf16[5,128,768]{2,1,0:T(8,128)(2,1)} %get-tuple-element.66.refs_4_), channel_id=1, source_target_pairs={{0,4},{1,5},{2,6},{3,7},{4,0},{5,1},{6,2},{7,3},{8,12},{9,13},{10,... | collective-permute-start | bytes 2949128 | tf_op jit(solution)/shard_map/ppermute | solution.py:916
  555.1 52.9 %collective-permute-start.20 = (bf16[7,128,768]{2,1,0:T(8,128)(2,1)}, bf16[7,128,768]{2,1,0:T(8,128)(2,1)}, u32[]{:S(2)}, u32[]{:S(2)}) collective-permute-start(bf16[7,128,768]{2,1,0:T(8,128)(2,1)} %get-tuple-element.72.refs_4_), channel_id=1, source_target_pairs={{0,4},{1,5},{2,6},{3,7},{4,0},{5,1},{6,2},{7,3},{8,12},{9,13},{10,... | collective-permute-start | bytes 4128776 | tf_op jit(solution)/shard_map/ppermute | solution.py:916
  556.3 52.2 %collective-permute-start.22 = (bf16[7,128,768]{2,1,0:T(8,128)(2,1)}, bf16[7,128,768]{2,1,0:T(8,128)(2,1)}, u32[]{:S(2)}, u32[]{:S(2)}) collective-permute-start(bf16[7,128,768]{2,1,0:T(8,128)(2,1)} %get-tuple-element.74.refs_8_), channel_id=1, source_target_pairs={{0,8},{1,9},{2,10},{3,11},{4,12},{5,13},{6,14},{7,15},{8,0},{9,1},... | collective-permute-start | bytes 4128776 | tf_op jit(solution)/shard_map/ppermute | solution.py:916
  575.2 32.8 %collective-permute-start.16 = (bf16[5,128,768]{2,1,0:T(8,128)(2,1)}, bf16[5,128,768]{2,1,0:T(8,128)(2,1)S(1)}, u32[]{:S(2)}, u32[]{:S(2)}) collective-permute-start(bf16[5,128,768]{2,1,0:T(8,128)(2,1)} %get-tuple-element.68.refs_8_), channel_id=1, source_target_pairs={{0,8},{1,9},{2,10},{3,11},{4,12},{5,13},{6,14},{7,15},{8,0},{9,1},... | collective-permute-start | bytes 2949128 | tf_op jit(solution)/shard_map/ppermute | solution.py:916
  579.1 29.5 %collective-permute-start.13 = (bf16[5,128,768]{2,1,0:T(8,128)(2,1)S(1)}, bf16[5,128,768]{2,1,0:T(8,128)(2,1)S(1)}, u32[]{:S(2)}, u32[]{:S(2)}) collective-permute-start(bf16[5,128,768]{2,1,0:T(8,128)(2,1)S(1)} %collective-permute-done.12.refs_2_), channel_id=1, source_target_pairs={{0,1},{1,0},{2,3},{3,2},{4,5},{5,4},{6,7},{7,6},{8,9},{9,8},{10,11... | collective-permute-start | bytes 2949128 | tf_op jit(solution)/shard_map/ppermute | solution.py:916
  605.2 7.8 %collective-permute-start.19 = (bf16[7,128,768]{2,1,0:T(8,128)(2,1)S(1)}, bf16[7,128,768]{2,1,0:T(8,128)(2,1)S(1)}, u32[]{:S(2)}, u32[]{:S(2)}) collective-permute-start(bf16[7,128,768]{2,1,0:T(8,128)(2,1)S(1)} %collective-permute-done.18.refs_2_), channel_id=1, source_target_pairs={{0,1},{1,0},{2,3},{3,2},{4,5},{5,4},{6,7},{7,6},{8,9},{9,8},{10,11... | collective-permute-start | bytes 4128776 | tf_op jit(solution)/shard_map/ppermute | solution.py:916
  608.0 2.6 collective-permute-start.15
  608.0 4.0 collective-permute-start.17
  608.5 39.1 %collective-permute-start.21 = (bf16[7,128,768]{2,1,0:T(8,128)(2,1)}, bf16[7,128,768]{2,1,0:T(8,128)(2,1)}, u32[]{:S(2)}, u32[]{:S(2)}) collective-permute-start(bf16[7,128,768]{2,1,0:T(8,128)(2,1)} %collective-permute-done.20.refs_6_), channel_id=1, source_target_pairs={{0,1},{1,0},{2,3},{3,2},{4,5},{5,4},{6,7},{7,6},{8,9},{9,8},{10,11... | collective-permute-start | bytes 4128776 | tf_op jit(solution)/shard_map/ppermute | solution.py:916
  608.6 39.6 %collective-permute-start.23 = (bf16[7,128,768]{2,1,0:T(8,128)(2,1)}, bf16[7,128,768]{2,1,0:T(8,128)(2,1)}, u32[]{:S(2)}, u32[]{:S(2)}) collective-permute-start(bf16[7,128,768]{2,1,0:T(8,128)(2,1)} %collective-permute-done.22.refs_10_), channel_id=1, source_target_pairs={{0,1},{1,0},{2,3},{3,2},{4,5},{5,4},{6,7},{7,6},{8,9},{9,8},{10,11... | collective-permute-start | bytes 4128776 | tf_op jit(solution)/shard_map/ppermute | solution.py:916
  610.6 48.1 %collective-permute-start.2 = (bf16[3,128,768]{2,1,0:T(8,128)(2,1)}, bf16[3,128,768]{2,1,0:T(8,128)(2,1)}, u32[]{:S(2)}, u32[]{:S(2)}) collective-permute-start(bf16[3,128,768]{2,1,0:T(8,128)(2,1)} %get-tuple-element.54.refs_4_), channel_id=1, source_target_pairs={{0,4},{1,5},{2,6},{3,7},{4,0},{5,1},{6,2},{7,3},{8,12},{9,13},{10,... | collective-permute-start | bytes 1769480 | tf_op jit(solution)/shard_map/ppermute | solution.py:916
  612.0 47.2 %collective-permute-start.4 = (bf16[3,128,768]{2,1,0:T(8,128)(2,1)}, bf16[3,128,768]{2,1,0:T(8,128)(2,1)}, u32[]{:S(2)}, u32[]{:S(2)}) collective-permute-start(bf16[3,128,768]{2,1,0:T(8,128)(2,1)} %get-tuple-element.56.refs_8_), channel_id=1, source_target_pairs={{0,8},{1,9},{2,10},{3,11},{4,12},{5,13},{6,14},{7,15},{8,0},{9,1},... | collective-permute-start | bytes 1769480 | tf_op jit(solution)/shard_map/ppermute | solution.py:916
  614.1 45.2 %collective-permute-start.7 = (bf16[3,128,768]{2,1,0:T(8,128)(2,1)}, bf16[3,128,768]{2,1,0:T(8,128)(2,1)}, u32[]{:S(2)}, u32[]{:S(2)}) collective-permute-start(bf16[3,128,768]{2,1,0:T(8,128)(2,1)} %collective-permute-done.6.refs_2_), channel_id=1, source_target_pairs={{0,1},{1,0},{2,3},{3,2},{4,5},{5,4},{6,7},{7,6},{8,9},{9,8},{10,11... | collective-permute-start | bytes 1769480 | tf_op jit(solution)/shard_map/ppermute | solution.py:916
  647.6 30.4 %collective-permute-start.9 = (bf16[3,128,768]{2,1,0:T(8,128)(2,1)}, bf16[3,128,768]{2,1,0:T(8,128)(2,1)}, u32[]{:S(2)}, u32[]{:S(2)}) collective-permute-start(bf16[3,128,768]{2,1,0:T(8,128)(2,1)} %copy-done.9), channel_id=1, source_target_pairs={{0,1},{1,0},{2,3},{3,2},{4,5},{5,4},{6,7},{7,6},{8,9},{9,8},{10,11... | collective-permute-start | bytes 1769480 | tf_op jit(solution)/shard_map/ppermute | solution.py:916
  648.1 29.9 %collective-permute-start.11 = (bf16[3,128,768]{2,1,0:T(8,128)(2,1)}, bf16[3,128,768]{2,1,0:T(8,128)(2,1)}, u32[]{:S(2)}, u32[]{:S(2)}) collective-permute-start(bf16[3,128,768]{2,1,0:T(8,128)(2,1)} %copy-done.10), channel_id=1, source_target_pairs={{0,1},{1,0},{2,3},{3,2},{4,5},{5,4},{6,7},{7,6},{8,9},{9,8},{10,11... | collective-permute-start | bytes 1769480 | tf_op jit(solution)/shard_map/ppermute | solution.py:916
  658.7 26.2 %collective-permute-start.1 = (bf16[3,128,768]{2,1,0:T(8,128)(2,1)}, bf16[3,128,768]{2,1,0:T(8,128)(2,1)}, u32[]{:S(2)}, u32[]{:S(2)}) collective-permute-start(bf16[3,128,768]{2,1,0:T(8,128)(2,1)} %copy-done.8), channel_id=1, source_target_pairs={{0,1},{1,0},{2,3},{3,2},{4,5},{5,4},{6,7},{7,6},{8,9},{9,8},{10,11... | collective-permute-start | bytes 1769480 | tf_op jit(solution)/shard_map/ppermute | solution.py:916
  659.2 25.7 %collective-permute-start.3 = (bf16[3,128,768]{2,1,0:T(8,128)(2,1)}, bf16[3,128,768]{2,1,0:T(8,128)(2,1)}, u32[]{:S(2)}, u32[]{:S(2)}) collective-permute-start(bf16[3,128,768]{2,1,0:T(8,128)(2,1)} %collective-permute-done.2.refs_6_), channel_id=1, source_target_pairs={{0,1},{1,0},{2,3},{3,2},{4,5},{5,4},{6,7},{7,6},{8,9},{9,8},{10,11... | collective-permute-start | bytes 1769480 | tf_op jit(solution)/shard_map/ppermute | solution.py:916
  659.3 25.7 %collective-permute-start.5 = (bf16[3,128,768]{2,1,0:T(8,128)(2,1)}, bf16[3,128,768]{2,1,0:T(8,128)(2,1)}, u32[]{:S(2)}, u32[]{:S(2)}) collective-permute-start(bf16[3,128,768]{2,1,0:T(8,128)(2,1)} %collective-permute-done.4.refs_10_), channel_id=1, source_target_pairs={{0,1},{1,0},{2,3},{3,2},{4,5},{5,4},{6,7},{7,6},{8,9},{9,8},{10,11... | collective-permute-start | bytes 1769480 | tf_op jit(solution)/shard_map/ppermute | solution.py:916
  (11 other events, 173.9 us)

commit v3 on v2

--- a/solution.py
+++ b/solution.py
@@ -43,11 +43,12 @@
     return (0.5 * values) * (1.0 + jnp.tanh(values * (GELU_SCALE + GELU_SCALE * GELU_CUBIC * (values * values))))
 
 
-def forward_kernel(
-    sizes, tokens, upstream, w_up, w_down, gain_in, bias_up_in, bias_down_in, hid_out, normed_out, pre_act_out, act_out,
-    grad_top_out, grad_top_b_out, small_out, hid, normed, branch, up_buf, down_buf, pre_buf, act_buf, up_rows, grad_b_buf,
-    gain, bias_up, bias_down, io_sem, up_sem, down_sem, pre_sem, act_sem,
+def forward_phase(
+    sizes, hbm, branch, grad_b, small_out, before_top, io_sem, up_sem, down_sem, pre_sem, act_sem, up_rows_sem,
+    hid, normed, up_buf, down_buf, pre_buf, act_buf, up_rows, gain, bias_up, bias_down,
 ):
+    (tokens, upstream, w_up, w_down, gain_in, bias_up_in, bias_down_in, hid_out, normed_out, pre_act_out, act_out,
+     grad_top_out, grad_b_out) = hbm
     num_layers, num_tiles, tile_cols = sizes
     num_tokens, row_dim = hid.shape
     steps = num_tiles + 1
@@ -78,7 +79,6 @@
     tokens_load = pltpu.make_async_copy(tokens, hid, io_sem.at[0])
     tokens_load.start()
     up_load(0, 0).start()
-    upstream_load = pltpu.make_async_copy(upstream, up_rows, io_sem.at[3])
     small_out[...] = jnp.zeros_like(small_out)
     branch[...] = jnp.zeros_like(branch)
     pre_buf[0, :, :UP_COLS] = jnp.zeros((num_tokens, UP_COLS), jnp.bfloat16)
@@ -147,7 +147,6 @@
             def _():
                 normed_store(0).start()
                 down_load(0, 0).start()
-                upstream_load.start()
 
             @pl.when(tile > 1)
             def _():
@@ -194,72 +193,38 @@
                 normed_store(layer + 1).start()
 
     hid_store().wait()
-    upstream_load.wait()
+    before_top()
     bias_start = small_out.shape[1] - row_dim
-
-    def grad_stores(rows):
-        return (
-            pltpu.make_async_copy(branch.at[rows, :], grad_top_out.at[rows, :], io_sem.at[0]),
-            pltpu.make_async_copy(grad_b_buf.at[rows, :], grad_top_b_out.at[rows, :], io_sem.at[1]),
-        )
-
-    def top_rows(rows):
+    num_blocks = num_tokens // NORM_ROWS
+
+    def block_rows(block):
+        return pl.ds(pl.multiple_of(block * NORM_ROWS, NORM_ROWS), NORM_ROWS)
+
+    def up_rows_load(block):
+        return pltpu.make_async_copy(upstream.at[block_rows(block), :], up_rows.at[block % 2], up_rows_sem.at[block % 2])
+
+    up_rows_load(0).start()
+
+    @pl.loop(0, num_blocks)
+    def _(block):
+        rows = block_rows(block)
+        up_rows_load(block).wait()
+
+        @pl.when(block + 1 < num_blocks)
+        def _():
+            up_rows_load(block + 1).start()
+
         top_f = next_rows(num_layers - 1, rows)
         top_scale = inverse_rms(top_f)
         top_hat = top_f * top_scale
-        up_f = up_rows[rows, :].astype(jnp.float32)
+        up_f = up_rows[block % 2].astype(jnp.float32)
         grad = top_scale * (up_f - top_hat * jnp.mean(up_f * top_hat, axis=-1, keepdims=True))
         branch[rows, :] = grad
-        grad_b_buf[rows, :] = grad.astype(jnp.bfloat16)
+        grad_b[rows, :] = grad.astype(jnp.bfloat16)
         small_out[num_layers - 1:, bias_start:] += jnp.sum(grad, axis=0, keepdims=True)
-        for copy in grad_stores(rows):
-            copy.start()
-
-    each_block(top_rows)
-    for copy in grad_stores(pl.ds(0, num_tokens)):
-        copy.wait()
-
-
-def forward_pass(tokens, upstream, norm_gain, w_up, bias_up, w_down, bias_down, tile_cols):
-    num_tokens, row_dim = tokens.shape
-    num_layers, _, hidden = w_up.shape
-    bf16, f32 = jnp.bfloat16, jnp.float32
-    dma = pltpu.SemaphoreType.DMA
-    any_spec = pl.BlockSpec(memory_space=pl.ANY)
-    vmem_spec = pl.BlockSpec(memory_space=pltpu.VMEM)
-    rows = (num_tokens, row_dim)
-    wide = (num_layers, num_tokens, hidden)
-    return pl.pallas_call(
-        functools.partial(forward_kernel, (num_layers, hidden // tile_cols, tile_cols)),
-        out_shape=(
-            jax.ShapeDtypeStruct(rows, bf16),
-            jax.ShapeDtypeStruct((num_layers,) + rows, bf16),
-            jax.ShapeDtypeStruct(wide, bf16),
-            jax.ShapeDtypeStruct(wide, bf16),
-            jax.ShapeDtypeStruct(rows, f32),
-            jax.ShapeDtypeStruct(rows, bf16),
-            jax.ShapeDtypeStruct((num_layers, 2 * row_dim + hidden), f32),
-        ),
-        in_specs=[any_spec] * 4 + [vmem_spec] * 3,
-        out_specs=(any_spec,) * 6 + (vmem_spec,),
-        scratch_shapes=[
-            pltpu.VMEM(rows, bf16),
-            pltpu.VMEM(rows, bf16),
-            pltpu.VMEM(rows, f32),
-            pltpu.VMEM((2, row_dim, tile_cols), bf16),
-            pltpu.VMEM((2, tile_cols, row_dim), bf16),
-            pltpu.VMEM((2, num_tokens, tile_cols), bf16),
-            pltpu.VMEM((2, num_tokens, tile_cols), bf16),
-            pltpu.VMEM(rows, bf16),
-            pltpu.VMEM(rows, bf16),
-            pltpu.VMEM((num_layers, row_dim), f32),
-            pltpu.VMEM((num_layers, hidden), f32),
-            pltpu.VMEM((num_layers, row_dim), f32),
-            dma((4,)), dma((2,)), dma((2,)), dma((2,)), dma((2,)),
-        ],
-        compiler_params=pltpu.CompilerParams(vmem_limit_bytes=60 * 2**20),
-        name="forward",
-    )(tokens, upstream, w_up, w_down, norm_gain, bias_up, bias_down)
+
+    pltpu.make_async_copy(branch, grad_top_out, io_sem.at[0]).start()
+    pltpu.make_async_copy(grad_b, grad_b_out, io_sem.at[1]).start()
 
 
 def gelu_slope(values):
@@ -268,25 +233,84 @@
     return 0.5 * (1.0 + bend) + (0.5 * values) * (1.0 - bend * bend) * (GELU_SCALE + 3.0 * GELU_SCALE * GELU_CUBIC * square)
 
 
-def backward_kernel(sizes, *refs):
-    num_layers, chunks_per_mat, row_dim, chunk_cols, region, down_subs, axis = sizes
+def stack_kernel(sizes, *refs):
+    num_layers, chunks_per_mat, row_dim, chunk_cols, region, _, tile_cols, axis = sizes
+    inputs, refs = refs[:7], refs[7:]
+    part_count = 2 * COLORS * len(PART_GROUPS)
+    outputs, part_refs, refs = refs[:9], refs[9:9 + part_count], refs[9 + part_count:]
+    tokens, upstream, w_up, w_down, gain_in, bias_up_in, bias_down_in = inputs
+    gathered, small_out, grad_pre_hbm, grad_b_hbm, hid_out, normed, pre_act, activated, grad_top = outputs
+    rows_buf, grad_b, grad_normed, *shared = refs[:9]
+    io_sem, up_sem, down_sem, pre_sem, act_sem, up_rows_sem, *sems = refs[9:]
+    load_sem = sems[0]
+    num_tokens = grad_b.shape[0]
+    hidden_dim = chunks_per_mat * chunk_cols
+    f32, bf16 = jnp.float32, jnp.bfloat16
+    me = lax.axis_index(axis)
+    barrier = pltpu.get_barrier_semaphore()
+    for dim in range(4):
+        pl.semaphore_signal(barrier, inc=1, device_id=(flip(me, dim),), device_id_type=MESH)
+
+    def first_rows_load():
+        pltpu.make_async_copy(activated.at[num_layers - 1, :, :row_dim], rows_buf, load_sem.at[0, 0]).start()
+
+    hbm = (tokens, upstream, w_up, w_down, gain_in, bias_up_in, bias_down_in, hid_out, normed, pre_act, activated, grad_top, grad_b_hbm)
+    pl.run_scoped(
+        functools.partial(
+            forward_phase, (num_layers, hidden_dim // tile_cols, tile_cols), hbm, grad_normed, grad_b, small_out, first_rows_load,
+            io_sem, up_sem, down_sem, pre_sem, act_sem, up_rows_sem),
+        pltpu.VMEM((num_tokens, row_dim), bf16),
+        pltpu.VMEM((num_tokens, row_dim), bf16),
+        pltpu.VMEM((2, row_dim, tile_cols), bf16),
+        pltpu.VMEM((2, tile_cols, row_dim), bf16),
+        pltpu.VMEM((2, num_tokens, tile_cols), bf16),
+        pltpu.VMEM((2, num_tokens, tile_cols), bf16),
+        pltpu.VMEM((2, NORM_ROWS, row_dim), bf16),
+        pltpu.VMEM((num_layers, row_dim), f32),
+        pltpu.VMEM((num_layers, hidden_dim), f32),
+        pltpu.VMEM((num_layers, row_dim), f32),
+    )
+    hbm = ((tokens, hid_out), normed, pre_act, activated, grad_top, w_up, w_down, gain_in, gathered, grad_pre_hbm, grad_b_hbm, part_refs)
+    pl.run_scoped(
+        functools.partial(
+            backward_phase, sizes, hbm, small_out, rows_buf, grad_b, grad_normed, shared, barrier, io_sem, sems),
+        pltpu.VMEM((row_dim, num_tokens), bf16),
+        pltpu.VMEM((2, num_tokens, chunk_cols), bf16),
+        pltpu.VMEM((COLORS, region, chunk_cols), bf16),
+        pltpu.VMEM((KEPT_SLOTS, COLORS, region, chunk_cols), f32),
+        pltpu.VMEM((COLORS, region // 2, chunk_cols), bf16),
+        pltpu.VMEM((COLORS, region // 4, chunk_cols), bf16),
+        pltpu.VMEM((COLORS, region // 8, chunk_cols), bf16),
+        pltpu.VMEM((2, chunk_cols, row_dim), bf16),
+        pltpu.VMEM((2, num_tokens, chunk_cols), bf16),
+        pltpu.VMEM((num_tokens, chunk_cols), bf16),
+        pltpu.VMEM((2, NORM_ROWS, row_dim), bf16),
+        pltpu.VMEM((2, NORM_ROWS, row_dim), f32),
+    )
+
+
+def flip(device, dim):
+    step = 1 << dim
+    return device + step - 2 * step * ((device // step) % 2)
+
+
+def backward_phase(
+    sizes, hbm, small_out, rows_buf, grad_b, grad_normed, shared, barrier, io_sem, sems, turned, cols_buf, sent_core, kept,
+    sent_1, sent_2, sent_3, weight_buf, pre_buf, grad_pre_buf, hid_buf, grad_buf,
+):
+    num_layers, chunks_per_mat, row_dim, chunk_cols, region, down_subs, _, axis = sizes
     num_mats = 2 * num_layers
     hidden_dim = chunks_per_mat * chunk_cols
-    hid_refs, refs = refs[:num_layers], refs[num_layers:]
-    (normed, pre_act, activated, grad_top, grad_top_b, w_up, w_down, gain_in, small_in,
-     gathered, small_out, grad_pre_hbm, grad_b_hbm) = refs[:13]
-    part_count = 2 * COLORS * len(PART_GROUPS)
-    part_refs, refs = refs[13:13 + part_count], refs[13 + part_count:]
-    (rows_buf, turned, cols_buf, sent_core, kept, recv_core, sent_1, sent_2, sent_3, recv_1, recv_2, recv_3, ring,
-     weight_buf, pre_buf, grad_pre_buf, grad_b, grad_normed, hid_buf, grad_buf,
-     small_recv, load_sem, grad_pre_sem, norm_sem, grad_b_sem, core_send, core_recv, out_send, out_recv, back_send, back_recv,
-     share_send, share_recv, store_sem, small_send_sem, small_recv_sem, part_sem) = refs
+    (hid_refs, normed, pre_act, activated, grad_top, w_up, w_down, gain_in, gathered, grad_pre_hbm, grad_b_hbm, part_refs) = hbm
+    recv_core, recv_1, recv_2, recv_3, ring, small_recv = shared[:6]
+    (load_sem, grad_pre_sem, norm_sem, grad_b_sem, core_send, core_recv, out_send, out_recv, back_send, back_recv,
+     share_send, share_recv, store_sem, small_send_sem, small_recv_sem, part_sem) = sems
     num_chunks = num_mats * chunks_per_mat
     full_chunks = num_chunks - sum(PART_GROUPS)
     half = COLORS * region
     me = lax.axis_index(axis)
     bits = [me % 2, (me // 2) % 2, (me // 4) % 2, me // 8]
-    partners = [me + (1 << d) - 2 * (1 << d) * bits[d] for d in range(4)]
+    partners = [flip(me, dim) for dim in range(4)]
     core = bits[CORE]
     sent_bufs, recv_bufs = (sent_1, sent_2, sent_3), (recv_1, recv_2, recv_3)
     spans = (region // 2, region // 4, region // 8)
@@ -331,8 +355,7 @@
     def cols_load(mat, chunk):
         sub = chunk % chunks_per_mat
         if mat % 2 == 0:
-            source = grad_top_b if mat == 0 else grad_b_hbm
-            source = source.at[:, pl.ds(pl.multiple_of((sub % down_subs) * chunk_cols, 128), chunk_cols)]
+            source = grad_b_hbm.at[:, pl.ds(pl.multiple_of((sub % down_subs) * chunk_cols, 128), chunk_cols)]
         else:
             source = grad_pre_hbm.at[sub]
         return pltpu.make_async_copy(source, cols_buf.at[chunk % 2], load_sem.at[3, chunk % 2])
@@ -430,16 +453,28 @@
                 def _(following=following):
                     for_mat(following, lambda mat: rows_load(mat, following).start())
 
+    grad_top_store = pltpu.make_async_copy(grad_normed, grad_top, io_sem.at[0])
+    grad_b_store = pltpu.make_async_copy(grad_b, grad_b_hbm, io_sem.at[1])
+
     def load(chunk):
         turn_rows(chunk)
-        for_mat(chunk, lambda mat: cols_load(mat, chunk).wait())
-        after = chunk + 1
+
+        @pl.when(chunk > 0)
+        def _():
+            for_mat(chunk, lambda mat: cols_load(mat, chunk).wait())
 
         @pl.when(chunk == 0)
         def _():
-            grad_b_copy.start()
             for copy in weight_loads(0, chunk):
                 copy.start()
+            grad_b_store.wait()
+
+        @pl.when(chunk == 1)
+        def _():
+            grad_top_store.wait()
+            grad_normed[...] = jnp.zeros_like(grad_normed)
+
+        after = chunk + 1
 
         @pl.when((after < num_chunks) & jnp.logical_not(opens_layer(after)))
         def _():
@@ -452,10 +487,6 @@
 
         for_mat(chunk, arrive)
         after, before = chunk + 1, chunk - 1
-
-        @pl.when(chunk == 0)
-        def _():
-            grad_b_copy.wait()
 
         @pl.when(after < num_chunks)
         def _():
@@ -668,15 +699,7 @@
         backward_0=functools.partial(backward, 0), backward_1=functools.partial(backward, 1),
         backward_2=functools.partial(backward, 2), input_grad=input_grad)
 
-    first = jnp.int32(0)
-    rows_load(0, first).start()
-    cols_load(0, first).start()
-    grad_b_copy = pltpu.make_async_copy(grad_top_b, grad_b, grad_b_sem)
-    barrier = pltpu.get_barrier_semaphore()
-    for partner in partners:
-        pl.semaphore_signal(barrier, inc=1, device_id=(partner,), device_id_type=MESH)
-    small_out[...] = small_in[...]
-    grad_normed[...] = jnp.zeros_like(grad_normed)
+    cols_buf[0] = grad_b[:, :chunk_cols]
     pl.semaphore_wait(barrier, 4)
 
     @pl.loop(0, num_chunks + MAX_LAG)
@@ -698,68 +721,57 @@
                 small_out[...] += small_recv[step]
 
 
-def backward_pass(hid_rows, saved, grad_top, grad_top_b, norm_gain, w_up, w_down, small, axis, chunk_cols):
+def run_stack(tokens, upstream, norm_gain, w_up, bias_up, w_down, bias_down, axis, chunk_cols, tile_cols):
     num_layers, row_dim, hidden = w_up.shape
-    tokens = grad_top.shape[0]
+    num_tokens = tokens.shape[0]
     chunks_per_mat = hidden // chunk_cols
     region = row_dim // (2 * COLORS)
     half = (COLORS, region, chunk_cols)
-    sizes = (num_layers, chunks_per_mat, row_dim, chunk_cols, region, row_dim // chunk_cols, axis)
-    num_chunks = 2 * num_layers * chunks_per_mat
+    sizes = (num_layers, chunks_per_mat, row_dim, chunk_cols, region, row_dim // chunk_cols, tile_cols, axis)
+    full_chunks = 2 * num_layers * chunks_per_mat - sum(PART_GROUPS)
     bf16, f32 = jnp.bfloat16, jnp.float32
     dma = pltpu.SemaphoreType.DMA
     any_spec = pl.BlockSpec(memory_space=pl.ANY)
     vmem_spec = pl.BlockSpec(memory_space=pltpu.VMEM)
-    full_chunks = num_chunks - sum(PART_GROUPS)
-    part_shapes = [jax.ShapeDtypeStruct((size, region // 2, chunk_cols), bf16) for size in PART_GROUPS for _ in range(2 * COLORS)]
-    gathered, small_sum, _, _, *parts = pl.pallas_call(
-        functools.partial(backward_kernel, sizes),
+    shape = jax.ShapeDtypeStruct
+    rows, wide, small = (num_tokens, row_dim), (num_layers, num_tokens, hidden), (num_layers, 2 * row_dim + hidden)
+    part_shapes = [shape((size, region // 2, chunk_cols), bf16) for size in PART_GROUPS for _ in range(2 * COLORS)]
+    gathered, small_sum, *rest = pl.pallas_call(
+        functools.partial(stack_kernel, sizes),
         out_shape=[
-            jax.ShapeDtypeStruct((full_chunks, 2) + half, bf16),
-            jax.ShapeDtypeStruct(small.shape, f32),
-            jax.ShapeDtypeStruct((chunks_per_mat, tokens, chunk_cols), bf16),
-            jax.ShapeDtypeStruct((tokens, row_dim), bf16),
+            shape((full_chunks, 2) + half, bf16), shape(small, f32), shape((chunks_per_mat, num_tokens, chunk_cols), bf16),
+            shape(rows, bf16), shape(rows, bf16), shape((num_layers,) + rows, bf16), shape(wide, bf16), shape(wide, bf16),
+            shape(rows, f32),
         ] + part_shapes,
-        in_specs=[any_spec] * (num_layers + 7) + [vmem_spec] * 2,
-        out_specs=[any_spec, vmem_spec, any_spec, any_spec] + [any_spec] * len(part_shapes),
+        in_specs=[any_spec] * 4 + [vmem_spec] * 3,
+        out_specs=[any_spec, vmem_spec] + [any_spec] * (7 + len(part_shapes)),
         scratch_shapes=[
-            pltpu.VMEM((tokens, row_dim), bf16),
-            pltpu.VMEM((row_dim, tokens), bf16),
-            pltpu.VMEM((2, tokens, chunk_cols), bf16),
-            pltpu.VMEM(half, bf16),
-            pltpu.VMEM((KEPT_SLOTS,) + half, f32),
+            pltpu.VMEM(rows, bf16),
+            pltpu.VMEM(rows, bf16),
+            pltpu.VMEM(rows, f32),
             pltpu.VMEM((RECV_SLOTS,) + half, bf16),
-            pltpu.VMEM((COLORS, region // 2, chunk_cols), bf16),
-            pltpu.VMEM((COLORS, region // 4, chunk_cols), bf16),
-            pltpu.VMEM((COLORS, region // 8, chunk_cols), bf16),
             pltpu.VMEM((RECV_SLOTS, COLORS, region // 2, chunk_cols), bf16),
             pltpu.VMEM((RECV_SLOTS, COLORS, region // 4, chunk_cols), bf16),
             pltpu.VMEM((RECV_SLOTS, COLORS, region // 8, chunk_cols), bf16),
             pltpu.VMEM((GATHER_SLOTS, 2) + half, bf16),
-            pltpu.VMEM((2, chunk_cols, row_dim), bf16),
-            pltpu.VMEM((2, tokens, chunk_cols), bf16),
-            pltpu.VMEM((tokens, chunk_cols), bf16),
-            pltpu.VMEM((tokens, row_dim), bf16),
-            pltpu.VMEM((tokens, row_dim), f32),
-            pltpu.VMEM((2, NORM_ROWS, row_dim), bf16),
-            pltpu.VMEM((2, NORM_ROWS, row_dim), f32),
-            pltpu.VMEM((4,) + small.shape, f32),
+            pltpu.VMEM((4,) + small, f32),
+            dma((3,)), dma((2,)), dma((2,)), dma((2,)), dma((2,)), dma((2,)),
             dma((4, 2)), dma, dma((2, 2)), dma,
             dma, dma((RECV_SLOTS,)), dma((3, COLORS)), dma((3, COLORS, RECV_SLOTS)),
             dma((3, COLORS, GATHER_SLOTS)), dma((3, COLORS, GATHER_SLOTS)), dma((GATHER_SLOTS,)), dma((GATHER_SLOTS,)),
             dma((GATHER_SLOTS,)), dma((4,)), dma((4,)), dma((COLORS, 2, GATHER_SLOTS)),
         ],
         compiler_params=pltpu.CompilerParams(collective_id=0, has_side_effects=True, vmem_limit_bytes=67043328),
-        name="backward",
-    )(*hid_rows, *saved, grad_top, grad_top_b, w_up, w_down, norm_gain, small)
-    return gathered, small_sum, parts
+        name="stack",
+    )(tokens, upstream, w_up, w_down, norm_gain, bias_up, bias_down)
+    return gathered, small_sum, rest[7:]
 
 
 def flip_pairs(num_devices, bit):
     return [(dev, dev ^ (1 << bit)) for dev in range(num_devices)]
 
 
-def stream_blocks(num_blocks, start_loads, wait_loads, store_of, in_buf, out_buf):
+def stream_blocks(num_blocks, start_loads, wait_loads, store_of, in_buf, out_buf, after_first=None):
     slots, region = in_buf.shape[0], in_buf.shape[2]
     for block in range(min(slots - 1, num_blocks)):
         start_loads(jnp.int32(block), block)
@@ -781,6 +793,8 @@
         for color in range(COLORS):
             out_buf[slot, color * region:(color + 1) * region, :] = in_buf[slot, color].astype(jnp.float32)
         store_of(block, slot).start()
+        if after_first is not None:
+            pl.when(block == 0)(after_first)
 
     for block in range(max(num_blocks - slots, 0), num_blocks):
         store_of(jnp.int32(block), block % slots).wait()
@@ -799,13 +813,23 @@
     if in_place:
         refs = refs[:1 + bool(small_widths)] + refs[2 + bool(small_widths):]
     if small_widths:
-        gathered, small, out_ref, *small_outs, in_buf, out_buf, in_sem, out_sem = refs
-        start = 0
-        for width, small_out in zip(small_widths, small_outs):
-            small_out[...] = small[:, start:start + width]
-            start += width
+        gathered, small, out_ref, *small_outs, in_buf, out_buf, in_sem, out_sem, small_buf, small_sem = refs
+        small_load = pltpu.make_async_copy(small, small_buf, small_sem.at[0])
+        small_load.start()
+        starts = [sum(small_widths[:n]) for n in range(len(small_widths))]
+        small_stores = [
+            pltpu.make_async_copy(small_buf.at[:, start:start + width], small_out, small_sem.at[1 + n])
+            for n, (start, width, small_out) in enumerate(zip(starts, small_widths, small_outs))]
     else:
         gathered, out_ref, in_buf, out_buf, in_sem, out_sem = refs
+        small_stores = []
+
+    def after_first():
+        if small_stores:
+            small_load.wait()
+        for copy in small_stores:
+            copy.start()
+
     rows, cols = out_buf.shape[1:]
 
     def load(block, slot):
@@ -817,7 +841,9 @@
 
     stream_blocks(
         2 * count, lambda block, slot: load(block, slot).start(), lambda block, slot: load(block, slot).wait(),
-        store, in_buf, out_buf)
+        store, in_buf, out_buf, after_first)
+    for copy in small_stores:
+        copy.wait()
 
 
 def join_kernel(spec, *refs):
@@ -875,15 +901,15 @@
 def widen(gathered, first, count, place, layer, kind, shape, into, down_subs, small, small_widths):
     region, cols = gathered.shape[3:]
     any_spec = pl.BlockSpec(memory_space=pl.ANY)
-    vmem_spec = pl.BlockSpec(memory_space=pltpu.VMEM)
     smalls = [jax.ShapeDtypeStruct((small.shape[0], width), jnp.float32) for width in small_widths]
+    small_scratch = [pltpu.VMEM(small.shape, jnp.float32), pltpu.SemaphoreType.DMA((1 + len(smalls),))] if smalls else []
     return pl.pallas_call(
         functools.partial(widen_kernel, (first, count, place, layer, kind, down_subs, small_widths, into is not None)),
-        in_specs=[any_spec] + [vmem_spec] * bool(smalls) + [any_spec] * (into is not None),
-        out_specs=[any_spec] + [vmem_spec] * len(smalls),
+        in_specs=[any_spec] * (1 + bool(smalls) + (into is not None)),
+        out_specs=[any_spec] * (1 + len(smalls)),
         out_shape=[jax.ShapeDtypeStruct(shape, jnp.float32)] + smalls,
         input_output_aliases={} if into is None else {1 + bool(smalls): 0},
-        scratch_shapes=widen_scratch(region, cols),
+        scratch_shapes=widen_scratch(region, cols) + small_scratch,
         cost_estimate=widen_cost(count, region, cols),
         compiler_params=pltpu.CompilerParams(vmem_limit_bytes=67043328),
     )(gathered, *([small] if smalls else []), *([] if into is None else [into]))
@@ -956,10 +982,8 @@
         num_layers, width = norm_gain.shape
         hidden_width = w_up.shape[2]
         chunk_cols = width // 2
-        hid_1, normed, pre_act, activated, grad_top, grad_top_b, small = forward_pass(
-            tokens, upstream, norm_gain, w_up, bias_up, w_down, bias_down, width)
-        gathered, small, parts = backward_pass(
-            (tokens, hid_1), (normed, pre_act, activated), grad_top, grad_top_b, norm_gain, w_up, w_down, small, axis, chunk_cols)
+        gathered, small, parts = run_stack(
+            tokens, upstream, norm_gain, w_up, bias_up, w_down, bias_down, axis, chunk_cols, 2 * UP_COLS)
         return full_gradients(gathered, parts, small, num_layers, width, hidden_width, chunk_cols, axis, mesh.size)
 
     row_spec = P(axis, None)

time: 693 us -> 698 us (level)
    pallas_call x2 -> x1, Pallas kernels: 524 us -> 531 us  [run_stack(): pl.pallas_call(functools.partial(stack_kernel, sizes), out_shape=[shape((...]
where the time goes in v3:
time: 698 us; the launch traced here: 697 us
  Pallas kernels  605 us (87%)
  waiting for transfers between devices  72 us (10%)
  starting transfers between devices  16.7 us (2%)
    pallas_call x1, Pallas kernels, run_stack(): pl.pallas_call(functools.partial(stack_kernel, sizes), out_shape=[shape((...  531 us
    ppermute x24, waiting for transfers between devices, swap(): return lax.ppermute(array, axis, flip_pairs(num_devices, bit))  72 us
    pallas_call x6, Pallas kernels, join(): pl.pallas_call(functools.partial(join_kernel, (skip, count, place, layer,...  42.5 us
    pallas_call x2, Pallas kernels, widen(): pl.pallas_call(functools.partial(widen_kernel, (first, count, place, laye...  32.2 us
    ppermute x24, starting transfers between devices, swap(): return lax.ppermute(array, axis, flip_pairs(num_devices, bit))  16.7 us
  transfers between devices with their start and end apart: 24, of which 8 were waited for; matrix products, arithmetic and copies ran while one was open for 0% of the time, Pallas kernels for 10%

profile of v3, /device:TPU:0, one launch (start us, length us, event | category | flops | bytes accessed | tf_op | source)
XLA Modules:
  0.0 697.1 jit_solution(251582772832514373)
XLA Ops:
  0.6 530.6 %stack.1 = (bf16[14,2,3,256,768]{4,3,2,1,0:T(8,128)(2,1)}, f32[2,9216]{1,0:T(2,128)}, bf16[8,1024,768]{2,1,0:T(8,128)(2,1)}, bf16[1024,1536]{1,0:T(8,128)(2,1)},...) custom-call(bf16[1024,1536]{1,0:T(8,128)(2,1)} %refs_0_.1, ...), custom_call_target="tpu_custom_call" | custom-call | tf_op jit(solution)/shard_map/stack/pallas_call | solution.py:739
  531.2 1.6 collective-permute-start
  533.3 1.5 collective-permute-start.12
  536.6 11.1 %collective-permute-done.refs_2_ = bf16[3,128,768]{2,1,0:T(8,128)(2,1)S(1)} collective-permute-done((bf16[3,128,768]{2,1,0:T(8,128)(2,1)}, bf16[3,128,768]{2,1,0:T(8,128)(2,1)S(1)}, u32[]{:S(2)}, u32[]{:S(2)}) %collective-permute-start) | collective-permute-done | bytes 589856 | tf_op jit(solution)/shard_map/ppermute | solution.py:942
  547.7 1.3 collective-permute-start.10
  549.0 11.4 %collective-permute-done.6.refs_2_ = bf16[3,128,768]{2,1,0:T(8,128)(2,1)} collective-permute-done((bf16[3,128,768]{2,1,0:T(8,128)(2,1)}, bf16[3,128,768]{2,1,0:T(8,128)(2,1)}, u32[]{:S(2)}, u32[]{:S(2)}) %collective-permute-start.6) | collective-permute-done | bytes 589856 | tf_op jit(solution)/shard_map/ppermute | solution.py:942
  560.4 1.3 collective-permute-start.14
  562.4 1.3 collective-permute-start.22
  563.8 17.6 %collective-permute-done.12.refs_2_ = bf16[5,128,768]{2,1,0:T(8,128)(2,1)S(1)} collective-permute-done((bf16[5,128,768]{2,1,0:T(8,128)(2,1)}, bf16[5,128,768]{2,1,0:T(8,128)(2,1)S(1)}, u32[]{:S(2)}, u32[]{:S(2)}) %collective-permute-start.12) | collective-permute-done | bytes 983072 | tf_op jit(solution)/shard_map/ppermute | solution.py:942
  581.4 1.3 collective-permute-start.16
  582.7 2.5 collective-permute-done.14.refs_6_
  585.3 25.0 %collective-permute-done.18.refs_2_ = bf16[7,128,768]{2,1,0:T(8,128)(2,1)S(1)} collective-permute-done((bf16[7,128,768]{2,1,0:T(8,128)(2,1)}, bf16[7,128,768]{2,1,0:T(8,128)(2,1)S(1)}, u32[]{:S(2)}, u32[]{:S(2)}) %collective-permute-start.18) | collective-permute-done | bytes 1376288 | tf_op jit(solution)/shard_map/ppermute | solution.py:942
  611.4 2.8 collective-permute-done.16.refs_10_
  615.2 1.5 collective-permute-done.15.refs_7_
  616.7 1.3 collective-permute-start.2
  618.1 1.3 collective-permute-start.4
  620.6 18.5 %shard_map.110 = (f32[2,6144,1536]{2,1,0:T(8,128)}, f32[2,1536]{1,0:T(2,128)}, f32[2,6144]{1,0:T(2,128)}, f32[2,1536]{1,0:T(2,128)}) custom-call(bf16[14,2,3,256,768]{4,3,2,1,0:T(8,128)(2,1)} %get-tuple-element.35.refs_0_, f32[2,9216]{1,0:T(2,128)} %get-tuple-element.36.refs_1_), custom_call_target="tpu_custom_call" | custom-call | flops 4718592000 | bytes 56623104 | tf_op jit(solution)/shard_map/pallas_call | solution.py:906
  639.1 13.6 %shard_map.111.refs_12_ = f32[2,1536,6144]{2,1,0:T(8,128)} custom-call(bf16[14,2,3,256,768]{4,3,2,1,0:T(8,128)(2,1)} %get-tuple-element.35.refs_0_), custom_call_target="tpu_custom_call" | custom-call | flops 3538944000 | bytes 42467328 | tf_op jit(solution)/shard_map/pallas_call | solution.py:906
  653.4 5.2 shard_map.112.refs_12_
  658.6 5.2 shard_map.113.refs_12_
  664.9 11.4 %shard_map.116.refs_12_ = f32[2,6144,1536]{2,1,0:T(8,128)} custom-call(bf16[7,128,768]{2,1,0:T(8,128)(2,1)} %get-tuple-element.56.refs_0_, bf16[7,128,768]{2,1,0:T(8,128)(2,1)} %get-tuple-element.57.refs_1_, bf16[7,128,768]{2,1,0:T(8,128)(2,1)} %copy-done, bf16[7,128,768]{2,1,0:T(8,128)(2,1)} %copy-done.1, ...), custom_call_target="tpu_custom_call", output_to_operand_aliasing={{}: (12, {})} | custom-call | flops 2949120000 | bytes 35389440 | tf_op jit(solution)/shard_map/pallas_call | solution.py:929
  676.3 6.9 shard_map.117
  683.2 6.9 shard_map.114.refs_12_
  690.1 6.9 shard_map.115
  (55 shorter events, 8.0 us)
Async XLA Ops:
  531.2 16.4 %collective-permute-start = (bf16[3,128,768]{2,1,0:T(8,128)(2,1)}, bf16[3,128,768]{2,1,0:T(8,128)(2,1)S(1)}, u32[]{:S(2)}, u32[]{:S(2)}) collective-permute-start(bf16[3,128,768]{2,1,0:T(8,128)(2,1)} %get-tuple-element.38.refs_0_), channel_id=1, source_target_pairs={{0,2},{1,3},{2,0},{3,1},{4,6},{5,7},{6,4},{7,5},{8,10},{9,11},{10,... | collective-permute-start | bytes 1769480 | tf_op jit(solution)/shard_map/ppermute | solution.py:942
  532.8 27.6 %collective-permute-start.6 = (bf16[3,128,768]{2,1,0:T(8,128)(2,1)}, bf16[3,128,768]{2,1,0:T(8,128)(2,1)}, u32[]{:S(2)}, u32[]{:S(2)}) collective-permute-start(bf16[3,128,768]{2,1,0:T(8,128)(2,1)} %get-tuple-element.44.refs_0_), channel_id=1, source_target_pairs={{0,2},{1,3},{2,0},{3,1},{4,6},{5,7},{6,4},{7,5},{8,10},{9,11},{10,... | collective-permute-start | bytes 1769480 | tf_op jit(solution)/shard_map/ppermute | solution.py:942
  533.3 48.1 %collective-permute-start.12 = (bf16[5,128,768]{2,1,0:T(8,128)(2,1)}, bf16[5,128,768]{2,1,0:T(8,128)(2,1)S(1)}, u32[]{:S(2)}, u32[]{:S(2)}) collective-permute-start(bf16[5,128,768]{2,1,0:T(8,128)(2,1)} %get-tuple-element.50.refs_0_), channel_id=1, source_target_pairs={{0,2},{1,3},{2,0},{3,1},{4,6},{5,7},{6,4},{7,5},{8,10},{9,11},{10,... | collective-permute-start | bytes 2949128 | tf_op jit(solution)/shard_map/ppermute | solution.py:942
  534.8 26.9 %collective-permute-start.8 = (bf16[3,128,768]{2,1,0:T(8,128)(2,1)}, bf16[3,128,768]{2,1,0:T(8,128)(2,1)S(1)}, u32[]{:S(2)}, u32[]{:S(2)}) collective-permute-start(bf16[3,128,768]{2,1,0:T(8,128)(2,1)} %get-tuple-element.46.refs_4_), channel_id=1, source_target_pairs={{0,4},{1,5},{2,6},{3,7},{4,0},{5,1},{6,2},{7,3},{8,12},{9,13},{10,... | collective-permute-start | bytes 1769480 | tf_op jit(solution)/shard_map/ppermute | solution.py:942
  535.8 74.4 %collective-permute-start.18 = (bf16[7,128,768]{2,1,0:T(8,128)(2,1)}, bf16[7,128,768]{2,1,0:T(8,128)(2,1)S(1)}, u32[]{:S(2)}, u32[]{:S(2)}) collective-permute-start(bf16[7,128,768]{2,1,0:T(8,128)(2,1)} %get-tuple-element.56.refs_0_), channel_id=1, source_target_pairs={{0,2},{1,3},{2,0},{3,1},{4,6},{5,7},{6,4},{7,5},{8,10},{9,11},{10,... | collective-permute-start | bytes 4128776 | tf_op jit(solution)/shard_map/ppermute | solution.py:942
  547.7 14.8 %collective-permute-start.10 = (bf16[3,128,768]{2,1,0:T(8,128)(2,1)}, bf16[3,128,768]{2,1,0:T(8,128)(2,1)S(1)}, u32[]{:S(2)}, u32[]{:S(2)}) collective-permute-start(bf16[3,128,768]{2,1,0:T(8,128)(2,1)} %get-tuple-element.48.refs_8_), channel_id=1, source_target_pairs={{0,8},{1,9},{2,10},{3,11},{4,12},{5,13},{6,14},{7,15},{8,0},{9,1},... | collective-permute-start | bytes 1769480 | tf_op jit(solution)/shard_map/ppermute | solution.py:942
  560.4 24.8 %collective-permute-start.14 = (bf16[5,128,768]{2,1,0:T(8,128)(2,1)}, bf16[5,128,768]{2,1,0:T(8,128)(2,1)S(1)}, u32[]{:S(2)}, u32[]{:S(2)}) collective-permute-start(bf16[5,128,768]{2,1,0:T(8,128)(2,1)} %get-tuple-element.52.refs_4_), channel_id=1, source_target_pairs={{0,4},{1,5},{2,6},{3,7},{4,0},{5,1},{6,2},{7,3},{8,12},{9,13},{10,... | collective-permute-start | bytes 2949128 | tf_op jit(solution)/shard_map/ppermute | solution.py:942
  561.7 52.5 %collective-permute-start.20 = (bf16[7,128,768]{2,1,0:T(8,128)(2,1)}, bf16[7,128,768]{2,1,0:T(8,128)(2,1)}, u32[]{:S(2)}, u32[]{:S(2)}) collective-permute-start(bf16[7,128,768]{2,1,0:T(8,128)(2,1)} %get-tuple-element.58.refs_4_), channel_id=1, source_target_pairs={{0,4},{1,5},{2,6},{3,7},{4,0},{5,1},{6,2},{7,3},{8,12},{9,13},{10,... | collective-permute-start | bytes 4128776 | tf_op jit(solution)/shard_map/ppermute | solution.py:942
  562.4 52.2 %collective-permute-start.22 = (bf16[7,128,768]{2,1,0:T(8,128)(2,1)}, bf16[7,128,768]{2,1,0:T(8,128)(2,1)}, u32[]{:S(2)}, u32[]{:S(2)}) collective-permute-start(bf16[7,128,768]{2,1,0:T(8,128)(2,1)} %get-tuple-element.60.refs_8_), channel_id=1, source_target_pairs={{0,8},{1,9},{2,10},{3,11},{4,12},{5,13},{6,14},{7,15},{8,0},{9,1},... | collective-permute-start | bytes 4128776 | tf_op jit(solution)/shard_map/ppermute | solution.py:942
  581.4 32.8 %collective-permute-start.16 = (bf16[5,128,768]{2,1,0:T(8,128)(2,1)}, bf16[5,128,768]{2,1,0:T(8,128)(2,1)S(1)}, u32[]{:S(2)}, u32[]{:S(2)}) collective-permute-start(bf16[5,128,768]{2,1,0:T(8,128)(2,1)} %get-tuple-element.54.refs_8_), channel_id=1, source_target_pairs={{0,8},{1,9},{2,10},{3,11},{4,12},{5,13},{6,14},{7,15},{8,0},{9,1},... | collective-permute-start | bytes 2949128 | tf_op jit(solution)/shard_map/ppermute | solution.py:942
  585.2 29.5 %collective-permute-start.13 = (bf16[5,128,768]{2,1,0:T(8,128)(2,1)S(1)}, bf16[5,128,768]{2,1,0:T(8,128)(2,1)S(1)}, u32[]{:S(2)}, u32[]{:S(2)}) collective-permute-start(bf16[5,128,768]{2,1,0:T(8,128)(2,1)S(1)} %collective-permute-done.12.refs_2_), channel_id=1, source_target_pairs={{0,1},{1,0},{2,3},{3,2},{4,5},{5,4},{6,7},{7,6},{8,9},{9,8},{10,11... | collective-permute-start | bytes 2949128 | tf_op jit(solution)/shard_map/ppermute | solution.py:942
  611.4 8.1 %collective-permute-start.19 = (bf16[7,128,768]{2,1,0:T(8,128)(2,1)S(1)}, bf16[7,128,768]{2,1,0:T(8,128)(2,1)S(1)}, u32[]{:S(2)}, u32[]{:S(2)}) collective-permute-start(bf16[7,128,768]{2,1,0:T(8,128)(2,1)S(1)} %collective-permute-done.18.refs_2_), channel_id=1, source_target_pairs={{0,1},{1,0},{2,3},{3,2},{4,5},{5,4},{6,7},{7,6},{8,9},{9,8},{10,11... | collective-permute-start | bytes 4128776 | tf_op jit(solution)/shard_map/ppermute | solution.py:942
  614.2 2.6 collective-permute-start.15
  614.2 4.0 collective-permute-start.17
  614.7 38.1 %collective-permute-start.21 = (bf16[7,128,768]{2,1,0:T(8,128)(2,1)}, bf16[7,128,768]{2,1,0:T(8,128)(2,1)}, u32[]{:S(2)}, u32[]{:S(2)}) collective-permute-start(bf16[7,128,768]{2,1,0:T(8,128)(2,1)} %collective-permute-done.20.refs_6_), channel_id=1, source_target_pairs={{0,1},{1,0},{2,3},{3,2},{4,5},{5,4},{6,7},{7,6},{8,9},{9,8},{10,11... | collective-permute-start | bytes 4128776 | tf_op jit(solution)/shard_map/ppermute | solution.py:942
  614.7 38.6 %collective-permute-start.23 = (bf16[7,128,768]{2,1,0:T(8,128)(2,1)}, bf16[7,128,768]{2,1,0:T(8,128)(2,1)}, u32[]{:S(2)}, u32[]{:S(2)}) collective-permute-start(bf16[7,128,768]{2,1,0:T(8,128)(2,1)} %collective-permute-done.22.refs_10_), channel_id=1, source_target_pairs={{0,1},{1,0},{2,3},{3,2},{4,5},{5,4},{6,7},{7,6},{8,9},{9,8},{10,11... | collective-permute-start | bytes 4128776 | tf_op jit(solution)/shard_map/ppermute | solution.py:942
  616.7 47.1 %collective-permute-start.2 = (bf16[3,128,768]{2,1,0:T(8,128)(2,1)}, bf16[3,128,768]{2,1,0:T(8,128)(2,1)}, u32[]{:S(2)}, u32[]{:S(2)}) collective-permute-start(bf16[3,128,768]{2,1,0:T(8,128)(2,1)} %get-tuple-element.40.refs_4_), channel_id=1, source_target_pairs={{0,4},{1,5},{2,6},{3,7},{4,0},{5,1},{6,2},{7,3},{8,12},{9,13},{10,... | collective-permute-start | bytes 1769480 | tf_op jit(solution)/shard_map/ppermute | solution.py:942
  618.1 46.2 %collective-permute-start.4 = (bf16[3,128,768]{2,1,0:T(8,128)(2,1)}, bf16[3,128,768]{2,1,0:T(8,128)(2,1)}, u32[]{:S(2)}, u32[]{:S(2)}) collective-permute-start(bf16[3,128,768]{2,1,0:T(8,128)(2,1)} %get-tuple-element.42.refs_8_), channel_id=1, source_target_pairs={{0,8},{1,9},{2,10},{3,11},{4,12},{5,13},{6,14},{7,15},{8,0},{9,1},... | collective-permute-start | bytes 1769480 | tf_op jit(solution)/shard_map/ppermute | solution.py:942
  620.5 43.9 %collective-permute-start.7 = (bf16[3,128,768]{2,1,0:T(8,128)(2,1)}, bf16[3,128,768]{2,1,0:T(8,128)(2,1)}, u32[]{:S(2)}, u32[]{:S(2)}) collective-permute-start(bf16[3,128,768]{2,1,0:T(8,128)(2,1)} %collective-permute-done.6.refs_2_), channel_id=1, source_target_pairs={{0,1},{1,0},{2,3},{3,2},{4,5},{5,4},{6,7},{7,6},{8,9},{9,8},{10,11... | collective-permute-start | bytes 1769480 | tf_op jit(solution)/shard_map/ppermute | solution.py:942
  652.8 30.4 %collective-permute-start.9 = (bf16[3,128,768]{2,1,0:T(8,128)(2,1)}, bf16[3,128,768]{2,1,0:T(8,128)(2,1)}, u32[]{:S(2)}, u32[]{:S(2)}) collective-permute-start(bf16[3,128,768]{2,1,0:T(8,128)(2,1)} %copy-done.9), channel_id=1, source_target_pairs={{0,1},{1,0},{2,3},{3,2},{4,5},{5,4},{6,7},{7,6},{8,9},{9,8},{10,11... | collective-permute-start | bytes 1769480 | tf_op jit(solution)/shard_map/ppermute | solution.py:942
  653.3 29.9 %collective-permute-start.11 = (bf16[3,128,768]{2,1,0:T(8,128)(2,1)}, bf16[3,128,768]{2,1,0:T(8,128)(2,1)}, u32[]{:S(2)}, u32[]{:S(2)}) collective-permute-start(bf16[3,128,768]{2,1,0:T(8,128)(2,1)} %copy-done.10), channel_id=1, source_target_pairs={{0,1},{1,0},{2,3},{3,2},{4,5},{5,4},{6,7},{7,6},{8,9},{9,8},{10,11... | collective-permute-start | bytes 1769480 | tf_op jit(solution)/shard_map/ppermute | solution.py:942
  663.9 26.2 %collective-permute-start.1 = (bf16[3,128,768]{2,1,0:T(8,128)(2,1)}, bf16[3,128,768]{2,1,0:T(8,128)(2,1)}, u32[]{:S(2)}, u32[]{:S(2)}) collective-permute-start(bf16[3,128,768]{2,1,0:T(8,128)(2,1)} %copy-done.8), channel_id=1, source_target_pairs={{0,1},{1,0},{2,3},{3,2},{4,5},{5,4},{6,7},{7,6},{8,9},{9,8},{10,11... | collective-permute-start | bytes 1769480 | tf_op jit(solution)/shard_map/ppermute | solution.py:942
  664.4 25.7 %collective-permute-start.3 = (bf16[3,128,768]{2,1,0:T(8,128)(2,1)}, bf16[3,128,768]{2,1,0:T(8,128)(2,1)}, u32[]{:S(2)}, u32[]{:S(2)}) collective-permute-start(bf16[3,128,768]{2,1,0:T(8,128)(2,1)} %collective-permute-done.2.refs_6_), channel_id=1, source_target_pairs={{0,1},{1,0},{2,3},{3,2},{4,5},{5,4},{6,7},{7,6},{8,9},{9,8},{10,11... | collective-permute-start | bytes 1769480 | tf_op jit(solution)/shard_map/ppermute | solution.py:942
  664.4 25.7 %collective-permute-start.5 = (bf16[3,128,768]{2,1,0:T(8,128)(2,1)}, bf16[3,128,768]{2,1,0:T(8,128)(2,1)}, u32[]{:S(2)}, u32[]{:S(2)}) collective-permute-start(bf16[3,128,768]{2,1,0:T(8,128)(2,1)} %collective-permute-done.4.refs_10_), channel_id=1, source_target_pairs={{0,1},{1,0},{2,3},{3,2},{4,5},{5,4},{6,7},{7,6},{8,9},{9,8},{10,11... | collective-permute-start | bytes 1769480 | tf_op jit(solution)/shard_map/ppermute | solution.py:942
  (11 other events, 175.3 us)

commit v4 on v3

--- a/solution.py
+++ b/solution.py
@@ -44,8 +44,8 @@
 
 
 def forward_phase(
-    sizes, hbm, branch, grad_b, small_out, before_top, io_sem, up_sem, down_sem, pre_sem, act_sem, up_rows_sem,
-    hid, normed, up_buf, down_buf, pre_buf, act_buf, up_rows, gain, bias_up, bias_down,
+    sizes, hbm, branch, grad_b, small_out, before_top, io_sem, up_sem, down_sem, pre_sem, act_sem,
+    hid, normed, up_buf, down_buf, pre_buf, act_buf, gain, bias_up, bias_down,
 ):
     (tokens, upstream, w_up, w_down, gain_in, bias_up_in, bias_down_in, hid_out, normed_out, pre_act_out, act_out,
      grad_top_out, grad_b_out) = hbm
@@ -56,11 +56,11 @@
 
     def up_load(layer, tile):
         cols = pl.ds(pl.multiple_of(tile * tile_cols, 128), tile_cols)
-        return pltpu.make_async_copy(w_up.at[layer, :, cols], up_buf.at[tile % 2], up_sem.at[tile % 2])
+        return pltpu.make_async_copy(w_up.at[layer, :, cols], up_buf, up_sem)
 
     def down_load(layer, tile):
         rows = pl.ds(pl.multiple_of(tile * tile_cols, 128), tile_cols)
-        return pltpu.make_async_copy(w_down.at[layer, rows, :], down_buf.at[tile % 2], down_sem.at[tile % 2])
+        return pltpu.make_async_copy(w_down.at[layer, rows, :], down_buf, down_sem)
 
     def pre_store(layer, tile):
         cols = pl.ds(pl.multiple_of(tile * tile_cols, 128), tile_cols)
@@ -74,8 +74,9 @@
         return pltpu.make_async_copy(normed, normed_out.at[layer], io_sem.at[1])
 
     def hid_store():
-        return pltpu.make_async_copy(hid, hid_out, io_sem.at[2])
-
+        return pltpu.make_async_copy(hid, hid_out, io_sem.at[3])
+
+    upstream_load = pltpu.make_async_copy(upstream, up_buf.at[:num_tokens, :], io_sem.at[2])
     tokens_load = pltpu.make_async_copy(tokens, hid, io_sem.at[0])
     tokens_load.start()
     up_load(0, 0).start()
@@ -116,14 +117,14 @@
             cols = pl.ds(pl.multiple_of(part * UP_COLS, 128), UP_COLS)
             bias = bias_up[pl.ds(layer, 1), pl.ds(pl.multiple_of(tile * tile_cols + part * UP_COLS, 128), UP_COLS)]
             pre_buf[tile % 2, :, cols] = (
-                jnp.dot(normed[...], up_buf[tile % 2, :, cols], preferred_element_type=jnp.float32) + bias
+                jnp.dot(normed[...], up_buf[:, cols], preferred_element_type=jnp.float32) + bias
             ).astype(jnp.bfloat16)
 
     def down_product(tile):
         slot = tile % 2
         for part in range(row_dim // UP_COLS):
             cols = slice(part * UP_COLS, (part + 1) * UP_COLS)
-            branch[:, cols] += jnp.dot(act_buf[slot], down_buf[slot, :, cols], preferred_element_type=jnp.float32)
+            branch[:, cols] += jnp.dot(act_buf[slot], down_buf[:, cols], preferred_element_type=jnp.float32)
 
     each_block(lambda rows: normalize(0, rows, hid[rows, :].astype(jnp.float32)))
 
@@ -134,14 +135,6 @@
         @pl.when(tile < num_tiles)
         def _():
             up_load(layer, tile).wait()
-
-            @pl.when(tile + 1 < num_tiles)
-            def _():
-                up_load(layer, tile + 1).start()
-
-            @pl.when((tile == num_tiles - 1) & (layer + 1 < num_layers))
-            def _():
-                up_load(layer + 1, 0).start()
 
             @pl.when(step == 0)
             def _():
@@ -156,6 +149,18 @@
             up_product(layer, tile)
             pre_store(layer, tile).start()
 
+            @pl.when(tile + 1 < num_tiles)
+            def _():
+                up_load(layer, tile + 1).start()
+
+            @pl.when((tile + 1 == num_tiles) & (layer + 1 < num_layers))
+            def _():
+                up_load(layer + 1, 0).start()
+
+            @pl.when((tile + 1 == num_tiles) & (layer + 1 == num_layers))
+            def _():
+                upstream_load.start()
+
         @pl.when(tile == num_tiles)
         def _():
             activate((num_tiles - 1) % 2, parts - 1)
@@ -164,6 +169,7 @@
         def _():
             act_store(layer, tile - 1).start()
             down_load(layer, tile - 1).wait()
+            down_product(tile - 1)
 
             @pl.when(tile < num_tiles)
             def _():
@@ -172,8 +178,6 @@
             @pl.when((tile == num_tiles) & (layer + 1 < num_layers))
             def _():
                 down_load(layer + 1, 0).start()
-
-            down_product(tile - 1)
 
         @pl.when(tile == num_tiles)
         def _():
@@ -195,36 +199,31 @@
     hid_store().wait()
     before_top()
     bias_start = small_out.shape[1] - row_dim
-    num_blocks = num_tokens // NORM_ROWS
-
-    def block_rows(block):
-        return pl.ds(pl.multiple_of(block * NORM_ROWS, NORM_ROWS), NORM_ROWS)
-
-    def up_rows_load(block):
-        return pltpu.make_async_copy(upstream.at[block_rows(block), :], up_rows.at[block % 2], up_rows_sem.at[block % 2])
-
-    up_rows_load(0).start()
-
-    @pl.loop(0, num_blocks)
-    def _(block):
-        rows = block_rows(block)
-        up_rows_load(block).wait()
-
-        @pl.when(block + 1 < num_blocks)
-        def _():
-            up_rows_load(block + 1).start()
-
+    upstream_load.wait()
+
+    def top_rows(rows):
         top_f = next_rows(num_layers - 1, rows)
         top_scale = inverse_rms(top_f)
         top_hat = top_f * top_scale
-        up_f = up_rows[block % 2].astype(jnp.float32)
+        up_f = up_buf[rows, :].astype(jnp.float32)
         grad = top_scale * (up_f - top_hat * jnp.mean(up_f * top_hat, axis=-1, keepdims=True))
         branch[rows, :] = grad
         grad_b[rows, :] = grad.astype(jnp.bfloat16)
         small_out[num_layers - 1:, bias_start:] += jnp.sum(grad, axis=0, keepdims=True)
 
-    pltpu.make_async_copy(branch, grad_top_out, io_sem.at[0]).start()
-    pltpu.make_async_copy(grad_b, grad_b_out, io_sem.at[1]).start()
+    def store_rows(block):
+        rows = pl.ds(pl.multiple_of(block * NORM_ROWS, NORM_ROWS), NORM_ROWS)
+        pltpu.make_async_copy(grad_b.at[rows, :], grad_b_out.at[rows, :], io_sem.at[1]).start()
+        pltpu.make_async_copy(branch.at[rows, :], grad_top_out.at[rows, :], io_sem.at[0]).start()
+
+    num_blocks = num_tokens // NORM_ROWS
+
+    @pl.loop(0, num_blocks)
+    def _(block):
+        top_rows(pl.ds(pl.multiple_of(block * NORM_ROWS, NORM_ROWS), NORM_ROWS))
+        pl.when(block > 0)(lambda: store_rows(block - 1))
+
+    store_rows(num_blocks - 1)
 
 
 def gelu_slope(values):
@@ -241,7 +240,7 @@
     tokens, upstream, w_up, w_down, gain_in, bias_up_in, bias_down_in = inputs
     gathered, small_out, grad_pre_hbm, grad_b_hbm, hid_out, normed, pre_act, activated, grad_top = outputs
     rows_buf, grad_b, grad_normed, *shared = refs[:9]
-    io_sem, up_sem, down_sem, pre_sem, act_sem, up_rows_sem, *sems = refs[9:]
+    io_sem, up_sem, down_sem, pre_sem, act_sem, *sems = refs[9:]
     load_sem = sems[0]
     num_tokens = grad_b.shape[0]
     hidden_dim = chunks_per_mat * chunk_cols
@@ -258,14 +257,13 @@
     pl.run_scoped(
         functools.partial(
             forward_phase, (num_layers, hidden_dim // tile_cols, tile_cols), hbm, grad_normed, grad_b, small_out, first_rows_load,
-            io_sem, up_sem, down_sem, pre_sem, act_sem, up_rows_sem),
+            io_sem, up_sem, down_sem, pre_sem, act_sem),
         pltpu.VMEM((num_tokens, row_dim), bf16),
         pltpu.VMEM((num_tokens, row_dim), bf16),
-        pltpu.VMEM((2, row_dim, tile_cols), bf16),
-        pltpu.VMEM((2, tile_cols, row_dim), bf16),
+        pltpu.VMEM((row_dim, tile_cols), bf16),
+        pltpu.VMEM((tile_cols, row_dim), bf16),
         pltpu.VMEM((2, num_tokens, tile_cols), bf16),
         pltpu.VMEM((2, num_tokens, tile_cols), bf16),
-        pltpu.VMEM((2, NORM_ROWS, row_dim), bf16),
         pltpu.VMEM((num_layers, row_dim), f32),
         pltpu.VMEM((num_layers, hidden_dim), f32),
         pltpu.VMEM((num_layers, row_dim), f32),
@@ -467,7 +465,6 @@
         def _():
             for copy in weight_loads(0, chunk):
                 copy.start()
-            grad_b_store.wait()
 
         @pl.when(chunk == 1)
         def _():
@@ -476,11 +473,16 @@
 
         after = chunk + 1
 
-        @pl.when((after < num_chunks) & jnp.logical_not(opens_layer(after)))
+        @pl.when((chunk > 0) & (after < num_chunks) & jnp.logical_not(opens_layer(after)))
         def _():
             for_mat(after, lambda mat: cols_load(mat, after).start())
 
     def load_weights(chunk):
+        @pl.when(chunk == 0)
+        def _():
+            grad_b_store.wait()
+            cols_load(0, chunk + 1).start()
+
         def arrive(mat):
             for copy in weight_loads(mat, chunk):
                 copy.wait()
@@ -755,7 +757,7 @@
             pltpu.VMEM((RECV_SLOTS, COLORS, region // 8, chunk_cols), bf16),
             pltpu.VMEM((GATHER_SLOTS, 2) + half, bf16),
             pltpu.VMEM((4,) + small, f32),
-            dma((3,)), dma((2,)), dma((2,)), dma((2,)), dma((2,)), dma((2,)),
+            dma((4,)), dma, dma, dma((2,)), dma((2,)),
             dma((4, 2)), dma, dma((2, 2)), dma,
             dma, dma((RECV_SLOTS,)), dma((3, COLORS)), dma((3, COLORS, RECV_SLOTS)),
             dma((3, COLORS, GATHER_SLOTS)), dma((3, COLORS, GATHER_SLOTS)), dma((GATHER_SLOTS,)), dma((GATHER_SLOTS,)),
@@ -983,7 +985,7 @@
         hidden_width = w_up.shape[2]
         chunk_cols = width // 2
         gathered, small, parts = run_stack(
-            tokens, upstream, norm_gain, w_up, bias_up, w_down, bias_down, axis, chunk_cols, 2 * UP_COLS)
+            tokens, upstream, norm_gain, w_up, bias_up, w_down, bias_down, axis, chunk_cols, width)
         return full_gradients(gathered, parts, small, num_layers, width, hidden_width, chunk_cols, axis, mesh.size)
 
     row_spec = P(axis, None)

time: 698 us -> 700 us (level)
  no operation moved by 1% of the time
where the time goes in v4:
time: 700 us
  Pallas kernels  608 us (87%)
  waiting for transfers between devices  72.7 us (10%)
  starting transfers between devices  15.9 us (2%)
    pallas_call x1, Pallas kernels, run_stack(): pl.pallas_call(functools.partial(stack_kernel, sizes), out_shape=[shape((...  533 us
    ppermute x24, waiting for transfers between devices, swap(): return lax.ppermute(array, axis, flip_pairs(num_devices, bit))  72.7 us
    pallas_call x6, Pallas kernels, join(): pl.pallas_call(functools.partial(join_kernel, (skip, count, place, layer,...  42.5 us
    pallas_call x2, Pallas kernels, widen(): pl.pallas_call(functools.partial(widen_kernel, (first, count, place, laye...  32.2 us
    ppermute x24, starting transfers between devices, swap(): return lax.ppermute(array, axis, flip_pairs(num_devices, bit))  15.9 us
  transfers between devices with their start and end apart: 24, of which 8 were waited for; matrix products, arithmetic and copies ran while one was open for 0% of the time, Pallas kernels for 10%

profile of v4, /device:TPU:0, one launch (start us, length us, event | category | flops | bytes accessed | tf_op | source)
XLA Modules:
  0.0 699.6 jit_solution(14850770836500041430)
XLA Ops:
  0.6 533.1 %stack.1 = (bf16[14,2,3,256,768]{4,3,2,1,0:T(8,128)(2,1)}, f32[2,9216]{1,0:T(2,128)}, bf16[8,1024,768]{2,1,0:T(8,128)(2,1)}, bf16[1024,1536]{1,0:T(8,128)(2,1)},...) custom-call(bf16[1024,1536]{1,0:T(8,128)(2,1)} %refs_0_.1, ...), custom_call_target="tpu_custom_call" | custom-call | tf_op jit(solution)/shard_map/stack/pallas_call | solution.py:741
  533.8 1.5 collective-permute-start
  535.8 1.4 collective-permute-start.12
  537.2 1.2 collective-permute-start.8
  539.0 11.2 %collective-permute-done.refs_2_ = bf16[3,128,768]{2,1,0:T(8,128)(2,1)S(1)} collective-permute-done((bf16[3,128,768]{2,1,0:T(8,128)(2,1)}, bf16[3,128,768]{2,1,0:T(8,128)(2,1)S(1)}, u32[]{:S(2)}, u32[]{:S(2)}) %collective-permute-start) | collective-permute-done | bytes 589856 | tf_op jit(solution)/shard_map/ppermute | solution.py:944
  550.2 1.2 collective-permute-start.10
  551.4 11.5 %collective-permute-done.6.refs_2_ = bf16[3,128,768]{2,1,0:T(8,128)(2,1)} collective-permute-done((bf16[3,128,768]{2,1,0:T(8,128)(2,1)}, bf16[3,128,768]{2,1,0:T(8,128)(2,1)}, u32[]{:S(2)}, u32[]{:S(2)}) %collective-permute-start.6) | collective-permute-done | bytes 589856 | tf_op jit(solution)/shard_map/ppermute | solution.py:944
  565.0 1.2 collective-permute-start.22
  566.2 17.7 %collective-permute-done.12.refs_2_ = bf16[5,128,768]{2,1,0:T(8,128)(2,1)S(1)} collective-permute-done((bf16[5,128,768]{2,1,0:T(8,128)(2,1)}, bf16[5,128,768]{2,1,0:T(8,128)(2,1)S(1)}, u32[]{:S(2)}, u32[]{:S(2)}) %collective-permute-start.12) | collective-permute-done | bytes 983072 | tf_op jit(solution)/shard_map/ppermute | solution.py:944
  583.9 1.2 collective-permute-start.16
  585.1 2.7 collective-permute-done.14.refs_6_
  587.8 25.0 %collective-permute-done.18.refs_2_ = bf16[7,128,768]{2,1,0:T(8,128)(2,1)S(1)} collective-permute-done((bf16[7,128,768]{2,1,0:T(8,128)(2,1)}, bf16[7,128,768]{2,1,0:T(8,128)(2,1)S(1)}, u32[]{:S(2)}, u32[]{:S(2)}) %collective-permute-start.18) | collective-permute-done | bytes 1376288 | tf_op jit(solution)/shard_map/ppermute | solution.py:944
  613.9 2.8 collective-permute-done.16.refs_10_
  617.7 1.5 collective-permute-done.15.refs_7_
  619.3 1.2 collective-permute-start.2
  620.7 1.2 collective-permute-start.4
  623.0 18.5 %shard_map.110 = (f32[2,6144,1536]{2,1,0:T(8,128)}, f32[2,1536]{1,0:T(2,128)}, f32[2,6144]{1,0:T(2,128)}, f32[2,1536]{1,0:T(2,128)}) custom-call(bf16[14,2,3,256,768]{4,3,2,1,0:T(8,128)(2,1)} %get-tuple-element.35.refs_0_, f32[2,9216]{1,0:T(2,128)} %get-tuple-element.36.refs_1_), custom_call_target="tpu_custom_call" | custom-call | flops 4718592000 | bytes 56623104 | tf_op jit(solution)/shard_map/pallas_call | solution.py:908
  641.6 13.6 %shard_map.111.refs_12_ = f32[2,1536,6144]{2,1,0:T(8,128)} custom-call(bf16[14,2,3,256,768]{4,3,2,1,0:T(8,128)(2,1)} %get-tuple-element.35.refs_0_), custom_call_target="tpu_custom_call" | custom-call | flops 3538944000 | bytes 42467328 | tf_op jit(solution)/shard_map/pallas_call | solution.py:908
  655.8 5.2 shard_map.112.refs_12_
  661.0 5.2 shard_map.113.refs_12_
  667.3 11.4 %shard_map.116.refs_12_ = f32[2,6144,1536]{2,1,0:T(8,128)} custom-call(bf16[7,128,768]{2,1,0:T(8,128)(2,1)} %get-tuple-element.56.refs_0_, bf16[7,128,768]{2,1,0:T(8,128)(2,1)} %get-tuple-element.57.refs_1_, bf16[7,128,768]{2,1,0:T(8,128)(2,1)} %copy-done, bf16[7,128,768]{2,1,0:T(8,128)(2,1)} %copy-done.1, ...), custom_call_target="tpu_custom_call", output_to_operand_aliasing={{}: (12, {})} | custom-call | flops 2949120000 | bytes 35389440 | tf_op jit(solution)/shard_map/pallas_call | solution.py:931
  678.7 6.9 shard_map.117
  685.6 6.9 shard_map.114.refs_12_
  692.5 6.9 shard_map.115
  (55 shorter events, 8.3 us)
Async XLA Ops:
  533.8 16.4 %collective-permute-start = (bf16[3,128,768]{2,1,0:T(8,128)(2,1)}, bf16[3,128,768]{2,1,0:T(8,128)(2,1)S(1)}, u32[]{:S(2)}, u32[]{:S(2)}) collective-permute-start(bf16[3,128,768]{2,1,0:T(8,128)(2,1)} %get-tuple-element.38.refs_0_), channel_id=1, source_target_pairs={{0,2},{1,3},{2,0},{3,1},{4,6},{5,7},{6,4},{7,5},{8,10},{9,11},{10,... | collective-permute-start | bytes 1769480 | tf_op jit(solution)/shard_map/ppermute | solution.py:944
  535.2 27.7 %collective-permute-start.6 = (bf16[3,128,768]{2,1,0:T(8,128)(2,1)}, bf16[3,128,768]{2,1,0:T(8,128)(2,1)}, u32[]{:S(2)}, u32[]{:S(2)}) collective-permute-start(bf16[3,128,768]{2,1,0:T(8,128)(2,1)} %get-tuple-element.44.refs_0_), channel_id=1, source_target_pairs={{0,2},{1,3},{2,0},{3,1},{4,6},{5,7},{6,4},{7,5},{8,10},{9,11},{10,... | collective-permute-start | bytes 1769480 | tf_op jit(solution)/shard_map/ppermute | solution.py:944
  535.8 48.1 %collective-permute-start.12 = (bf16[5,128,768]{2,1,0:T(8,128)(2,1)}, bf16[5,128,768]{2,1,0:T(8,128)(2,1)S(1)}, u32[]{:S(2)}, u32[]{:S(2)}) collective-permute-start(bf16[5,128,768]{2,1,0:T(8,128)(2,1)} %get-tuple-element.50.refs_0_), channel_id=1, source_target_pairs={{0,2},{1,3},{2,0},{3,1},{4,6},{5,7},{6,4},{7,5},{8,10},{9,11},{10,... | collective-permute-start | bytes 2949128 | tf_op jit(solution)/shard_map/ppermute | solution.py:944
  537.2 26.9 %collective-permute-start.8 = (bf16[3,128,768]{2,1,0:T(8,128)(2,1)}, bf16[3,128,768]{2,1,0:T(8,128)(2,1)S(1)}, u32[]{:S(2)}, u32[]{:S(2)}) collective-permute-start(bf16[3,128,768]{2,1,0:T(8,128)(2,1)} %get-tuple-element.46.refs_4_), channel_id=1, source_target_pairs={{0,4},{1,5},{2,6},{3,7},{4,0},{5,1},{6,2},{7,3},{8,12},{9,13},{10,... | collective-permute-start | bytes 1769480 | tf_op jit(solution)/shard_map/ppermute | solution.py:944
  538.4 74.4 %collective-permute-start.18 = (bf16[7,128,768]{2,1,0:T(8,128)(2,1)}, bf16[7,128,768]{2,1,0:T(8,128)(2,1)S(1)}, u32[]{:S(2)}, u32[]{:S(2)}) collective-permute-start(bf16[7,128,768]{2,1,0:T(8,128)(2,1)} %get-tuple-element.56.refs_0_), channel_id=1, source_target_pairs={{0,2},{1,3},{2,0},{3,1},{4,6},{5,7},{6,4},{7,5},{8,10},{9,11},{10,... | collective-permute-start | bytes 4128776 | tf_op jit(solution)/shard_map/ppermute | solution.py:944
  550.2 14.8 %collective-permute-start.10 = (bf16[3,128,768]{2,1,0:T(8,128)(2,1)}, bf16[3,128,768]{2,1,0:T(8,128)(2,1)S(1)}, u32[]{:S(2)}, u32[]{:S(2)}) collective-permute-start(bf16[3,128,768]{2,1,0:T(8,128)(2,1)} %get-tuple-element.48.refs_8_), channel_id=1, source_target_pairs={{0,8},{1,9},{2,10},{3,11},{4,12},{5,13},{6,14},{7,15},{8,0},{9,1},... | collective-permute-start | bytes 1769480 | tf_op jit(solution)/shard_map/ppermute | solution.py:944
  563.0 24.8 %collective-permute-start.14 = (bf16[5,128,768]{2,1,0:T(8,128)(2,1)}, bf16[5,128,768]{2,1,0:T(8,128)(2,1)S(1)}, u32[]{:S(2)}, u32[]{:S(2)}) collective-permute-start(bf16[5,128,768]{2,1,0:T(8,128)(2,1)} %get-tuple-element.52.refs_4_), channel_id=1, source_target_pairs={{0,4},{1,5},{2,6},{3,7},{4,0},{5,1},{6,2},{7,3},{8,12},{9,13},{10,... | collective-permute-start | bytes 2949128 | tf_op jit(solution)/shard_map/ppermute | solution.py:944
  564.1 52.6 %collective-permute-start.20 = (bf16[7,128,768]{2,1,0:T(8,128)(2,1)}, bf16[7,128,768]{2,1,0:T(8,128)(2,1)}, u32[]{:S(2)}, u32[]{:S(2)}) collective-permute-start(bf16[7,128,768]{2,1,0:T(8,128)(2,1)} %get-tuple-element.58.refs_4_), channel_id=1, source_target_pairs={{0,4},{1,5},{2,6},{3,7},{4,0},{5,1},{6,2},{7,3},{8,12},{9,13},{10,... | collective-permute-start | bytes 4128776 | tf_op jit(solution)/shard_map/ppermute | solution.py:944
  565.0 52.2 %collective-permute-start.22 = (bf16[7,128,768]{2,1,0:T(8,128)(2,1)}, bf16[7,128,768]{2,1,0:T(8,128)(2,1)}, u32[]{:S(2)}, u32[]{:S(2)}) collective-permute-start(bf16[7,128,768]{2,1,0:T(8,128)(2,1)} %get-tuple-element.60.refs_8_), channel_id=1, source_target_pairs={{0,8},{1,9},{2,10},{3,11},{4,12},{5,13},{6,14},{7,15},{8,0},{9,1},... | collective-permute-start | bytes 4128776 | tf_op jit(solution)/shard_map/ppermute | solution.py:944
  583.9 32.8 %collective-permute-start.16 = (bf16[5,128,768]{2,1,0:T(8,128)(2,1)}, bf16[5,128,768]{2,1,0:T(8,128)(2,1)S(1)}, u32[]{:S(2)}, u32[]{:S(2)}) collective-permute-start(bf16[5,128,768]{2,1,0:T(8,128)(2,1)} %get-tuple-element.54.refs_8_), channel_id=1, source_target_pairs={{0,8},{1,9},{2,10},{3,11},{4,12},{5,13},{6,14},{7,15},{8,0},{9,1},... | collective-permute-start | bytes 2949128 | tf_op jit(solution)/shard_map/ppermute | solution.py:944
  587.8 29.5 %collective-permute-start.13 = (bf16[5,128,768]{2,1,0:T(8,128)(2,1)S(1)}, bf16[5,128,768]{2,1,0:T(8,128)(2,1)S(1)}, u32[]{:S(2)}, u32[]{:S(2)}) collective-permute-start(bf16[5,128,768]{2,1,0:T(8,128)(2,1)S(1)} %collective-permute-done.12.refs_2_), channel_id=1, source_target_pairs={{0,1},{1,0},{2,3},{3,2},{4,5},{5,4},{6,7},{7,6},{8,9},{9,8},{10,11... | collective-permute-start | bytes 2949128 | tf_op jit(solution)/shard_map/ppermute | solution.py:944
  613.9 8.0 %collective-permute-start.19 = (bf16[7,128,768]{2,1,0:T(8,128)(2,1)S(1)}, bf16[7,128,768]{2,1,0:T(8,128)(2,1)S(1)}, u32[]{:S(2)}, u32[]{:S(2)}) collective-permute-start(bf16[7,128,768]{2,1,0:T(8,128)(2,1)S(1)} %collective-permute-done.18.refs_2_), channel_id=1, source_target_pairs={{0,1},{1,0},{2,3},{3,2},{4,5},{5,4},{6,7},{7,6},{8,9},{9,8},{10,11... | collective-permute-start | bytes 4128776 | tf_op jit(solution)/shard_map/ppermute | solution.py:944
  616.7 2.6 collective-permute-start.15
  616.7 4.0 collective-permute-start.17
  617.2 38.0 %collective-permute-start.21 = (bf16[7,128,768]{2,1,0:T(8,128)(2,1)}, bf16[7,128,768]{2,1,0:T(8,128)(2,1)}, u32[]{:S(2)}, u32[]{:S(2)}) collective-permute-start(bf16[7,128,768]{2,1,0:T(8,128)(2,1)} %collective-permute-done.20.refs_6_), channel_id=1, source_target_pairs={{0,1},{1,0},{2,3},{3,2},{4,5},{5,4},{6,7},{7,6},{8,9},{9,8},{10,11... | collective-permute-start | bytes 4128776 | tf_op jit(solution)/shard_map/ppermute | solution.py:944
  617.3 38.5 %collective-permute-start.23 = (bf16[7,128,768]{2,1,0:T(8,128)(2,1)}, bf16[7,128,768]{2,1,0:T(8,128)(2,1)}, u32[]{:S(2)}, u32[]{:S(2)}) collective-permute-start(bf16[7,128,768]{2,1,0:T(8,128)(2,1)} %collective-permute-done.22.refs_10_), channel_id=1, source_target_pairs={{0,1},{1,0},{2,3},{3,2},{4,5},{5,4},{6,7},{7,6},{8,9},{9,8},{10,11... | collective-permute-start | bytes 4128776 | tf_op jit(solution)/shard_map/ppermute | solution.py:944
  619.3 47.0 %collective-permute-start.2 = (bf16[3,128,768]{2,1,0:T(8,128)(2,1)}, bf16[3,128,768]{2,1,0:T(8,128)(2,1)}, u32[]{:S(2)}, u32[]{:S(2)}) collective-permute-start(bf16[3,128,768]{2,1,0:T(8,128)(2,1)} %get-tuple-element.40.refs_4_), channel_id=1, source_target_pairs={{0,4},{1,5},{2,6},{3,7},{4,0},{5,1},{6,2},{7,3},{8,12},{9,13},{10,... | collective-permute-start | bytes 1769480 | tf_op jit(solution)/shard_map/ppermute | solution.py:944
  620.7 46.1 %collective-permute-start.4 = (bf16[3,128,768]{2,1,0:T(8,128)(2,1)}, bf16[3,128,768]{2,1,0:T(8,128)(2,1)}, u32[]{:S(2)}, u32[]{:S(2)}) collective-permute-start(bf16[3,128,768]{2,1,0:T(8,128)(2,1)} %get-tuple-element.42.refs_8_), channel_id=1, source_target_pairs={{0,8},{1,9},{2,10},{3,11},{4,12},{5,13},{6,14},{7,15},{8,0},{9,1},... | collective-permute-start | bytes 1769480 | tf_op jit(solution)/shard_map/ppermute | solution.py:944
  623.0 43.9 %collective-permute-start.7 = (bf16[3,128,768]{2,1,0:T(8,128)(2,1)}, bf16[3,128,768]{2,1,0:T(8,128)(2,1)}, u32[]{:S(2)}, u32[]{:S(2)}) collective-permute-start(bf16[3,128,768]{2,1,0:T(8,128)(2,1)} %collective-permute-done.6.refs_2_), channel_id=1, source_target_pairs={{0,1},{1,0},{2,3},{3,2},{4,5},{5,4},{6,7},{7,6},{8,9},{9,8},{10,11... | collective-permute-start | bytes 1769480 | tf_op jit(solution)/shard_map/ppermute | solution.py:944
  655.2 30.4 %collective-permute-start.9 = (bf16[3,128,768]{2,1,0:T(8,128)(2,1)}, bf16[3,128,768]{2,1,0:T(8,128)(2,1)}, u32[]{:S(2)}, u32[]{:S(2)}) collective-permute-start(bf16[3,128,768]{2,1,0:T(8,128)(2,1)} %copy-done.9), channel_id=1, source_target_pairs={{0,1},{1,0},{2,3},{3,2},{4,5},{5,4},{6,7},{7,6},{8,9},{9,8},{10,11... | collective-permute-start | bytes 1769480 | tf_op jit(solution)/shard_map/ppermute | solution.py:944
  655.7 29.9 %collective-permute-start.11 = (bf16[3,128,768]{2,1,0:T(8,128)(2,1)}, bf16[3,128,768]{2,1,0:T(8,128)(2,1)}, u32[]{:S(2)}, u32[]{:S(2)}) collective-permute-start(bf16[3,128,768]{2,1,0:T(8,128)(2,1)} %copy-done.10), channel_id=1, source_target_pairs={{0,1},{1,0},{2,3},{3,2},{4,5},{5,4},{6,7},{7,6},{8,9},{9,8},{10,11... | collective-permute-start | bytes 1769480 | tf_op jit(solution)/shard_map/ppermute | solution.py:944
  666.3 26.2 %collective-permute-start.1 = (bf16[3,128,768]{2,1,0:T(8,128)(2,1)}, bf16[3,128,768]{2,1,0:T(8,128)(2,1)}, u32[]{:S(2)}, u32[]{:S(2)}) collective-permute-start(bf16[3,128,768]{2,1,0:T(8,128)(2,1)} %copy-done.8), channel_id=1, source_target_pairs={{0,1},{1,0},{2,3},{3,2},{4,5},{5,4},{6,7},{7,6},{8,9},{9,8},{10,11... | collective-permute-start | bytes 1769480 | tf_op jit(solution)/shard_map/ppermute | solution.py:944
  666.8 25.7 %collective-permute-start.3 = (bf16[3,128,768]{2,1,0:T(8,128)(2,1)}, bf16[3,128,768]{2,1,0:T(8,128)(2,1)}, u32[]{:S(2)}, u32[]{:S(2)}) collective-permute-start(bf16[3,128,768]{2,1,0:T(8,128)(2,1)} %collective-permute-done.2.refs_6_), channel_id=1, source_target_pairs={{0,1},{1,0},{2,3},{3,2},{4,5},{5,4},{6,7},{7,6},{8,9},{9,8},{10,11... | collective-permute-start | bytes 1769480 | tf_op jit(solution)/shard_map/ppermute | solution.py:944
  666.8 25.7 %collective-permute-start.5 = (bf16[3,128,768]{2,1,0:T(8,128)(2,1)}, bf16[3,128,768]{2,1,0:T(8,128)(2,1)}, u32[]{:S(2)}, u32[]{:S(2)}) collective-permute-start(bf16[3,128,768]{2,1,0:T(8,128)(2,1)} %collective-permute-done.4.refs_10_), channel_id=1, source_target_pairs={{0,1},{1,0},{2,3},{3,2},{4,5},{5,4},{6,7},{7,6},{8,9},{9,8},{10,11... | collective-permute-start | bytes 1769480 | tf_op jit(solution)/shard_map/ppermute | solution.py:944
  (11 other events, 174.7 us)

commit v5 on v2

--- a/solution.py
+++ b/solution.py
@@ -20,8 +20,8 @@
     ("send_1", 0), ("backward_2", 0), ("send_back_3", 2), ("store", 6), ("input_grad", 0),
 )
 MAX_LAG = 6
-PART_GROUPS = (7, 5, 3, 3)
-WIDEN_CALLS = (8, 6)
+PART_GROUPS = (7, 5, 2, 3, 3)
+WIDEN_CALLS = (8, 4)
 RECV_SLOTS = 2
 KEPT_SLOTS = 3
 GATHER_SLOTS = 6
@@ -212,10 +212,19 @@
         branch[rows, :] = grad
         grad_b_buf[rows, :] = grad.astype(jnp.bfloat16)
         small_out[num_layers - 1:, bias_start:] += jnp.sum(grad, axis=0, keepdims=True)
-        for copy in grad_stores(rows):
+
+    num_blocks = num_tokens // NORM_ROWS
+
+    def store_block(block):
+        for copy in grad_stores(pl.ds(pl.multiple_of(block * NORM_ROWS, NORM_ROWS), NORM_ROWS)):
             copy.start()
 
-    each_block(top_rows)
+    @pl.loop(0, num_blocks)
+    def _(block):
+        top_rows(pl.ds(pl.multiple_of(block * NORM_ROWS, NORM_ROWS), NORM_ROWS))
+        pl.when(block > 0)(lambda: store_block(block - 1))
+
+    store_block(num_blocks - 1)
     for copy in grad_stores(pl.ds(0, num_tokens)):
         copy.wait()
 
@@ -759,7 +768,7 @@
     return [(dev, dev ^ (1 << bit)) for dev in range(num_devices)]
 
 
-def stream_blocks(num_blocks, start_loads, wait_loads, store_of, in_buf, out_buf):
+def stream_blocks(num_blocks, start_loads, wait_loads, store_of, in_buf, out_buf, after_first=None):
     slots, region = in_buf.shape[0], in_buf.shape[2]
     for block in range(min(slots - 1, num_blocks)):
         start_loads(jnp.int32(block), block)
@@ -781,6 +790,8 @@
         for color in range(COLORS):
             out_buf[slot, color * region:(color + 1) * region, :] = in_buf[slot, color].astype(jnp.float32)
         store_of(block, slot).start()
+        if after_first is not None:
+            pl.when(block == 0)(after_first)
 
     for block in range(max(num_blocks - slots, 0), num_blocks):
         store_of(jnp.int32(block), block % slots).wait()
@@ -799,13 +810,23 @@
     if in_place:
         refs = refs[:1 + bool(small_widths)] + refs[2 + bool(small_widths):]
     if small_widths:
-        gathered, small, out_ref, *small_outs, in_buf, out_buf, in_sem, out_sem = refs
-        start = 0
-        for width, small_out in zip(small_widths, small_outs):
-            small_out[...] = small[:, start:start + width]
-            start += width
+        gathered, small, out_ref, *small_outs, in_buf, out_buf, in_sem, out_sem, small_buf, small_sem = refs
+        small_load = pltpu.make_async_copy(small, small_buf, small_sem.at[0])
+        small_load.start()
+        starts = [sum(small_widths[:n]) for n in range(len(small_widths))]
+        small_stores = [
+            pltpu.make_async_copy(small_buf.at[:, start:start + width], small_out, small_sem.at[1 + n])
+            for n, (start, width, small_out) in enumerate(zip(starts, small_widths, small_outs))]
     else:
         gathered, out_ref, in_buf, out_buf, in_sem, out_sem = refs
+        small_stores = []
+
+    def after_first():
+        if small_stores:
+            small_load.wait()
+        for copy in small_stores:
+            copy.start()
+
     rows, cols = out_buf.shape[1:]
 
     def load(block, slot):
@@ -817,7 +838,9 @@
 
     stream_blocks(
         2 * count, lambda block, slot: load(block, slot).start(), lambda block, slot: load(block, slot).wait(),
-        store, in_buf, out_buf)
+        store, in_buf, out_buf, after_first)
+    for copy in small_stores:
+        copy.wait()
 
 
 def join_kernel(spec, *refs):
@@ -875,15 +898,15 @@
 def widen(gathered, first, count, place, layer, kind, shape, into, down_subs, small, small_widths):
     region, cols = gathered.shape[3:]
     any_spec = pl.BlockSpec(memory_space=pl.ANY)
-    vmem_spec = pl.BlockSpec(memory_space=pltpu.VMEM)
     smalls = [jax.ShapeDtypeStruct((small.shape[0], width), jnp.float32) for width in small_widths]
+    small_scratch = [pltpu.VMEM(small.shape, jnp.float32), pltpu.SemaphoreType.DMA((1 + len(smalls),))] if smalls else []
     return pl.pallas_call(
         functools.partial(widen_kernel, (first, count, place, layer, kind, down_subs, small_widths, into is not None)),
-        in_specs=[any_spec] + [vmem_spec] * bool(smalls) + [any_spec] * (into is not None),
-        out_specs=[any_spec] + [vmem_spec] * len(smalls),
+        in_specs=[any_spec] * (1 + bool(smalls) + (into is not None)),
+        out_specs=[any_spec] * (1 + len(smalls)),
         out_shape=[jax.ShapeDtypeStruct(shape, jnp.float32)] + smalls,
         input_output_aliases={} if into is None else {1 + bool(smalls): 0},
-        scratch_shapes=widen_scratch(region, cols),
+        scratch_shapes=widen_scratch(region, cols) + small_scratch,
         cost_estimate=widen_cost(count, region, cols),
         compiler_params=pltpu.CompilerParams(vmem_limit_bytes=67043328),
     )(gathered, *([small] if smalls else []), *([] if into is None else [into]))

time: 693 us -> 706 us (1.019)
  waiting for transfers between devices: 73.8 us -> 92.8 us
  Pallas kernels: 600 us -> 590 us
    ppermute x24 -> x30, waiting for transfers between devices: 73.8 us -> 92.8 us  [swap(): return lax.ppermute(array, axis, flip_pairs(num_devices, bit))]
    pallas_call x1, Pallas kernels: 427 us -> 418 us  [backward_pass(): pl.pallas_call(functools.partial(backward_kernel, sizes), out_shape=[jax....]
    ppermute x24 -> x30, starting transfers between devices: 14.6 us -> 18 us  [swap(): return lax.ppermute(array, axis, flip_pairs(num_devices, bit))]
  transfers between devices with their start and end apart: 24 -> 30, of which waited for: 8 -> 11; matrix products, arithmetic and copies ran while one was open for 0% -> 0% of each run, Pallas kernels for 10% -> 10%
where the time goes in v5:
time: 706 us
  Pallas kernels  590 us (84%)
  waiting for transfers between devices  92.8 us (13%)
  starting transfers between devices  18 us (3%)
    pallas_call x1, Pallas kernels, backward_pass(): pl.pallas_call(functools.partial(backward_kernel, sizes), out_shape=[jax....  418 us
    pallas_call x1, Pallas kernels, forward_pass(): pl.pallas_call(functools.partial(forward_kernel, (num_layers, hidden // t...  98.1 us
    ppermute x30, waiting for transfers between devices, swap(): return lax.ppermute(array, axis, flip_pairs(num_devices, bit))  92.8 us
    pallas_call x6, Pallas kernels, join(): pl.pallas_call(functools.partial(join_kernel, (skip, count, place, layer,...  46.4 us
    pallas_call x2, Pallas kernels, widen(): pl.pallas_call(functools.partial(widen_kernel, (first, count, place, laye...  27.6 us
    ppermute x30, starting transfers between devices, swap(): return lax.ppermute(array, axis, flip_pairs(num_devices, bit))  18 us
  transfers between devices with their start and end apart: 30, of which 11 were waited for; matrix products, arithmetic and copies ran while one was open for 0% of the time, Pallas kernels for 10%

profile of v5, /device:TPU:0, one launch (start us, length us, event | category | flops | bytes accessed | tf_op | source)
XLA Modules:
  0.0 705.6 jit_solution(1518697812717343076)
XLA Ops:
  0.6 98.1 %forward.1 = (bf16[1024,1536]{1,0:T(8,128)(2,1)}, bf16[2,1024,1536]{2,1,0:T(8,128)(2,1)}, bf16[2,1024,6144]{2,1,0:T(8,128)(2,1)}, bf16[2,1024,6144]{2,1,0:T(8,12...) custom-call(bf16[1024,1536]{1,0:T(8,128)(2,1)} %refs_0_.1, ...), custom_call_target="tpu_custom_call" | custom-call | tf_op jit(solution)/shard_map/forward/pallas_call | solution.py:241
  98.7 418.1 %backward.1 = (bf16[12,2,3,256,768]{4,3,2,1,0:T(8,128)(2,1)}, f32[2,9216]{1,0:T(2,128)}, bf16[8,1024,768]{2,1,0:T(8,128)(2,1)}, bf16[1024,1536]{1,0:T(8,128)(2,1...) custom-call(bf16[1024,1536]{1,0:T(8,128)(2,1)} %refs_0_.1, ...), custom_call_target="tpu_custom_call" | custom-call | tf_op jit(solution)/shard_map/backward/pallas_call | solution.py:724
  519.8 1.1 collective-permute-start.16
  521.9 7.2 %collective-permute-done.12.refs_2_ = bf16[2,128,768]{2,1,0:T(8,128)(2,1)S(1)} collective-permute-done((bf16[2,128,768]{2,1,0:T(8,128)(2,1)}, bf16[2,128,768]{2,1,0:T(8,128)(2,1)S(1)}, u32[]{:S(2)}, u32[]{:S(2)}) %collective-permute-start.12) | collective-permute-done | bytes 393248 | tf_op jit(solution)/shard_map/ppermute | solution.py:939
  531.1 11.5 %collective-permute-done.16.refs_10_ = bf16[2,128,768]{2,1,0:T(8,128)(2,1)S(1)} collective-permute-done((bf16[2,128,768]{2,1,0:T(8,128)(2,1)}, bf16[2,128,768]{2,1,0:T(8,128)(2,1)S(1)}, u32[]{:S(2)}, u32[]{:S(2)}) %collective-permute-start.16) | collective-permute-done | bytes 393248 | tf_op jit(solution)/shard_map/ppermute | solution.py:939
  544.6 1.1 collective-permute-start.18
  546.6 7.8 %collective-permute-done.refs_2_ = bf16[3,128,768]{2,1,0:T(8,128)(2,1)S(1)} collective-permute-done((bf16[3,128,768]{2,1,0:T(8,128)(2,1)}, bf16[3,128,768]{2,1,0:T(8,128)(2,1)S(1)}, u32[]{:S(2)}, u32[]{:S(2)}) %collective-permute-start) | collective-permute-done | bytes 589856 | tf_op jit(solution)/shard_map/ppermute | solution.py:939
  556.3 2.8 collective-permute-done.2.refs_6_
  559.5 1.2 collective-permute-done.13.refs_3_
  561.7 1.7 collective-permute-done.17.refs_11_
  564.5 19.4 %collective-permute-done.18.refs_2_ = bf16[7,128,768]{2,1,0:T(8,128)(2,1)S(1)} collective-permute-done((bf16[7,128,768]{2,1,0:T(8,128)(2,1)}, bf16[7,128,768]{2,1,0:T(8,128)(2,1)S(1)}, u32[]{:S(2)}, u32[]{:S(2)}) %collective-permute-start.18) | collective-permute-done | bytes 1376288 | tf_op jit(solution)/shard_map/ppermute | solution.py:939
  583.9 1.1 copy-done
  585.1 3.4 collective-permute-done.20.refs_6_
  589.1 15.4 %collective-permute-done.24.refs_2_ = bf16[5,128,768]{2,1,0:T(8,128)(2,1)} collective-permute-done((bf16[5,128,768]{2,1,0:T(8,128)(2,1)}, bf16[5,128,768]{2,1,0:T(8,128)(2,1)}, u32[]{:S(2)}, u32[]{:S(2)}) %collective-permute-start.24) | collective-permute-done | bytes 983072 | tf_op jit(solution)/shard_map/ppermute | solution.py:939
  605.5 2.3 collective-permute-done.26.refs_6_
  607.8 20.2 %collective-permute-done.28.refs_10_ = bf16[5,128,768]{2,1,0:T(8,128)(2,1)} collective-permute-done((bf16[5,128,768]{2,1,0:T(8,128)(2,1)}, bf16[5,128,768]{2,1,0:T(8,128)(2,1)}, u32[]{:S(2)}, u32[]{:S(2)}) %collective-permute-start.28) | collective-permute-done | bytes 983072 | tf_op jit(solution)/shard_map/ppermute | solution.py:939
  630.7 18.5 %shard_map.110 = (f32[2,6144,1536]{2,1,0:T(8,128)}, f32[2,1536]{1,0:T(2,128)}, f32[2,6144]{1,0:T(2,128)}, f32[2,1536]{1,0:T(2,128)}) custom-call(bf16[12,2,3,256,768]{4,3,2,1,0:T(8,128)(2,1)} %get-tuple-element.55.refs_0_, f32[2,9216]{1,0:T(2,128)} %get-tuple-element.56.refs_1_), custom_call_target="tpu_custom_call" | custom-call | flops 4718592000 | bytes 56623104 | tf_op jit(solution)/shard_map/pallas_call | solution.py:903
  649.2 9.1 %shard_map.111.refs_12_ = f32[2,1536,6144]{2,1,0:T(8,128)} custom-call(bf16[12,2,3,256,768]{4,3,2,1,0:T(8,128)(2,1)} %get-tuple-element.55.refs_0_), custom_call_target="tpu_custom_call" | custom-call | flops 2359296000 | bytes 28311552 | tf_op jit(solution)/shard_map/pallas_call | solution.py:903
  658.3 9.2 %shard_map.112.refs_12_ = f32[2,1536,6144]{2,1,0:T(8,128)} custom-call(bf16[7,128,768]{2,1,0:T(8,128)(2,1)} %get-tuple-element.76.refs_0_, bf16[7,128,768]{2,1,0:T(8,128)(2,1)} %get-tuple-element.77.refs_1_, bf16[7,128,768]{2,1,0:T(8,128)(2,1)} %copy-done, bf16[7,128,768]{2,1,0:T(8,128)(2,1)} %copy-done.3, ...), custom_call_target="tpu_custom_call", output_to_operand_aliasing={{}: (12, {})} | custom-call | flops 2359296000 | bytes 28311552 | tf_op jit(solution)/shard_map/pallas_call | solution.py:926
  667.4 5.2 shard_map.113.refs_12_
  673.3 6.8 shard_map.116.refs_12_
  680.2 6.9 shard_map.114.refs_12_
  687.1 11.4 %shard_map.117 = f32[2,6144,1536]{2,1,0:T(8,128)} custom-call(bf16[5,128,768]{2,1,0:T(8,128)(2,1)} %get-tuple-element.83.refs_0_, bf16[5,128,768]{2,1,0:T(8,128)(2,1)} %get-tuple-element.84.refs_1_, bf16[5,128,768]{2,1,0:T(8,128)(2,1)} %collective-permute-done.24.refs_2_, ...), custom_call_target="tpu_custom_call", output_to_operand_aliasing={{}: (12, {})} | custom-call | flops 2949120000 | bytes 35389440 | tf_op jit(solution)/shard_map/pallas_call | solution.py:926
  698.6 6.9 shard_map.115
  (80 shorter events, 18.2 us)
Async XLA Ops:
  518.9 24.8 %collective-permute-start.10 = (bf16[3,128,768]{2,1,0:T(8,128)(2,1)}, bf16[3,128,768]{2,1,0:T(8,128)(2,1)S(1)}, u32[]{:S(2)}, u32[]{:S(2)}) collective-permute-start(bf16[3,128,768]{2,1,0:T(8,128)(2,1)} %get-tuple-element.68.refs_8_), channel_id=1, source_target_pairs={{0,8},{1,9},{2,10},{3,11},{4,12},{5,13},{6,14},{7,15},{8,0},{9,1},... | collective-permute-start | bytes 1769480 | tf_op jit(solution)/shard_map/ppermute | solution.py:939
  519.8 22.8 %collective-permute-start.16 = (bf16[2,128,768]{2,1,0:T(8,128)(2,1)}, bf16[2,128,768]{2,1,0:T(8,128)(2,1)S(1)}, u32[]{:S(2)}, u32[]{:S(2)}) collective-permute-start(bf16[2,128,768]{2,1,0:T(8,128)(2,1)} %get-tuple-element.74.refs_8_), channel_id=1, source_target_pairs={{0,8},{1,9},{2,10},{3,11},{4,12},{5,13},{6,14},{7,15},{8,0},{9,1},... | collective-permute-start | bytes 1179656 | tf_op jit(solution)/shard_map/ppermute | solution.py:939
  520.9 23.6 %collective-permute-start.6 = (bf16[3,128,768]{2,1,0:T(8,128)(2,1)}, bf16[3,128,768]{2,1,0:T(8,128)(2,1)}, u32[]{:S(2)}, u32[]{:S(2)}) collective-permute-start(bf16[3,128,768]{2,1,0:T(8,128)(2,1)} %get-tuple-element.64.refs_0_), channel_id=1, source_target_pairs={{0,2},{1,3},{2,0},{3,1},{4,6},{5,7},{6,4},{7,5},{8,10},{9,11},{10,... | collective-permute-start | bytes 1769480 | tf_op jit(solution)/shard_map/ppermute | solution.py:939
  529.1 16.6 %collective-permute-start.8 = (bf16[3,128,768]{2,1,0:T(8,128)(2,1)}, bf16[3,128,768]{2,1,0:T(8,128)(2,1)}, u32[]{:S(2)}, u32[]{:S(2)}) collective-permute-start(bf16[3,128,768]{2,1,0:T(8,128)(2,1)} %get-tuple-element.66.refs_4_), channel_id=1, source_target_pairs={{0,4},{1,5},{2,6},{3,7},{4,0},{5,1},{6,2},{7,3},{8,12},{9,13},{10,... | collective-permute-start | bytes 1769480 | tf_op jit(solution)/shard_map/ppermute | solution.py:939
  530.1 24.3 %collective-permute-start = (bf16[3,128,768]{2,1,0:T(8,128)(2,1)}, bf16[3,128,768]{2,1,0:T(8,128)(2,1)S(1)}, u32[]{:S(2)}, u32[]{:S(2)}) collective-permute-start(bf16[3,128,768]{2,1,0:T(8,128)(2,1)} %get-tuple-element.58.refs_0_), channel_id=1, source_target_pairs={{0,2},{1,3},{2,0},{3,1},{4,6},{5,7},{6,4},{7,5},{8,10},{9,11},{10,... | collective-permute-start | bytes 1769480 | tf_op jit(solution)/shard_map/ppermute | solution.py:939
  542.6 16.4 %collective-permute-start.2 = (bf16[3,128,768]{2,1,0:T(8,128)(2,1)}, bf16[3,128,768]{2,1,0:T(8,128)(2,1)S(1)}, u32[]{:S(2)}, u32[]{:S(2)}) collective-permute-start(bf16[3,128,768]{2,1,0:T(8,128)(2,1)} %get-tuple-element.60.refs_4_), channel_id=1, source_target_pairs={{0,4},{1,5},{2,6},{3,7},{4,0},{5,1},{6,2},{7,3},{8,12},{9,13},{10,... | collective-permute-start | bytes 1769480 | tf_op jit(solution)/shard_map/ppermute | solution.py:939
  544.6 39.3 %collective-permute-start.18 = (bf16[7,128,768]{2,1,0:T(8,128)(2,1)}, bf16[7,128,768]{2,1,0:T(8,128)(2,1)S(1)}, u32[]{:S(2)}, u32[]{:S(2)}) collective-permute-start(bf16[7,128,768]{2,1,0:T(8,128)(2,1)} %get-tuple-element.76.refs_0_), channel_id=1, source_target_pairs={{0,2},{1,3},{2,0},{3,1},{4,6},{5,7},{6,4},{7,5},{8,10},{9,11},{10,... | collective-permute-start | bytes 4128776 | tf_op jit(solution)/shard_map/ppermute | solution.py:939
  545.7 42.8 %collective-permute-start.20 = (bf16[7,128,768]{2,1,0:T(8,128)(2,1)}, bf16[7,128,768]{2,1,0:T(8,128)(2,1)S(1)}, u32[]{:S(2)}, u32[]{:S(2)}) collective-permute-start(bf16[7,128,768]{2,1,0:T(8,128)(2,1)} %get-tuple-element.78.refs_4_), channel_id=1, source_target_pairs={{0,4},{1,5},{2,6},{3,7},{4,0},{5,1},{6,2},{7,3},{8,12},{9,13},{10,... | collective-permute-start | bytes 4128776 | tf_op jit(solution)/shard_map/ppermute | solution.py:939
  555.2 33.3 %collective-permute-start.22 = (bf16[7,128,768]{2,1,0:T(8,128)(2,1)}, bf16[7,128,768]{2,1,0:T(8,128)(2,1)S(1)}, u32[]{:S(2)}, u32[]{:S(2)}) collective-permute-start(bf16[7,128,768]{2,1,0:T(8,128)(2,1)} %get-tuple-element.80.refs_8_), channel_id=1, source_target_pairs={{0,8},{1,9},{2,10},{3,11},{4,12},{5,13},{6,14},{7,15},{8,0},{9,1},... | collective-permute-start | bytes 4128776 | tf_op jit(solution)/shard_map/ppermute | solution.py:939
  560.7 43.7 %collective-permute-start.24 = (bf16[5,128,768]{2,1,0:T(8,128)(2,1)}, bf16[5,128,768]{2,1,0:T(8,128)(2,1)}, u32[]{:S(2)}, u32[]{:S(2)}) collective-permute-start(bf16[5,128,768]{2,1,0:T(8,128)(2,1)} %get-tuple-element.83.refs_0_), channel_id=1, source_target_pairs={{0,2},{1,3},{2,0},{3,1},{4,6},{5,7},{6,4},{7,5},{8,10},{9,11},{10,... | collective-permute-start | bytes 2949128 | tf_op jit(solution)/shard_map/ppermute | solution.py:939
  563.5 44.3 %collective-permute-start.26 = (bf16[5,128,768]{2,1,0:T(8,128)(2,1)}, bf16[5,128,768]{2,1,0:T(8,128)(2,1)}, u32[]{:S(2)}, u32[]{:S(2)}) collective-permute-start(bf16[5,128,768]{2,1,0:T(8,128)(2,1)} %get-tuple-element.85.refs_4_), channel_id=1, source_target_pairs={{0,4},{1,5},{2,6},{3,7},{4,0},{5,1},{6,2},{7,3},{8,12},{9,13},{10,... | collective-permute-start | bytes 2949128 | tf_op jit(solution)/shard_map/ppermute | solution.py:939
  585.0 43.4 %collective-permute-start.19 = (bf16[7,128,768]{2,1,0:T(8,128)(2,1)S(1)}, bf16[7,128,768]{2,1,0:T(8,128)(2,1)S(1)}, u32[]{:S(2)}, u32[]{:S(2)}) collective-permute-start(bf16[7,128,768]{2,1,0:T(8,128)(2,1)S(1)} %collective-permute-done.18.refs_2_), channel_id=1, source_target_pairs={{0,1},{1,0},{2,3},{3,2},{4,5},{5,4},{6,7},{7,6},{8,9},{9,8},{10,11... | collective-permute-start | bytes 4128776 | tf_op jit(solution)/shard_map/ppermute | solution.py:939
  588.5 40.1 %collective-permute-start.21 = (bf16[7,128,768]{2,1,0:T(8,128)(2,1)S(1)}, bf16[7,128,768]{2,1,0:T(8,128)(2,1)S(1)}, u32[]{:S(2)}, u32[]{:S(2)}) collective-permute-start(bf16[7,128,768]{2,1,0:T(8,128)(2,1)S(1)} %collective-permute-done.20.refs_6_), channel_id=1, source_target_pairs={{0,1},{1,0},{2,3},{3,2},{4,5},{5,4},{6,7},{7,6},{8,9},{9,8},{10,11... | collective-permute-start | bytes 4128776 | tf_op jit(solution)/shard_map/ppermute | solution.py:939
  588.5 40.5 %collective-permute-start.23 = (bf16[7,128,768]{2,1,0:T(8,128)(2,1)S(1)}, bf16[7,128,768]{2,1,0:T(8,128)(2,1)S(1)}, u32[]{:S(2)}, u32[]{:S(2)}) collective-permute-start(bf16[7,128,768]{2,1,0:T(8,128)(2,1)S(1)} %collective-permute-done.22.refs_10_), channel_id=1, source_target_pairs={{0,1},{1,0},{2,3},{3,2},{4,5},{5,4},{6,7},{7,6},{8,9},{9,8},{10,11... | collective-permute-start | bytes 4128776 | tf_op jit(solution)/shard_map/ppermute | solution.py:939
  604.5 23.5 %collective-permute-start.28 = (bf16[5,128,768]{2,1,0:T(8,128)(2,1)}, bf16[5,128,768]{2,1,0:T(8,128)(2,1)}, u32[]{:S(2)}, u32[]{:S(2)}) collective-permute-start(bf16[5,128,768]{2,1,0:T(8,128)(2,1)} %get-tuple-element.87.refs_8_), channel_id=1, source_target_pairs={{0,8},{1,9},{2,10},{3,11},{4,12},{5,13},{6,14},{7,15},{8,0},{9,1},... | collective-permute-start | bytes 2949128 | tf_op jit(solution)/shard_map/ppermute | solution.py:939
  607.8 20.2 %collective-permute-start.11 = (bf16[3,128,768]{2,1,0:T(8,128)(2,1)S(1)}, bf16[3,128,768]{2,1,0:T(8,128)(2,1)S(1)}, u32[]{:S(2)}, u32[]{:S(2)}) collective-permute-start(bf16[3,128,768]{2,1,0:T(8,128)(2,1)S(1)} %collective-permute-done.10.refs_10_), channel_id=1, source_target_pairs={{0,1},{1,0},{2,3},{3,2},{4,5},{5,4},{6,7},{7,6},{8,9},{9,8},{10,11... | collective-permute-start | bytes 1769480 | tf_op jit(solution)/shard_map/ppermute | solution.py:939
  628.0 44.7 %collective-permute-start.7 = (bf16[3,128,768]{2,1,0:T(8,128)(2,1)}, bf16[3,128,768]{2,1,0:T(8,128)(2,1)}, u32[]{:S(2)}, u32[]{:S(2)}) collective-permute-start(bf16[3,128,768]{2,1,0:T(8,128)(2,1)} %collective-permute-done.6.refs_2_), channel_id=1, source_target_pairs={{0,1},{1,0},{2,3},{3,2},{4,5},{5,4},{6,7},{7,6},{8,9},{9,8},{10,11... | collective-permute-start | bytes 1769480 | tf_op jit(solution)/shard_map/ppermute | solution.py:939
  628.0 44.9 %collective-permute-start.9 = (bf16[3,128,768]{2,1,0:T(8,128)(2,1)}, bf16[3,128,768]{2,1,0:T(8,128)(2,1)}, u32[]{:S(2)}, u32[]{:S(2)}) collective-permute-start(bf16[3,128,768]{2,1,0:T(8,128)(2,1)} %collective-permute-done.8.refs_6_), channel_id=1, source_target_pairs={{0,1},{1,0},{2,3},{3,2},{4,5},{5,4},{6,7},{7,6},{8,9},{9,8},{10,11... | collective-permute-start | bytes 1769480 | tf_op jit(solution)/shard_map/ppermute | solution.py:939
  628.5 44.8 %collective-permute-start.25 = (bf16[5,128,768]{2,1,0:T(8,128)(2,1)}, bf16[5,128,768]{2,1,0:T(8,128)(2,1)}, u32[]{:S(2)}, u32[]{:S(2)}) collective-permute-start(bf16[5,128,768]{2,1,0:T(8,128)(2,1)} %collective-permute-done.24.refs_2_), channel_id=1, source_target_pairs={{0,1},{1,0},{2,3},{3,2},{4,5},{5,4},{6,7},{7,6},{8,9},{9,8},{10,11... | collective-permute-start | bytes 2949128 | tf_op jit(solution)/shard_map/ppermute | solution.py:939
  628.6 58.5 %collective-permute-start.27 = (bf16[5,128,768]{2,1,0:T(8,128)(2,1)}, bf16[5,128,768]{2,1,0:T(8,128)(2,1)}, u32[]{:S(2)}, u32[]{:S(2)}) collective-permute-start(bf16[5,128,768]{2,1,0:T(8,128)(2,1)} %collective-permute-done.26.refs_6_), channel_id=1, source_target_pairs={{0,1},{1,0},{2,3},{3,2},{4,5},{5,4},{6,7},{7,6},{8,9},{9,8},{10,11... | collective-permute-start | bytes 2949128 | tf_op jit(solution)/shard_map/ppermute | solution.py:939
  629.6 57.5 %collective-permute-start.29 = (bf16[5,128,768]{2,1,0:T(8,128)(2,1)}, bf16[5,128,768]{2,1,0:T(8,128)(2,1)}, u32[]{:S(2)}, u32[]{:S(2)}) collective-permute-start(bf16[5,128,768]{2,1,0:T(8,128)(2,1)} %collective-permute-done.28.refs_10_), channel_id=1, source_target_pairs={{0,1},{1,0},{2,3},{3,2},{4,5},{5,4},{6,7},{7,6},{8,9},{9,8},{10,11... | collective-permute-start | bytes 2949128 | tf_op jit(solution)/shard_map/ppermute | solution.py:939
  672.7 25.9 %collective-permute-start.1 = (bf16[3,128,768]{2,1,0:T(8,128)(2,1)}, bf16[3,128,768]{2,1,0:T(8,128)(2,1)}, u32[]{:S(2)}, u32[]{:S(2)}) collective-permute-start(bf16[3,128,768]{2,1,0:T(8,128)(2,1)} %copy-done.6), channel_id=1, source_target_pairs={{0,1},{1,0},{2,3},{3,2},{4,5},{5,4},{6,7},{7,6},{8,9},{9,8},{10,11... | collective-permute-start | bytes 1769480 | tf_op jit(solution)/shard_map/ppermute | solution.py:939
  672.8 25.7 %collective-permute-start.3 = (bf16[3,128,768]{2,1,0:T(8,128)(2,1)}, bf16[3,128,768]{2,1,0:T(8,128)(2,1)}, u32[]{:S(2)}, u32[]{:S(2)}) collective-permute-start(bf16[3,128,768]{2,1,0:T(8,128)(2,1)} %copy-done.7), channel_id=1, source_target_pairs={{0,1},{1,0},{2,3},{3,2},{4,5},{5,4},{6,7},{7,6},{8,9},{9,8},{10,11... | collective-permute-start | bytes 1769480 | tf_op jit(solution)/shard_map/ppermute | solution.py:939
  673.2 25.3 %collective-permute-start.5 = (bf16[3,128,768]{2,1,0:T(8,128)(2,1)}, bf16[3,128,768]{2,1,0:T(8,128)(2,1)}, u32[]{:S(2)}, u32[]{:S(2)}) collective-permute-start(bf16[3,128,768]{2,1,0:T(8,128)(2,1)} %copy-done.8), channel_id=1, source_target_pairs={{0,1},{1,0},{2,3},{3,2},{4,5},{5,4},{6,7},{7,6},{8,9},{9,8},{10,11... | collective-permute-start | bytes 1769480 | tf_op jit(solution)/shard_map/ppermute | solution.py:939
  (23 other events, 439.7 us)

commit v6 on v5

--- a/solution.py
+++ b/solution.py
@@ -80,7 +80,6 @@
     up_load(0, 0).start()
     upstream_load = pltpu.make_async_copy(upstream, up_rows, io_sem.at[3])
     small_out[...] = jnp.zeros_like(small_out)
-    branch[...] = jnp.zeros_like(branch)
     pre_buf[0, :, :UP_COLS] = jnp.zeros((num_tokens, UP_COLS), jnp.bfloat16)
     gain[...] = gain_in[...].astype(jnp.float32)
     bias_up[...] = bias_up_in[...].astype(jnp.float32)
@@ -121,9 +120,21 @@
 
     def down_product(tile):
         slot = tile % 2
-        for part in range(row_dim // UP_COLS):
-            cols = slice(part * UP_COLS, (part + 1) * UP_COLS)
-            branch[:, cols] += jnp.dot(act_buf[slot], down_buf[slot, :, cols], preferred_element_type=jnp.float32)
+
+        def product(cols):
+            return jnp.dot(act_buf[slot], down_buf[slot, :, cols], preferred_element_type=jnp.float32)
+
+        all_cols = [slice(start, start + UP_COLS) for start in range(0, row_dim, UP_COLS)]
+
+        @pl.when(tile == 0)
+        def _():
+            for cols in all_cols:
+                branch[:, cols] = product(cols)
+
+        @pl.when(tile > 0)
+        def _():
+            for cols in all_cols:
+                branch[:, cols] += product(cols)
 
     each_block(lambda rows: normalize(0, rows, hid[rows, :].astype(jnp.float32)))
 
@@ -187,7 +198,6 @@
             def _():
                 def to_next(rows):
                     normalize(layer + 1, rows, next_rows(layer, rows))
-                    branch[rows, :] = jnp.zeros((NORM_ROWS, row_dim), jnp.float32)
 
                 each_block(to_next)
                 hid_store().start()
@@ -312,14 +322,18 @@
     def rows_at(start, size):
         return pl.ds(pl.multiple_of(start, spans[2]), size)
 
-    def rows_load(mat, chunk):
+    def rows_loads(mat, chunk):
         layer = num_layers - 1 - mat // 2
-        if mat % 2 == 0:
-            start = ((chunk % chunks_per_mat) // down_subs) * row_dim
-            source = activated.at[layer, :, pl.ds(pl.multiple_of(start, 128), row_dim)]
-        else:
-            source = normed.at[layer]
-        return pltpu.make_async_copy(source, rows_buf, load_sem.at[0, 0])
+        copies = []
+        for order, which_core in enumerate((1 - core, core)):
+            cols = pl.ds(pl.multiple_of(which_core * half, 128), half)
+            if mat % 2 == 0:
+                start = ((chunk % chunks_per_mat) // down_subs) * row_dim + which_core * half
+                source = activated.at[layer, :, pl.ds(pl.multiple_of(start, 128), half)]
+            else:
+                source = normed.at[layer, :, cols]
+            copies.append(pltpu.make_async_copy(source, rows_buf.at[:, cols], load_sem.at[0, order]))
+        return copies
 
     def weight_loads(mat, chunk):
         slot = chunk % 2
@@ -389,12 +403,12 @@
             send_sem=back_send.at[0, color, slot], recv_sem=back_recv.at[0, color, slot],
             device_id=(partners[CORE],), device_id_type=MESH)
 
-    def part_stores(group, chunk):
+    def part_stores(group, chunk, which_parts=(0, 1)):
         slot = chunk % GATHER_SLOTS
         place = chunk - full_chunks - sum(PART_GROUPS[:group])
         copies = []
         for color in range(COLORS):
-            for which in range(2):
+            for which in which_parts:
                 out_ref = part_refs[(group * COLORS + color) * 2 + which]
                 source = ring.at[slot, core if which == 0 else 1 - core, color, part_rows(color), :]
                 copies.append(pltpu.make_async_copy(
@@ -424,24 +438,35 @@
     def opens_layer(chunk):
         return (chunk > 0) & (chunk % (2 * chunks_per_mat) == 0)
 
-    def turn_rows(chunk):
+    def opens_rows(chunk):
         down = (chunk // chunks_per_mat) % 2 == 0
-
-        @pl.when((chunk % chunks_per_mat == 0) | (down & (chunk % down_subs == 0)))
-        def _():
-            rows_load(1, chunk).wait()
-            for start in range(0, row_dim, TILE):
-                turned[start:start + TILE, :] = rows_buf[:, start:start + TILE].T
-            for period, here in ((down_subs, down), (chunks_per_mat, jnp.logical_not(down))):
-                following = chunk + period
-
-                @pl.when(here & (following < num_chunks))
-                def _(following=following):
-                    for_mat(following, lambda mat: rows_load(mat, following).start())
+        return (chunk % chunks_per_mat == 0) | (down & (chunk % down_subs == 0))
+
+    def turn_rows(chunk, order):
+        @pl.when(opens_rows(chunk))
+        def _():
+            rows_loads(1, chunk)[order].wait()
+            first = (1 - core if order == 0 else core) * half
+            for start in range(0, half, TILE):
+                cols = pl.ds(pl.multiple_of(first + start, 128), TILE)
+                turned[cols, :] = rows_buf[:, cols].T
+
+    def next_rows_loads(chunk):
+        down = (chunk // chunks_per_mat) % 2 == 0
+        for period, here in ((down_subs, down), (chunks_per_mat, jnp.logical_not(down))):
+            following = chunk + period
+
+            @pl.when(opens_rows(chunk) & here & (following < num_chunks))
+            def _(following=following):
+                def start(mat):
+                    for copy in rows_loads(mat, following):
+                        copy.start()
+
+                for_mat(following, start)
 
     def load(chunk):
-        turn_rows(chunk)
         for_mat(chunk, lambda mat: cols_load(mat, chunk).wait())
+        turn_rows(chunk, 0)
         after = chunk + 1
 
         @pl.when(chunk == 0)
@@ -487,6 +512,8 @@
         core_copy(chunk).start()
 
     def compute_kept(chunk):
+        turn_rows(chunk, 1)
+        next_rows_loads(chunk)
         value = product(chunk, core)
         for color in range(COLORS):
             kept[chunk % KEPT_SLOTS, color] = value[color * region:(color + 1) * region]
@@ -545,6 +572,17 @@
                 back_copy(1, color, chunk, True).wait()
                 part_share_copy(color, chunk, False).start()
 
+        start_part_stores(chunk, (0,))
+
+    def start_part_stores(chunk, which_parts):
+        for group, size in enumerate(PART_GROUPS):
+            first = full_chunks + sum(PART_GROUPS[:group])
+
+            @pl.when((chunk >= first) & (chunk < first + size))
+            def _(group=group):
+                for copy in part_stores(group, chunk, which_parts):
+                    copy.start()
+
     def send_back_core(chunk):
         @pl.when(chunk < full_chunks)
         def _():
@@ -557,13 +595,7 @@
             for color in range(COLORS):
                 part_share_copy(color, chunk, True).wait()
 
-        for group, size in enumerate(PART_GROUPS):
-            first = full_chunks + sum(PART_GROUPS[:group])
-
-            @pl.when((chunk >= first) & (chunk < first + size))
-            def _(group=group):
-                for copy in part_stores(group, chunk):
-                    copy.start()
+        start_part_stores(chunk, (1,))
 
     def store(chunk):
         @pl.when(chunk < full_chunks)
@@ -582,8 +614,6 @@
             def _(group=group):
                 for copy in part_stores(group, chunk):
                     copy.wait()
-
-    token_half = grad_b.shape[0] // 2
 
     def backward(part, chunk):
         slot = chunk % 2
@@ -595,15 +625,12 @@
         def _():
             cols = slice(part * TILE, (part + 1) * TILE)
 
-            @pl.loop(0, 2)
-            def _(which):
-                rows = pl.ds(pl.multiple_of(which * token_half, 128), token_half)
-                grad_act = lax.dot_general(
-                    grad_b[rows, :], weight_buf[slot, cols, :], FEATURE_DIMS, preferred_element_type=jnp.float32)
-                grad_pre = grad_act * gelu_slope(pre_buf[slot, rows, cols].astype(jnp.float32))
-                grad_pre_buf[rows, cols] = grad_pre.astype(jnp.bfloat16)
-                start = row_dim + sub * chunk_cols + part * TILE
-                small_out[pl.ds(layer, 1), pl.ds(pl.multiple_of(start, 128), TILE)] += jnp.sum(grad_pre, axis=0, keepdims=True)
+            grad_act = lax.dot_general(
+                grad_b[...], weight_buf[slot, cols, :], FEATURE_DIMS, preferred_element_type=jnp.float32)
+            grad_pre = grad_act * gelu_slope(pre_buf[slot, :, cols].astype(jnp.float32))
+            grad_pre_buf[:, cols] = grad_pre.astype(jnp.bfloat16)
+            start = row_dim + sub * chunk_cols + part * TILE
+            small_out[pl.ds(layer, 1), pl.ds(pl.multiple_of(start, 128), TILE)] += jnp.sum(grad_pre, axis=0, keepdims=True)
 
             if part == chunk_cols // TILE - 1:
                 grad_pre_store(sub).start()
@@ -678,8 +705,10 @@
         backward_2=functools.partial(backward, 2), input_grad=input_grad)
 
     first = jnp.int32(0)
-    rows_load(0, first).start()
+    other_rows, own_rows = rows_loads(0, first)
+    other_rows.start()
     cols_load(0, first).start()
+    own_rows.start()
     grad_b_copy = pltpu.make_async_copy(grad_top_b, grad_b, grad_b_sem)
     barrier = pltpu.get_barrier_semaphore()
     for partner in partners:

time: 706 us -> 704 us (level)
  transfers between devices with their start and end apart: 30 -> 30, of which waited for: 11 -> 12; matrix products, arithmetic and copies ran while one was open for 0% -> 0% of each run, Pallas kernels for 10% -> 10%
where the time goes in v6:
time: 704 us; the launch traced here: 703 us
  Pallas kernels  588 us (84%)
  waiting for transfers between devices  92.2 us (13%)
  starting transfers between devices  18.7 us (3%)
    pallas_call x1, Pallas kernels, backward_pass(): pl.pallas_call(functools.partial(backward_kernel, sizes), out_shape=[jax....  416 us
    pallas_call x1, Pallas kernels, forward_pass(): pl.pallas_call(functools.partial(forward_kernel, (num_layers, hidden // t...  97.8 us
    ppermute x30, waiting for transfers between devices, swap(): return lax.ppermute(array, axis, flip_pairs(num_devices, bit))  92.2 us
    pallas_call x6, Pallas kernels, join(): pl.pallas_call(functools.partial(join_kernel, (skip, count, place, layer,...  46.4 us
    pallas_call x2, Pallas kernels, widen(): pl.pallas_call(functools.partial(widen_kernel, (first, count, place, laye...  27.6 us
    ppermute x30, starting transfers between devices, swap(): return lax.ppermute(array, axis, flip_pairs(num_devices, bit))  18.7 us
  transfers between devices with their start and end apart: 30, of which 12 were waited for; matrix products, arithmetic and copies ran while one was open for 0% of the time, Pallas kernels for 10%

profile of v6, /device:TPU:0, one launch (start us, length us, event | category | flops | bytes accessed | tf_op | source)
XLA Modules:
  0.0 703.5 jit_solution(6912927668600214786)
XLA Ops:
  0.6 97.8 %forward.1 = (bf16[1024,1536]{1,0:T(8,128)(2,1)}, bf16[2,1024,1536]{2,1,0:T(8,128)(2,1)}, bf16[2,1024,6144]{2,1,0:T(8,128)(2,1)}, bf16[2,1024,6144]{2,1,0:T(8,12...) custom-call(bf16[1024,1536]{1,0:T(8,128)(2,1)} %refs_0_.1, ...), custom_call_target="tpu_custom_call" | custom-call | tf_op jit(solution)/shard_map/forward/pallas_call | solution.py:251
  98.5 416.3 %backward.1 = (bf16[12,2,3,256,768]{4,3,2,1,0:T(8,128)(2,1)}, f32[2,9216]{1,0:T(2,128)}, bf16[8,1024,768]{2,1,0:T(8,128)(2,1)}, bf16[1024,1536]{1,0:T(8,128)(2,1...) custom-call(bf16[1024,1536]{1,0:T(8,128)(2,1)} %refs_0_.1, ...), custom_call_target="tpu_custom_call" | custom-call | tf_op jit(solution)/shard_map/backward/pallas_call | solution.py:753
  514.7 1.3 collective-permute-start.12
  520.1 6.9 collective-permute-done.12.refs_2_
  529.0 11.5 %collective-permute-done.16.refs_10_ = bf16[2,128,768]{2,1,0:T(8,128)(2,1)S(1)} collective-permute-done((bf16[2,128,768]{2,1,0:T(8,128)(2,1)}, bf16[2,128,768]{2,1,0:T(8,128)(2,1)S(1)}, u32[]{:S(2)}, u32[]{:S(2)}) %collective-permute-start.16) | collective-permute-done | bytes 393248 | tf_op jit(solution)/shard_map/ppermute | solution.py:968
  542.5 1.3 collective-permute-start.18
  544.6 7.7 %collective-permute-done.refs_2_ = bf16[3,128,768]{2,1,0:T(8,128)(2,1)S(1)} collective-permute-done((bf16[3,128,768]{2,1,0:T(8,128)(2,1)}, bf16[3,128,768]{2,1,0:T(8,128)(2,1)S(1)}, u32[]{:S(2)}, u32[]{:S(2)}) %collective-permute-start) | collective-permute-done | bytes 589856 | tf_op jit(solution)/shard_map/ppermute | solution.py:968
  553.1 1.3 collective-permute-start.22
  554.4 2.5 collective-permute-done.2.refs_6_
  559.9 1.7 collective-permute-done.17.refs_11_
  562.4 19.4 %collective-permute-done.18.refs_2_ = bf16[7,128,768]{2,1,0:T(8,128)(2,1)S(1)} collective-permute-done((bf16[7,128,768]{2,1,0:T(8,128)(2,1)}, bf16[7,128,768]{2,1,0:T(8,128)(2,1)S(1)}, u32[]{:S(2)}, u32[]{:S(2)}) %collective-permute-start.18) | collective-permute-done | bytes 1376288 | tf_op jit(solution)/shard_map/ppermute | solution.py:968
  582.9 3.5 collective-permute-done.20.refs_6_
  587.0 15.4 %collective-permute-done.24.refs_2_ = bf16[5,128,768]{2,1,0:T(8,128)(2,1)} collective-permute-done((bf16[5,128,768]{2,1,0:T(8,128)(2,1)}, bf16[5,128,768]{2,1,0:T(8,128)(2,1)}, u32[]{:S(2)}, u32[]{:S(2)}) %collective-permute-start.24) | collective-permute-done | bytes 983072 | tf_op jit(solution)/shard_map/ppermute | solution.py:968
  602.3 1.3 collective-permute-start.28
  603.6 2.1 collective-permute-done.26.refs_6_
  605.7 20.1 %collective-permute-done.28.refs_10_ = bf16[5,128,768]{2,1,0:T(8,128)(2,1)} collective-permute-done((bf16[5,128,768]{2,1,0:T(8,128)(2,1)}, bf16[5,128,768]{2,1,0:T(8,128)(2,1)}, u32[]{:S(2)}, u32[]{:S(2)}) %collective-permute-start.28) | collective-permute-done | bytes 983072 | tf_op jit(solution)/shard_map/ppermute | solution.py:968
  628.5 18.5 %shard_map.110 = (f32[2,6144,1536]{2,1,0:T(8,128)}, f32[2,1536]{1,0:T(2,128)}, f32[2,6144]{1,0:T(2,128)}, f32[2,1536]{1,0:T(2,128)}) custom-call(bf16[12,2,3,256,768]{4,3,2,1,0:T(8,128)(2,1)} %get-tuple-element.55.refs_0_, f32[2,9216]{1,0:T(2,128)} %get-tuple-element.56.refs_1_), custom_call_target="tpu_custom_call" | custom-call | flops 4718592000 | bytes 56623104 | tf_op jit(solution)/shard_map/pallas_call | solution.py:932
  647.1 9.1 %shard_map.111.refs_12_ = f32[2,1536,6144]{2,1,0:T(8,128)} custom-call(bf16[12,2,3,256,768]{4,3,2,1,0:T(8,128)(2,1)} %get-tuple-element.55.refs_0_), custom_call_target="tpu_custom_call" | custom-call | flops 2359296000 | bytes 28311552 | tf_op jit(solution)/shard_map/pallas_call | solution.py:932
  656.1 9.2 %shard_map.112.refs_12_ = f32[2,1536,6144]{2,1,0:T(8,128)} custom-call(bf16[7,128,768]{2,1,0:T(8,128)(2,1)} %get-tuple-element.76.refs_0_, bf16[7,128,768]{2,1,0:T(8,128)(2,1)} %get-tuple-element.77.refs_1_, bf16[7,128,768]{2,1,0:T(8,128)(2,1)} %copy-done, bf16[7,128,768]{2,1,0:T(8,128)(2,1)} %copy-done.3, ...), custom_call_target="tpu_custom_call", output_to_operand_aliasing={{}: (12, {})} | custom-call | flops 2359296000 | bytes 28311552 | tf_op jit(solution)/shard_map/pallas_call | solution.py:955
  665.3 5.2 shard_map.113.refs_12_
  671.2 6.8 shard_map.116.refs_12_
  678.1 6.9 shard_map.114.refs_12_
  685.0 11.4 %shard_map.117 = f32[2,6144,1536]{2,1,0:T(8,128)} custom-call(bf16[5,128,768]{2,1,0:T(8,128)(2,1)} %get-tuple-element.83.refs_0_, bf16[5,128,768]{2,1,0:T(8,128)(2,1)} %get-tuple-element.84.refs_1_, bf16[5,128,768]{2,1,0:T(8,128)(2,1)} %collective-permute-done.24.refs_2_, ...), custom_call_target="tpu_custom_call", output_to_operand_aliasing={{}: (12, {})} | custom-call | flops 2949120000 | bytes 35389440 | tf_op jit(solution)/shard_map/pallas_call | solution.py:955
  696.4 6.9 shard_map.115
  (80 shorter events, 18.5 us)
Async XLA Ops:
  516.8 25.0 %collective-permute-start.10 = (bf16[3,128,768]{2,1,0:T(8,128)(2,1)}, bf16[3,128,768]{2,1,0:T(8,128)(2,1)S(1)}, u32[]{:S(2)}, u32[]{:S(2)}) collective-permute-start(bf16[3,128,768]{2,1,0:T(8,128)(2,1)} %get-tuple-element.68.refs_8_), channel_id=1, source_target_pairs={{0,8},{1,9},{2,10},{3,11},{4,12},{5,13},{6,14},{7,15},{8,0},{9,1},... | collective-permute-start | bytes 1769480 | tf_op jit(solution)/shard_map/ppermute | solution.py:968
  518.1 22.4 %collective-permute-start.16 = (bf16[2,128,768]{2,1,0:T(8,128)(2,1)}, bf16[2,128,768]{2,1,0:T(8,128)(2,1)S(1)}, u32[]{:S(2)}, u32[]{:S(2)}) collective-permute-start(bf16[2,128,768]{2,1,0:T(8,128)(2,1)} %get-tuple-element.74.refs_8_), channel_id=1, source_target_pairs={{0,8},{1,9},{2,10},{3,11},{4,12},{5,13},{6,14},{7,15},{8,0},{9,1},... | collective-permute-start | bytes 1179656 | tf_op jit(solution)/shard_map/ppermute | solution.py:968
  518.8 23.7 %collective-permute-start.6 = (bf16[3,128,768]{2,1,0:T(8,128)(2,1)}, bf16[3,128,768]{2,1,0:T(8,128)(2,1)}, u32[]{:S(2)}, u32[]{:S(2)}) collective-permute-start(bf16[3,128,768]{2,1,0:T(8,128)(2,1)} %get-tuple-element.64.refs_0_), channel_id=1, source_target_pairs={{0,2},{1,3},{2,0},{3,1},{4,6},{5,7},{6,4},{7,5},{8,10},{9,11},{10,... | collective-permute-start | bytes 1769480 | tf_op jit(solution)/shard_map/ppermute | solution.py:968
  527.0 16.8 %collective-permute-start.8 = (bf16[3,128,768]{2,1,0:T(8,128)(2,1)}, bf16[3,128,768]{2,1,0:T(8,128)(2,1)}, u32[]{:S(2)}, u32[]{:S(2)}) collective-permute-start(bf16[3,128,768]{2,1,0:T(8,128)(2,1)} %get-tuple-element.66.refs_4_), channel_id=1, source_target_pairs={{0,4},{1,5},{2,6},{3,7},{4,0},{5,1},{6,2},{7,3},{8,12},{9,13},{10,... | collective-permute-start | bytes 1769480 | tf_op jit(solution)/shard_map/ppermute | solution.py:968
  528.3 24.0 %collective-permute-start = (bf16[3,128,768]{2,1,0:T(8,128)(2,1)}, bf16[3,128,768]{2,1,0:T(8,128)(2,1)S(1)}, u32[]{:S(2)}, u32[]{:S(2)}) collective-permute-start(bf16[3,128,768]{2,1,0:T(8,128)(2,1)} %get-tuple-element.58.refs_0_), channel_id=1, source_target_pairs={{0,2},{1,3},{2,0},{3,1},{4,6},{5,7},{6,4},{7,5},{8,10},{9,11},{10,... | collective-permute-start | bytes 1769480 | tf_op jit(solution)/shard_map/ppermute | solution.py:968
  540.5 16.4 %collective-permute-start.2 = (bf16[3,128,768]{2,1,0:T(8,128)(2,1)}, bf16[3,128,768]{2,1,0:T(8,128)(2,1)S(1)}, u32[]{:S(2)}, u32[]{:S(2)}) collective-permute-start(bf16[3,128,768]{2,1,0:T(8,128)(2,1)} %get-tuple-element.60.refs_4_), channel_id=1, source_target_pairs={{0,4},{1,5},{2,6},{3,7},{4,0},{5,1},{6,2},{7,3},{8,12},{9,13},{10,... | collective-permute-start | bytes 1769480 | tf_op jit(solution)/shard_map/ppermute | solution.py:968
  542.5 39.2 %collective-permute-start.18 = (bf16[7,128,768]{2,1,0:T(8,128)(2,1)}, bf16[7,128,768]{2,1,0:T(8,128)(2,1)S(1)}, u32[]{:S(2)}, u32[]{:S(2)}) collective-permute-start(bf16[7,128,768]{2,1,0:T(8,128)(2,1)} %get-tuple-element.76.refs_0_), channel_id=1, source_target_pairs={{0,2},{1,3},{2,0},{3,1},{4,6},{5,7},{6,4},{7,5},{8,10},{9,11},{10,... | collective-permute-start | bytes 4128776 | tf_op jit(solution)/shard_map/ppermute | solution.py:968
  543.8 42.6 %collective-permute-start.20 = (bf16[7,128,768]{2,1,0:T(8,128)(2,1)}, bf16[7,128,768]{2,1,0:T(8,128)(2,1)S(1)}, u32[]{:S(2)}, u32[]{:S(2)}) collective-permute-start(bf16[7,128,768]{2,1,0:T(8,128)(2,1)} %get-tuple-element.78.refs_4_), channel_id=1, source_target_pairs={{0,4},{1,5},{2,6},{3,7},{4,0},{5,1},{6,2},{7,3},{8,12},{9,13},{10,... | collective-permute-start | bytes 4128776 | tf_op jit(solution)/shard_map/ppermute | solution.py:968
  553.1 33.3 %collective-permute-start.22 = (bf16[7,128,768]{2,1,0:T(8,128)(2,1)}, bf16[7,128,768]{2,1,0:T(8,128)(2,1)S(1)}, u32[]{:S(2)}, u32[]{:S(2)}) collective-permute-start(bf16[7,128,768]{2,1,0:T(8,128)(2,1)} %get-tuple-element.80.refs_8_), channel_id=1, source_target_pairs={{0,8},{1,9},{2,10},{3,11},{4,12},{5,13},{6,14},{7,15},{8,0},{9,1},... | collective-permute-start | bytes 4128776 | tf_op jit(solution)/shard_map/ppermute | solution.py:968
  558.6 43.7 %collective-permute-start.24 = (bf16[5,128,768]{2,1,0:T(8,128)(2,1)}, bf16[5,128,768]{2,1,0:T(8,128)(2,1)}, u32[]{:S(2)}, u32[]{:S(2)}) collective-permute-start(bf16[5,128,768]{2,1,0:T(8,128)(2,1)} %get-tuple-element.83.refs_0_), channel_id=1, source_target_pairs={{0,2},{1,3},{2,0},{3,1},{4,6},{5,7},{6,4},{7,5},{8,10},{9,11},{10,... | collective-permute-start | bytes 2949128 | tf_op jit(solution)/shard_map/ppermute | solution.py:968
  561.6 44.0 %collective-permute-start.26 = (bf16[5,128,768]{2,1,0:T(8,128)(2,1)}, bf16[5,128,768]{2,1,0:T(8,128)(2,1)}, u32[]{:S(2)}, u32[]{:S(2)}) collective-permute-start(bf16[5,128,768]{2,1,0:T(8,128)(2,1)} %get-tuple-element.85.refs_4_), channel_id=1, source_target_pairs={{0,4},{1,5},{2,6},{3,7},{4,0},{5,1},{6,2},{7,3},{8,12},{9,13},{10,... | collective-permute-start | bytes 2949128 | tf_op jit(solution)/shard_map/ppermute | solution.py:968
  582.9 43.4 %collective-permute-start.19 = (bf16[7,128,768]{2,1,0:T(8,128)(2,1)S(1)}, bf16[7,128,768]{2,1,0:T(8,128)(2,1)S(1)}, u32[]{:S(2)}, u32[]{:S(2)}) collective-permute-start(bf16[7,128,768]{2,1,0:T(8,128)(2,1)S(1)} %collective-permute-done.18.refs_2_), channel_id=1, source_target_pairs={{0,1},{1,0},{2,3},{3,2},{4,5},{5,4},{6,7},{7,6},{8,9},{9,8},{10,11... | collective-permute-start | bytes 4128776 | tf_op jit(solution)/shard_map/ppermute | solution.py:968
  586.4 40.0 %collective-permute-start.21 = (bf16[7,128,768]{2,1,0:T(8,128)(2,1)S(1)}, bf16[7,128,768]{2,1,0:T(8,128)(2,1)S(1)}, u32[]{:S(2)}, u32[]{:S(2)}) collective-permute-start(bf16[7,128,768]{2,1,0:T(8,128)(2,1)S(1)} %collective-permute-done.20.refs_6_), channel_id=1, source_target_pairs={{0,1},{1,0},{2,3},{3,2},{4,5},{5,4},{6,7},{7,6},{8,9},{9,8},{10,11... | collective-permute-start | bytes 4128776 | tf_op jit(solution)/shard_map/ppermute | solution.py:968
  586.4 40.5 %collective-permute-start.23 = (bf16[7,128,768]{2,1,0:T(8,128)(2,1)S(1)}, bf16[7,128,768]{2,1,0:T(8,128)(2,1)S(1)}, u32[]{:S(2)}, u32[]{:S(2)}) collective-permute-start(bf16[7,128,768]{2,1,0:T(8,128)(2,1)S(1)} %collective-permute-done.22.refs_10_), channel_id=1, source_target_pairs={{0,1},{1,0},{2,3},{3,2},{4,5},{5,4},{6,7},{7,6},{8,9},{9,8},{10,11... | collective-permute-start | bytes 4128776 | tf_op jit(solution)/shard_map/ppermute | solution.py:968
  602.3 23.5 %collective-permute-start.28 = (bf16[5,128,768]{2,1,0:T(8,128)(2,1)}, bf16[5,128,768]{2,1,0:T(8,128)(2,1)}, u32[]{:S(2)}, u32[]{:S(2)}) collective-permute-start(bf16[5,128,768]{2,1,0:T(8,128)(2,1)} %get-tuple-element.87.refs_8_), channel_id=1, source_target_pairs={{0,8},{1,9},{2,10},{3,11},{4,12},{5,13},{6,14},{7,15},{8,0},{9,1},... | collective-permute-start | bytes 2949128 | tf_op jit(solution)/shard_map/ppermute | solution.py:968
  605.7 20.2 %collective-permute-start.11 = (bf16[3,128,768]{2,1,0:T(8,128)(2,1)S(1)}, bf16[3,128,768]{2,1,0:T(8,128)(2,1)S(1)}, u32[]{:S(2)}, u32[]{:S(2)}) collective-permute-start(bf16[3,128,768]{2,1,0:T(8,128)(2,1)S(1)} %collective-permute-done.10.refs_10_), channel_id=1, source_target_pairs={{0,1},{1,0},{2,3},{3,2},{4,5},{5,4},{6,7},{7,6},{8,9},{9,8},{10,11... | collective-permute-start | bytes 1769480 | tf_op jit(solution)/shard_map/ppermute | solution.py:968
  625.8 44.7 %collective-permute-start.7 = (bf16[3,128,768]{2,1,0:T(8,128)(2,1)}, bf16[3,128,768]{2,1,0:T(8,128)(2,1)}, u32[]{:S(2)}, u32[]{:S(2)}) collective-permute-start(bf16[3,128,768]{2,1,0:T(8,128)(2,1)} %collective-permute-done.6.refs_2_), channel_id=1, source_target_pairs={{0,1},{1,0},{2,3},{3,2},{4,5},{5,4},{6,7},{7,6},{8,9},{9,8},{10,11... | collective-permute-start | bytes 1769480 | tf_op jit(solution)/shard_map/ppermute | solution.py:968
  625.8 44.9 %collective-permute-start.9 = (bf16[3,128,768]{2,1,0:T(8,128)(2,1)}, bf16[3,128,768]{2,1,0:T(8,128)(2,1)}, u32[]{:S(2)}, u32[]{:S(2)}) collective-permute-start(bf16[3,128,768]{2,1,0:T(8,128)(2,1)} %collective-permute-done.8.refs_6_), channel_id=1, source_target_pairs={{0,1},{1,0},{2,3},{3,2},{4,5},{5,4},{6,7},{7,6},{8,9},{9,8},{10,11... | collective-permute-start | bytes 1769480 | tf_op jit(solution)/shard_map/ppermute | solution.py:968
  626.3 44.8 %collective-permute-start.25 = (bf16[5,128,768]{2,1,0:T(8,128)(2,1)}, bf16[5,128,768]{2,1,0:T(8,128)(2,1)}, u32[]{:S(2)}, u32[]{:S(2)}) collective-permute-start(bf16[5,128,768]{2,1,0:T(8,128)(2,1)} %collective-permute-done.24.refs_2_), channel_id=1, source_target_pairs={{0,1},{1,0},{2,3},{3,2},{4,5},{5,4},{6,7},{7,6},{8,9},{9,8},{10,11... | collective-permute-start | bytes 2949128 | tf_op jit(solution)/shard_map/ppermute | solution.py:968
  626.4 58.5 %collective-permute-start.27 = (bf16[5,128,768]{2,1,0:T(8,128)(2,1)}, bf16[5,128,768]{2,1,0:T(8,128)(2,1)}, u32[]{:S(2)}, u32[]{:S(2)}) collective-permute-start(bf16[5,128,768]{2,1,0:T(8,128)(2,1)} %collective-permute-done.26.refs_6_), channel_id=1, source_target_pairs={{0,1},{1,0},{2,3},{3,2},{4,5},{5,4},{6,7},{7,6},{8,9},{9,8},{10,11... | collective-permute-start | bytes 2949128 | tf_op jit(solution)/shard_map/ppermute | solution.py:968
  627.4 57.5 %collective-permute-start.29 = (bf16[5,128,768]{2,1,0:T(8,128)(2,1)}, bf16[5,128,768]{2,1,0:T(8,128)(2,1)}, u32[]{:S(2)}, u32[]{:S(2)}) collective-permute-start(bf16[5,128,768]{2,1,0:T(8,128)(2,1)} %collective-permute-done.28.refs_10_), channel_id=1, source_target_pairs={{0,1},{1,0},{2,3},{3,2},{4,5},{5,4},{6,7},{7,6},{8,9},{9,8},{10,11... | collective-permute-start | bytes 2949128 | tf_op jit(solution)/shard_map/ppermute | solution.py:968
  670.5 25.9 %collective-permute-start.1 = (bf16[3,128,768]{2,1,0:T(8,128)(2,1)}, bf16[3,128,768]{2,1,0:T(8,128)(2,1)}, u32[]{:S(2)}, u32[]{:S(2)}) collective-permute-start(bf16[3,128,768]{2,1,0:T(8,128)(2,1)} %copy-done.6), channel_id=1, source_target_pairs={{0,1},{1,0},{2,3},{3,2},{4,5},{5,4},{6,7},{7,6},{8,9},{9,8},{10,11... | collective-permute-start | bytes 1769480 | tf_op jit(solution)/shard_map/ppermute | solution.py:968
  670.7 25.7 %collective-permute-start.3 = (bf16[3,128,768]{2,1,0:T(8,128)(2,1)}, bf16[3,128,768]{2,1,0:T(8,128)(2,1)}, u32[]{:S(2)}, u32[]{:S(2)}) collective-permute-start(bf16[3,128,768]{2,1,0:T(8,128)(2,1)} %copy-done.7), channel_id=1, source_target_pairs={{0,1},{1,0},{2,3},{3,2},{4,5},{5,4},{6,7},{7,6},{8,9},{9,8},{10,11... | collective-permute-start | bytes 1769480 | tf_op jit(solution)/shard_map/ppermute | solution.py:968
  671.1 25.3 %collective-permute-start.5 = (bf16[3,128,768]{2,1,0:T(8,128)(2,1)}, bf16[3,128,768]{2,1,0:T(8,128)(2,1)}, u32[]{:S(2)}, u32[]{:S(2)}) collective-permute-start(bf16[3,128,768]{2,1,0:T(8,128)(2,1)} %copy-done.8), channel_id=1, source_target_pairs={{0,1},{1,0},{2,3},{3,2},{4,5},{5,4},{6,7},{7,6},{8,9},{9,8},{10,11... | collective-permute-start | bytes 1769480 | tf_op jit(solution)/shard_map/ppermute | solution.py:968
  (23 other events, 438.3 us)
